TPU v7x, 128 devices: a whole 4x4x4 slice. The times are simulated.
128 devices in a mesh: dp: 32 (over x_hi, z, y), head: 4 (over x_lo, core).
Axes of the slice: x: 4 (x_hi: 2, x_lo: 2; x = x_hi * 2 + x_lo), y: 4, z: 4, core: 2. Of those that a mesh axis runs over, the one named last changes fastest.
Arguments:
- q_latent: bfloat16 [4096, 1536], P('dp'), may hold values from -1000 to 1000
- kv_latent: bfloat16 [4096, 576], P('dp'), may hold values from -6 to 6
- kv_gain: float32 [512], replicated, may hold values from 0.1 to 1.9
- w_q_b: bfloat16 [1536, 12288], P(None, 'head'), may hold values from -0.15625 to 0.15625
- w_kv_b: bfloat16 [512, 16384], P(None, 'head'), may hold values from -0.25 to 0.25
- w_o: bfloat16 [8192, 7168], P('head', 'dp'), may hold values from -0.5 to 0.5
- prompt_len: int32 [1], replicated, may hold values from 1 to 1023
- response_mask: int32 [4096], replicated, may hold values 0 or 1
Outputs:
- mixed: bfloat16 [4096, 7168], P('dp', 'head')
All inputs are finite; a program needn't handle non-finite values.
Results may differ from a plain program's by a relative error of at most 0.013.
The roundings to bfloat16 on the way count: a program that leaves them out, or rounds other values in their place, can miss the bound.
Values may be sent and summed in bfloat16 or wider, within the bound.
A program may use at most 192 MiB of HBM per device.

v0:
```python
import math

import jax
import jax.numpy as jnp
from jax import lax
from jax.sharding import Mesh
from jax.sharding import PartitionSpec as P

KVR = 512
ROPE = 64
NOPE = 128
VD = 128
DP = ("dp_0", "dp_1", "dp_2")


epsilon = 1e-06


def laid_out(pieces, dim):
    pieces = jnp.moveaxis(pieces, 0, dim)
    dims = pieces.shape
    return pieces.reshape(*dims[:dim], dims[dim] * dims[dim + 1], *dims[dim + 2 :])


def stacked_from(array, axes, turns):
    pieces = array[None]
    for k in turns:
        pieces = lax.all_gather(pieces, axes[k], axis=0, tiled=True)
    current = [lax.axis_size(axes[k]) for k in reversed(turns)]
    pieces = pieces.reshape(*current, *array.shape)
    turned = sorted(range(len(turns)), key=lambda place: turns[len(turns) - 1 - place])
    return pieces.transpose(*turned, *range(len(turns), pieces.ndim)).reshape(-1, *array.shape)


def whole_of(array, axes, turns, dim):
    return laid_out(stacked_from(array, axes, turns), dim)


def cut_along(array, dim, size):
    before, after = (array.shape[:dim], array.shape[dim + 1 :])
    return jnp.moveaxis(array.reshape(*before, size, -1, *after), dim, 0)


def summed_on_arrival(array, axis, dim):
    size = lax.axis_size(axis)
    pieces = lax.all_to_all(cut_along(array, dim, size), axis, 0, 0, tiled=True)
    return jnp.sum(pieces, axis=0)


def tables(positions):
    half_width = ROPE // 2
    frequency = 10000.0 ** (-jnp.arange(half_width, dtype=jnp.float32) * 2.0 / ROPE)
    angles = positions.astype(jnp.float32)[:, None] * frequency[None, :]
    return (jnp.cos(angles), jnp.sin(angles))


def rotate(values, cosine, sine_table):
    half_width = values.shape[-1] // 2
    leading = values[..., :half_width]
    trailing = values[..., half_width:]
    return jnp.concatenate(
        [leading * cosine - trailing * sine_table, trailing * cosine + leading * sine_table],
        axis=-1,
    )


def attend(full_query, keys, allowed, w_value):
    rows_here, head_count = (full_query.shape[0], full_query.shape[1])
    group_size = math.gcd(head_count, 4)
    groups = head_count // group_size
    grouped = full_query.reshape(rows_here, groups, group_size, KVR + ROPE).transpose(1, 0, 2, 3)
    value_blocks = w_value.reshape(KVR, groups, group_size, VD).transpose(1, 0, 2, 3)
    latent_values = keys[:, :KVR]
    scale = 1.0 / math.sqrt(NOPE + ROPE)

    def one_group(operands):
        chosen, w_group = operands
        scores = jnp.einsum("tgc,sc->tgs", chosen, keys, preferred_element_type=jnp.float32) * scale
        scores = jnp.where(allowed[:, None, :], scores, -1e30)
        row_max = jnp.max(scores, axis=-1, keepdims=True)
        lifted = jnp.exp(scores - row_max)
        weights = (lifted / jnp.sum(lifted, axis=-1, keepdims=True)).astype(jnp.bfloat16)
        context = jnp.einsum(
            "tgs,sc->tgc", weights, latent_values, preferred_element_type=jnp.float32
        ).astype(jnp.bfloat16)
        return jnp.einsum(
            "tgc,cgv->tgv", context, w_group, preferred_element_type=jnp.float32
        ).astype(jnp.bfloat16)

    outputs = lax.map(one_group, (grouped, value_blocks))
    return outputs.transpose(1, 0, 2, 3).reshape(rows_here, head_count * VD)


def local(q_latent, kv_latent, kv_gain, w_q_b, w_kv_b, w_o, prompt_len, response_mask):
    rows_here = q_latent.shape[0]
    offset = lax.axis_index(DP) * rows_here
    local_positions = offset + jnp.arange(rows_here, dtype=jnp.int32)
    cosine, sine_table = tables(local_positions)
    latent = kv_latent[:, :KVR].astype(jnp.float32)
    normed = (
        latent * lax.rsqrt(jnp.mean(latent * latent, axis=-1, keepdims=True) + epsilon) * kv_gain
    )
    key_rope = rotate(kv_latent[:, KVR:].astype(jnp.float32), cosine, sine_table)
    local_keys = jnp.concatenate([normed, key_rope], axis=1).astype(jnp.bfloat16)
    keys = whole_of(local_keys, DP, (0, 1, 2), 0)
    head_count = w_q_b.shape[1] // (NOPE + ROPE)
    queries = jnp.dot(q_latent, w_q_b, preferred_element_type=jnp.float32).astype(jnp.bfloat16)
    queries = queries.reshape(rows_here, head_count, NOPE + ROPE)
    query_rope = rotate(
        queries[:, :, NOPE:].astype(jnp.float32), cosine[:, None, :], sine_table[:, None, :]
    ).astype(jnp.bfloat16)
    w_heads = w_kv_b.reshape(KVR, head_count, NOPE + VD)
    absorbed = jnp.einsum(
        "thn,khn->thk",
        queries[:, :, :NOPE],
        w_heads[:, :, :NOPE],
        preferred_element_type=jnp.float32,
    ).astype(jnp.bfloat16)
    full_query = jnp.concatenate([absorbed, query_rope], axis=-1)
    key_positions = jnp.arange(keys.shape[0], dtype=jnp.int32)
    usable = (key_positions < prompt_len[0]) | (response_mask == 1)
    allowed = (key_positions[None, :] <= local_positions[:, None]) & usable[None, :]
    attended = attend(full_query, keys, allowed, w_heads[:, :, NOPE:])
    partial_value = jnp.dot(
        attended, lax.all_gather(w_o, DP, axis=1, tiled=True), preferred_element_type=jnp.float32
    )
    return summed_on_arrival(partial_value, "head", 1).astype(jnp.bfloat16)


def solution(mesh):
    finer = Mesh(
        mesh.devices.reshape(2, 4, 4, mesh.shape["head"]), ("dp_0", "dp_1", "dp_2", "head")
    )
    placed = (
        P(DP, None),
        P(DP, None),
        P(),
        P(None, "head"),
        P(None, "head"),
        P("head", DP),
        P(),
        P(),
    )
    return jax.shard_map(
        local, mesh=finer, in_specs=placed, out_specs=P(DP, "head"), check_vma=False
    )
```

profile of v0, /device:TPU:100, one launch (start us, length us, event | category | flops | bytes accessed | tf_op | source)
XLA Modules:
  0.0 404.6 jit_solution(208382671456469531)
XLA Ops:
  6.6 0.8 slice_convert_fusion
  7.3 1.0 fusion.48
  8.3 1.1 fusion.51
  9.4 0.1 fusion.53
  9.6 7.9 %all_gather.12 = bf16[2,128,576]{1,2,0:T(8,128)(2,1)} all-gather(bf16[1,128,576]{1,2,0:T(8,128)(2,1)S(1)} %pad_maximum_fusion.1), channel_id=1, replica_groups=mesh['dp_0'=2,'dp_1'=4,'dp_2'=4,'head'=4] {'dp_0'}, dimensions={0}, use_global_device_ids=true | all-gather | bytes 442368 | tf_op jit(solution)/shard_map/all_gather | solution.py:28
  17.5 24.8 %all-gather.4.cloned.1.call-done = bf16[8,128,576]{1,2,0:T(8,128)(2,1)} async-done(((bf16[2,128,576]{1,2,0:T(8,128)(2,1)}), bf16[8,128,576]{1,2,0:T(8,128)(2,1)}) %all-gather.4.cloned.1.call-update) | async-done | bytes 1179664 | tf_op jit(solution)/shard_map/all_gather | solution.py:28
  42.3 0.7 all-gather.8.cloned.1.call-update
  43.0 0.1 copy.34
  43.2 5.1 %convolution_convert_fusion = bf16[128,3072]{1,0:T(8,128)(2,1)S(1)} fusion(bf16[128,1536]{1,0:T(8,128)(2,1)S(1)} %copy-done, bf16[1536,3072]{1,0:T(8,128)(2,1)} %param.13), kind=kOutput, calls=%fused_computation.31 | convolution fusion | flops 1208352768 | bytes 10616832 | tf_op jit(solution)/shard_map/dot_general | solution.py:107
  48.3 0.4 copy.30
  48.7 0.3 copy.44
  49.0 0.1 convert_element_type.52
  49.1 6.6 %copy.29 = bf16[512,4096]{0,1:T(8,128)(2,1)} copy(bf16[512,4096]{1,0:T(8,128)(2,1)} %param.14) | data formatting | bytes 8388608 | tf_op args[4]
  55.7 3.4 slice.44
  59.1 0.4 subtract_convert_fusion
  59.5 0.8 convert_bitcast_fusion
  60.3 2.0 pad_maximum_fusion
  62.3 3.2 copy.36
  66.1 32.1 %all-gather.6.cloned.1.call-done = bf16[32,128,576]{1,2,0:T(8,128)(2,1)} async-done(((bf16[8,128,576]{1,2,0:T(8,128)(2,1)}), bf16[32,128,576]{1,2,0:T(8,128)(2,1)}) %all-gather.6.cloned.1.call-update) | async-done | bytes 4718608 | tf_op jit(solution)/shard_map/all_gather | solution.py:28
  98.2 8.1 %copy.37 = bf16[2,4,4,128,576]{3,2,1,0,4:T(4,128)(2,1)} copy(bf16[2,4,4,128,576]{3,4,0,1,2:T(8,128)(2,1)} %bitcast.79) | data formatting | bytes 9437184 | tf_op jit(solution)/shard_map/transpose | solution.py:32
  106.3 8.9 %reshape_reshape.3 = bf16[4096,576]{0,1:T(8,128)(2,1)} reshape(bf16[2,4,4,128,576]{3,2,1,0,4:T(4,128)(2,1)} %copy.37) | data formatting | bytes 9437184 | tf_op jit(solution)/shard_map/reshape;reshape | solution.py:22
  115.2 4.7 %slice.52 = bf16[4096,512]{0,1:T(8,128)(2,1)} slice(bf16[4096,576]{0,1:T(8,128)(2,1)} %reshape_reshape.3), slice={[0:4096], [0:512]} | slice | bytes 8388608 | tf_op jit(solution)/shard_map/slice | solution.py:73
  119.8 6.5 %copy.45 = bf16[4096,512]{1,0:T(8,128)(2,1)} copy(bf16[4096,512]{0,1:T(8,128)(2,1)} %slice.52) | data formatting | bytes 8388608
  126.4 73.9 %while.11 = (s32[]{:T(128)}, bf16[4,128,4,128]{1,3,2,0:T(8,128)(2,1)}, bf16[4,512,4,128]{1,3,2,0:T(8,128)(2,1)}, bf16[4,128,4,576]{1,3,2,0:T(8,128)(2,1)S(1)}, b...) while((s32[]{:T(128)}, ...), condition=%wide.region_4.5_spmd.clone, body=%wide.region_1.4_spmd.clone.sunk | while | flops 4650770944 | bytes 70461056 | solution.py:90
  126.4 5.4 %fusion.73 = f32[128,4,4096]{2,0,1:T(8,128)S(1)} fusion(bf16[4096,576]{0,1:T(8,128)(2,1)} %get-tuple-element.158, bf16[4,128,4,576]{1,3,2,0:T(8,128)(2,1)S(1)} %get-tuple-element.157, s32[]{:T(128)} %get-tuple-element.145), kind=kOutput, calls=%fused_computation.6.clone.1 | convolution fusion | flops 2415919104 | bytes 13697028 | tf_op jit(solution)/shard_map/while/body/eval_jaxpr/tgc,sc->tgs/dot_general | solution.py:78
  131.8 0.4 fusion.74
  132.2 2.5 fusion.75
  134.7 0.4 copy-done.2
  135.1 9.5 %fusion.76 = bf16[4,128,4,128]{1,3,2,0:T(8,128)(2,1)} fusion(bf16[4,128,4,128]{1,3,2,0:T(8,128)(2,1)} %get-tuple-element.146, s32[]{:T(128)} %get-tuple-element.145, bf16[4096,512]{1,0:T(8,128)(2,1)} %get-tuple-element.159, f32[128,4]{0,1:T(4,128)S(1)} %fusion.75, bf16[4,512,4,128]{1,3,2,0:T(8,128)(2,1)} %get-tuple-element.156, ...), kind=kOutput, calls=%fused_computation.19.clone.1 | convolution fusion | flops 2225410560 | bytes 13765632 | tf_op jit(solution)/shard_map/while/body/eval_jaxpr/tgc,cgv->tgv/dot_general | solution.py:86
  144.5 5.4 %fusion.73 = f32[128,4,4096]{2,0,1:T(8,128)S(1)} fusion(bf16[4096,576]{0,1:T(8,128)(2,1)} %get-tuple-element.158, bf16[4,128,4,576]{1,3,2,0:T(8,128)(2,1)S(1)} %get-tuple-element.157, s32[]{:T(128)} %get-tuple-element.145), kind=kOutput, calls=%fused_computation.6.clone.1 | convolution fusion | flops 2415919104 | bytes 13697028 | tf_op jit(solution)/shard_map/while/body/eval_jaxpr/tgc,sc->tgs/dot_general | solution.py:78
  150.0 0.4 fusion.74
  150.4 2.5 fusion.75
  152.9 0.4 copy-done.2
  153.2 9.5 %fusion.76 = bf16[4,128,4,128]{1,3,2,0:T(8,128)(2,1)} fusion(bf16[4,128,4,128]{1,3,2,0:T(8,128)(2,1)} %get-tuple-element.146, s32[]{:T(128)} %get-tuple-element.145, bf16[4096,512]{1,0:T(8,128)(2,1)} %get-tuple-element.159, f32[128,4]{0,1:T(4,128)S(1)} %fusion.75, bf16[4,512,4,128]{1,3,2,0:T(8,128)(2,1)} %get-tuple-element.156, ...), kind=kOutput, calls=%fused_computation.19.clone.1 | convolution fusion | flops 2225410560 | bytes 13765632 | tf_op jit(solution)/shard_map/while/body/eval_jaxpr/tgc,cgv->tgv/dot_general | solution.py:86
  162.7 5.4 %fusion.73 = f32[128,4,4096]{2,0,1:T(8,128)S(1)} fusion(bf16[4096,576]{0,1:T(8,128)(2,1)} %get-tuple-element.158, bf16[4,128,4,576]{1,3,2,0:T(8,128)(2,1)S(1)} %get-tuple-element.157, s32[]{:T(128)} %get-tuple-element.145), kind=kOutput, calls=%fused_computation.6.clone.1 | convolution fusion | flops 2415919104 | bytes 13697028 | tf_op jit(solution)/shard_map/while/body/eval_jaxpr/tgc,sc->tgs/dot_general | solution.py:78
  168.1 0.4 fusion.74
  168.5 2.5 fusion.75
  171.0 0.4 copy-done.2
  171.4 9.3 %fusion.76 = bf16[4,128,4,128]{1,3,2,0:T(8,128)(2,1)} fusion(bf16[4,128,4,128]{1,3,2,0:T(8,128)(2,1)} %get-tuple-element.146, s32[]{:T(128)} %get-tuple-element.145, bf16[4096,512]{1,0:T(8,128)(2,1)} %get-tuple-element.159, f32[128,4]{0,1:T(4,128)S(1)} %fusion.75, bf16[4,512,4,128]{1,3,2,0:T(8,128)(2,1)} %get-tuple-element.156, ...), kind=kOutput, calls=%fused_computation.19.clone.1 | convolution fusion | flops 2225410560 | bytes 13765632 | tf_op jit(solution)/shard_map/while/body/eval_jaxpr/tgc,cgv->tgv/dot_general | solution.py:86
  180.7 5.4 %fusion.73 = f32[128,4,4096]{2,0,1:T(8,128)S(1)} fusion(bf16[4096,576]{0,1:T(8,128)(2,1)} %get-tuple-element.158, bf16[4,128,4,576]{1,3,2,0:T(8,128)(2,1)S(1)} %get-tuple-element.157, s32[]{:T(128)} %get-tuple-element.145), kind=kOutput, calls=%fused_computation.6.clone.1 | convolution fusion | flops 2415919104 | bytes 13697028 | tf_op jit(solution)/shard_map/while/body/eval_jaxpr/tgc,sc->tgs/dot_general | solution.py:78
  186.1 0.4 fusion.74
  186.5 2.5 fusion.75
  189.0 0.4 copy-done.2
  189.4 10.8 %fusion.76 = bf16[4,128,4,128]{1,3,2,0:T(8,128)(2,1)} fusion(bf16[4,128,4,128]{1,3,2,0:T(8,128)(2,1)} %get-tuple-element.146, s32[]{:T(128)} %get-tuple-element.145, bf16[4096,512]{1,0:T(8,128)(2,1)} %get-tuple-element.159, f32[128,4]{0,1:T(4,128)S(1)} %fusion.75, bf16[4,512,4,128]{1,3,2,0:T(8,128)(2,1)} %get-tuple-element.156, ...), kind=kOutput, calls=%fused_computation.19.clone.1 | convolution fusion | flops 2225410560 | bytes 13765632 | tf_op jit(solution)/shard_map/while/body/eval_jaxpr/tgc,cgv->tgv/dot_general | solution.py:86
  200.2 134.8 %all-gather.8.cloned.1.call-done = bf16[2048,7168]{0,1:T(8,128)(2,1)} async-done(((bf16[2048,224]{0,1:T(8,128)(2,1)}), bf16[2048,7168]{0,1:T(8,128)(2,1)}) %all-gather.8.cloned.1.call-update) | async-done | bytes 29360144 | tf_op jit(solution)/shard_map/all_gather | solution.py:125
  335.0 14.1 %convolution_bitcast_fusion = f32[4,128,1792]{2,1,0:T(8,128)S(1)} fusion(bf16[128,2048,1]{0,1,2:T(8,128)(2,1)} %bitcast.83, bf16[4,1792,2048]{2,1,0:T(8,128)(2,1)} %bitcast.74), kind=kOutput, calls=%fused_computation.32 | convolution fusion | flops 3758096384 | bytes 33554432 | tf_op jit(solution)/shard_map/dot_general | solution.py:124
  349.0 45.9 %all_to_all.5 = f32[4,128,1792]{2,1,0:T(8,128)} all-to-all(f32[4,128,1792]{2,1,0:T(8,128)S(1)} %convolution_bitcast_fusion), channel_id=1, replica_groups=mesh['dp_0'=2,'dp_1'=4,'dp_2'=4,'head'=4] {'head'}, dimensions={0} | all-to-all | bytes 7340032 | tf_op jit(solution)/shard_map/all_to_all | solution.py:46
  394.9 3.1 reduce_sum.28
  (25 shorter events, 0.3 us)
Async XLA Ops:
  6.5 36.7 %copy-start = (bf16[128,1536]{1,0:T(8,128)(2,1)S(1)}, bf16[128,1536]{1,0:T(8,128)(2,1)}, u32[]{:S(2)}) copy-start(bf16[128,1536]{1,0:T(8,128)(2,1)} %param.10) | copy-start | bytes 1179652
  6.5 35.7 %all-gather.4.cloned.1.call-start = ((), (), s32[]{:S(2)}) async-start(), calls=%async_computation.1 | async-start | bytes 1474560 | tf_op jit(solution)/shard_map/all_gather | solution.py:28
  17.5 80.8 %all-gather.6.cloned.1.call-start = ((), (), s32[]{:S(2)}) async-start(), calls=%async_computation.2 | async-start | bytes 5898240 | tf_op jit(solution)/shard_map/all_gather | solution.py:28
  42.3 292.7 %all-gather.8.cloned.1.call-start = ((), (), s32[]{:S(2)}) async-start(), calls=%async_computation.3 | async-start | bytes 30277632 | tf_op jit(solution)/shard_map/all_gather | solution.py:125
  55.7 3.8 copy-start.3
  60.3 5.8 %copy-start.4 = (s32[4096]{0:T(1024)S(1)}, s32[4096]{0:T(1024)}, u32[]{:S(2)}) copy-start(s32[4096]{0:T(1024)} %param.17) | copy-start | bytes 49156
  131.8 3.3 copy-start.2
  150.0 3.3 copy-start.2
  168.1 3.3 copy-start.2
  186.1 3.3 copy-start.2
  335.0 63.1 %copy-start.1 = (bf16[128,1536]{1,0:T(8,128)(2,1)S(1)}, bf16[128,1536]{1,0:T(8,128)(2,1)}, u32[]{:S(2)}) copy-start(bf16[128,1536]{1,0:T(8,128)(2,1)} %param.10) | copy-start | bytes 1179652
Sparse Core Ops, SparseCore 0:
  17.6 24.6 all-gather.3
  43.9 54.2 all-gather.5
  101.4 233.5 all-gather.7
where the time goes:
time: 410 us; the launch traced here: 405 us
  waiting for transfers between devices  192 us (47%)
  matrix products  80.6 us (20%)
  blocking collectives  53.8 us (13%)
  local copies, waits for them, and re-layouts  43.7 us (11%)
  other arithmetic  20.2 us (5%)
  between operations  13.9 us (3%)
    all_gather x1, waiting for transfers between devices, local(): lax.all_gather(w_o, DP, axis=1, tiled=True)  135 us
    all_gather x2, waiting for transfers between devices, stacked_from(): pieces = lax.all_gather(pieces, axes[k], axis=0, tiled=True)  56.8 us
    all_to_all x1, blocking collectives, summed_on_arrival(): pieces = lax.all_to_all(cut_along(array, dim, size), axis, 0, 0, tiled=True)  45.9 us
    dot_general x4, matrix products, one_group(): jnp.einsum('tgc,cgv->tgv', context, w_group, preferred_element_type=jnp.f...  39.1 us
    dot_general x4, matrix products, one_group(): jnp.einsum('tgc,sc->tgs', chosen, keys, preferred_element_type=jnp.float32)  21.6 us
    dot_general x1, matrix products, local(): jnp.dot(attended, lax.all_gather(w_o, DP, axis=1, tiled=True), preferred_...  14.1 us
    unnamed x11, local copies, waits for them, and re-layouts  13.4 us
    sub x4, other arithmetic, one_group(): lifted = jnp.exp(scores - row_max)  9.9 us
  transfers between devices with their start and end apart: 3, of which 3 were waited for; matrix products, arithmetic and copies ran while one was open for 30% of the time, Pallas kernels for 0%

commit v1 on v0

v1 whole, which is shorter than its diff:
```python
import functools
import math

import jax
import jax.numpy as jnp
from jax import lax
from jax.experimental import pallas as pl
from jax.experimental.pallas import tpu as pltpu
from jax.sharding import Mesh
from jax.sharding import PartitionSpec as P

KVR = 512
ROPE = 64
NOPE = 128
VD = 128
WIDE = KVR + ROPE
AXES = ("xh", "z", "y", "xl", "c")
DP = ("xh", "z", "y")
HEAD = ("xl", "c")
MESH = pl.DeviceIdType.MESH

HEADS = 16
CHUNKS = 4
PER = HEADS // CHUNKS
HALF = 64
BLOCK = 512
LOG2E = 1.4426950408889634
EPS = 1e-06

CROSS = 0
SWAP = 1
D1 = 2
D1H = 6
D2 = 10
D2H = 26
PAIR = 42
WFULL = 74
WHALF = 78
WPAIR = 80
ABASE = 84
APAIR, AX, AZ, AZH = 0, 1, 2, 6
ASTRIDE = 10
OUT = ABASE + ASTRIDE * CHUNKS
NSEM = OUT + 4


def turn(values, cosine, sine):
    swapped = jnp.concatenate([values[:, ROPE // 2 :], values[:, : ROPE // 2]], axis=1)
    return values * cosine + swapped * sine


def body(
    q_lat,
    kv_lat,
    gain,
    cos_tab,
    sin_tab,
    bias,
    wq_hbm,
    wkv_hbm,
    wo_hbm,
    out_ref,
    out_sem,
    in_sem,
    local_sem,
    qx,
    wq,
    wkv,
    keys,
    qs,
    ctx,
    astage,
    ag,
    wg,
    part,
    outgoing,
    landed,
    m_ref,
    l_ref,
    acc_ref,
):
    xh, z, y, xl, c = (lax.axis_index(a) for a in AXES)
    d1 = y + c * (z - y)
    d2 = z + c * (y - z)

    def place(t, o1, o2):
        a = lax.rem(d1 + o1 + 4, 4)
        b = lax.rem(d2 + o2 + 4, 4)
        zz = b + c * (a - b)
        yy = a + c * (b - a)
        xx = xh + t - 2 * xh * t
        return xx, zz, yy

    def unit(t, o1, o2):
        xx, zz, yy = place(t, o1, o2)
        return xx * 16 + zz * 4 + yy

    def near(o1, o2):
        _, zz, yy = place(0, o1, o2)
        return (xh, zz, yy, xl, c)

    def copy(src, dst, number, device, leaving=None):
        return pltpu.make_async_remote_copy(
            src_ref=src,
            dst_ref=dst,
            send_sem=out_sem.at[number if leaving is None else leaving],
            recv_sem=in_sem.at[number],
            device_id=device,
            device_id_type=MESH,
        )

    me = unit(0, 0, 0)
    partner = (xh, z, y, xl, 1 - c)
    cross = (1 - xh, z, y, 1 - xl, c)
    swap_peer = (1 - xh, 3 - z, y, 1 - xl, c)
    across = (1 - xh, z, y, xl, c)
    up_y = (xh, z, lax.rem(y + 1, 4), xl, c)
    down_y = (xh, z, lax.rem(y + 3, 4), xl, c)
    up_z = (xh, lax.rem(z + 1, 4), y, xl, c)
    down_z = (xh, lax.rem(z + 3, 4), y, xl, c)
    owners = [(c, k, y, xh, z // 2) for k in range(4)]
    makers = [(xl, 2 * c + k // 2, y, k % 2, xh) for k in range(4)]
    same = lambda u, v: 1 - jnp.minimum((u - v) * (u - v), 1)
    mine = same(c, xh) * same(xl, xh) * same(z // 2, c)

    for j in range(8):
        pltpu.make_async_copy(wq_hbm.at[:, pl.ds(j * 384, 384)], wq.at[j], local_sem.at[j]).start()
    pltpu.make_async_copy(wkv_hbm, wkv, local_sem.at[8]).start()
    pltpu.make_async_copy(wo_hbm, wg.at[y, c], local_sem.at[9]).start()

    barrier = pltpu.get_barrier_semaphore()
    for peer in (partner, cross, swap_peer, across, up_y, down_y, up_z, down_z):
        pl.semaphore_signal(barrier, inc=1, device_id=peer, device_id_type=MESH)
    for k in range(4):

        @pl.when((mine == 0) | (z != k))
        def _(k=k):
            pl.semaphore_signal(barrier, inc=1, device_id=owners[k], device_id_type=MESH)

    for k in range(4):
        maker = makers[k]

        @pl.when((mine == 0) | (maker[1] != z) | (maker[3] != xl))
        def _(maker=maker):
            pl.semaphore_signal(barrier, inc=1, device_id=maker, device_id_type=MESH)

    rows = kv_lat[pl.ds(pl.multiple_of(c * HALF, HALF), HALF), :].astype(jnp.float32)
    latent = rows[:, :KVR]
    inverse = lax.rsqrt(jnp.mean(latent * latent, axis=-1, keepdims=True) + EPS)
    keys[me, c, :, :KVR] = (latent * inverse * gain[...]).astype(jnp.bfloat16)
    keys[me, c, :, KVR:] = turn(
        rows[:, KVR:], cos_tab[: HALF, :], sin_tab[: HALF, :]
    ).astype(jnp.bfloat16)
    qx[xh] = q_lat[xh]

    pl.semaphore_wait(barrier, 16 - 2 * mine)

    def key(t, o1, o2, which=None):
        ref = keys.at[unit(t, o1, o2), c]
        if which is None:
            return ref
        return ref.at[pl.ds(32 * which, 32)]

    def key_copy(number, t, o1, o2, device, which=None):
        ref = key(t, o1, o2, which)
        return copy(ref, ref, number, device)

    offsets = (0, 1, 3, 2)

    def spread(k):
        t, o = k % 2, offsets[k // 2]
        key_copy(D2 + 2 * k, t, o, 0, near(0, 1)).start()
        key_copy(D2 + 2 * k + 1, t, o, 0, near(0, -1)).start()
        key_copy(PAIR + k, t, o, 0, partner).start()

    key_copy(CROSS, 0, 0, 0, cross).start()
    swap = copy(q_lat.at[1 - xh], qx.at[xh], SWAP, swap_peer)
    swap_in = copy(q_lat.at[1 - xh], qx.at[1 - xh], SWAP, swap_peer)
    key_copy(D1, 0, 0, 0, near(1, 0)).start()
    key_copy(D1 + 1, 0, 0, 0, near(-1, 0)).start()
    swap.start()
    spread(0)
    key_copy(CROSS, 1, 0, 0, cross).wait_recv()
    key_copy(D1 + 2, 1, 0, 0, near(1, 0)).start()
    key_copy(D1 + 3, 1, 0, 0, near(-1, 0)).start()
    spread(1)
    for t in range(2):
        key_copy(D1 + 2 * t, t, -1, 0, near(1, 0)).wait_recv()
        key_copy(D1H + 2 * t, t, -1, 0, near(1, 0), 0).start()
        spread(4 + t)
        key_copy(D1 + 2 * t + 1, t, 1, 0, near(-1, 0)).wait_recv()
        key_copy(D1H + 2 * t + 1, t, 1, 0, near(-1, 0), 1).start()
        spread(2 + t)
    swap_in.wait_recv()
    pltpu.make_async_copy(wkv_hbm, wkv, local_sem.at[8]).wait()

    def project(j):
        pltpu.make_async_copy(
            wq_hbm.at[:, pl.ds(0, 384)], wq.at[j], local_sem.at[j]
        ).wait()
        both = jnp.dot(
            qx[...].reshape(2 * HALF, -1), wq[j], preferred_element_type=jnp.float32
        ).astype(jnp.bfloat16)
        for e in range(2):
            h = 2 * j + e
            plain = both[:, e * 192 : e * 192 + NOPE]
            roped = both[:, e * 192 + NOPE : (e + 1) * 192].astype(jnp.float32)
            w_key = wkv[:, pl.ds(pl.multiple_of(h * 256, 256), NOPE)]
            absorbed = lax.dot_general(
                plain, w_key, (((1,), (1,)), ((), ())), preferred_element_type=jnp.float32
            ).astype(jnp.bfloat16)
            turned = turn(roped, cos_tab[HALF:, :], sin_tab[HALF:, :]).astype(jnp.bfloat16)
            for half in range(2):
                qs[half, h, :, :KVR] = absorbed[half * HALF : (half + 1) * HALF]
                qs[half, h, :, KVR:] = turned[half * HALF : (half + 1) * HALF]

    def relay(k):
        t = lax.rem(k, 2)
        q = k // 2
        o = q + q // 2 - 2 * (q // 3)
        key_copy(D2 + 2 * k, t, o, -1, near(0, 1)).wait_recv()
        key_copy(D2H + 2 * k, t, o, -1, near(0, 1), 0).start()
        key_copy(PAIR + 8 + k, t, o, -1, partner).start()
        key_copy(D2 + 2 * k + 1, t, o, 1, near(0, -1)).wait_recv()
        key_copy(D2H + 2 * k + 1, t, o, 1, near(0, -1), 1).start()
        key_copy(PAIR + 16 + k, t, o, 1, partner).start()

    project(0)
    for t in range(2):
        key_copy(D1H + 2 * t, t, 2, 0, near(1, 0), 0).wait_recv()
        key_copy(D1H + 2 * t + 1, t, 2, 0, near(-1, 0), 1).wait_recv()
        spread(6 + t)

    w_mine = wg.at[y, c]
    pltpu.make_async_copy(wo_hbm, w_mine, local_sem.at[9]).wait()
    span = wo_hbm.shape[0] // 2

    def w_copy(number, row, device, which):
        ref = wg.at[row, c, pl.ds(which * span, span)]
        return copy(ref, ref, number, device)

    def project_step(k, carry):
        relay(k - 1)
        project(k)
        return carry

    lax.fori_loop(1, 8, project_step, 0)
    relay(7)
    for which in range(2):
        w_copy(WFULL + which, y, up_y, which).start()
        w_copy(WFULL + 3 - which, y, down_y, 1 - which).start()

    def w_pair(row, number):
        return copy(wg.at[row, c], wg.at[row, c], WPAIR + number, partner)

    def w_pair_in(row, number):
        return copy(wg.at[row, 1 - c], wg.at[row, 1 - c], WPAIR + number, partner)

    w_pair(y, 0).start()

    def last_in(k, carry):
        t = lax.rem(k, 2)
        q = k // 2
        o = q + q // 2 - 2 * (q // 3)
        key_copy(D2H + 2 * k, t, o, 2, near(0, 1), 0).wait_recv()
        key_copy(D2H + 2 * k + 1, t, o, 2, near(0, -1), 1).wait_recv()
        key_copy(PAIR + 24 + k, t, o, 2, partner).start()
        return carry

    lax.fori_loop(0, 8, last_in, 0)

    def pair_in(n, carry):
        ref = keys.at[0, 1 - c]
        copy(ref, ref, PAIR + n, partner).wait_recv()
        return carry

    lax.fori_loop(0, 32, pair_in, 0)

    z_low = z + xh * (3 - 2 * z)
    shard = (z_low * 4 + y, 16 + (3 - z_low) * 4 + y)
    scale = LOG2E / math.sqrt(NOPE + ROPE)
    tile_rows = PER * HALF
    reach = BLOCK // 128

    def attend(half, g):
        where = shard[half]
        blocks = where // reach
        m_ref[...] = jnp.full_like(m_ref, -1e30)
        l_ref[...] = jnp.zeros_like(l_ref)
        acc_ref[...] = jnp.zeros_like(acc_ref)
        query = qs[half, pl.ds(g * PER, PER)].reshape(tile_rows, WIDE)

        def step(b, causal):
            block = keys[pl.ds(b * reach, reach)].reshape(BLOCK, WIDE)
            scores = lax.dot_general(
                query, block, (((1,), (1,)), ((), ())), preferred_element_type=jnp.float32
            )
            scores = scores * scale + bias[pl.ds(b, 1), :]
            if causal is not None:
                scores = (scores.reshape(PER, HALF, BLOCK) + causal[None]).reshape(
                    tile_rows, BLOCK
                )
            before = m_ref[...]
            m_new = jnp.maximum(before, jnp.max(scores, axis=1, keepdims=True))
            alpha = jnp.exp2(before - m_new)
            lifted = jnp.exp2(scores - jnp.concatenate([m_new] * (BLOCK // 128), axis=1))
            total = l_ref[...] * alpha
            for k in range(BLOCK // 128):
                total = total + lifted[:, k * 128 : (k + 1) * 128]
            l_ref[...] = total
            m_ref[...] = m_new
            acc_ref[...] = acc_ref[...] * jnp.concatenate([alpha] * (KVR // 128), axis=1) + jnp.dot(
                lifted.astype(jnp.bfloat16), block[:, :KVR], preferred_element_type=jnp.float32
            )

        def open_step(b, carry):
            step(b, None)
            return carry

        lax.fori_loop(0, blocks, open_step, 0)
        token = where * 128 + xh * HALF + lax.broadcasted_iota(jnp.int32, (HALF, BLOCK), 0)
        position = blocks * BLOCK + lax.broadcasted_iota(jnp.int32, (HALF, BLOCK), 1)
        step(blocks, jnp.where(position <= token, 0.0, -1e30))
        total = jnp.sum(l_ref[...], axis=1, keepdims=True)
        ctx[half] = (acc_ref[...] / total).astype(jnp.bfloat16).reshape(PER, HALF, KVR)

    here = xh * 4 + z

    def values(g):
        for n in range(PER):
            h = g * PER + n
            context = jnp.concatenate([ctx[0, n], ctx[1, n]], axis=0)
            w_value = wkv[:, pl.ds(pl.multiple_of(h * 256 + NOPE, NOPE), VD)]
            attended = jnp.dot(context, w_value, preferred_element_type=jnp.float32).astype(
                jnp.bfloat16
            )
            astage[g, 0, :, n * VD : (n + 1) * VD] = attended[:HALF]
            astage[g, 1, :, n * VD : (n + 1) * VD] = attended[HALF:]
        ag[here, g, c] = astage[g, c]

    def a_copy(g, number, t, o, device, which=None):
        slot = (xh + t - 2 * xh * t) * 4 + lax.rem(z + o + 4, 4)
        ref = ag.at[slot, g]
        if which is not None:
            ref = ref.at[which]
        return copy(ref, ref, ABASE + ASTRIDE * g + number, device)

    def pair_copy(g):
        return copy(
            astage.at[g, 1 - c], ag.at[here, g, c], ABASE + ASTRIDE * g + APAIR, partner
        )

    def pair_copy_in(g):
        ref = ag.at[here, g, 1 - c]
        return copy(ref, ref, ABASE + ASTRIDE * g + APAIR, partner)

    def stage1(g):
        pair_copy_in(g).wait_recv()
        a_copy(g, AX, 0, 0, across).start()
        a_copy(g, AZ, 0, 0, up_z).start()
        a_copy(g, AZ + 1, 0, 0, down_z).start()

    def stage2(g):
        a_copy(g, AX, 1, 0, across).wait_recv()
        a_copy(g, AZ + 2, 1, 0, up_z).start()
        a_copy(g, AZ + 3, 1, 0, down_z).start()
        for t in range(1):
            a_copy(g, AZ + 2 * t, t, -1, up_z).wait_recv()
            a_copy(g, AZH + 2 * t, t, -1, up_z, 0).start()
            a_copy(g, AZ + 2 * t + 1, t, 1, down_z).wait_recv()
            a_copy(g, AZH + 2 * t + 1, t, 1, down_z, 1).start()

    def stage3(g):
        t = 1
        a_copy(g, AZ + 2 * t, t, -1, up_z).wait_recv()
        a_copy(g, AZH + 2 * t, t, -1, up_z, 0).start()
        a_copy(g, AZ + 2 * t + 1, t, 1, down_z).wait_recv()
        a_copy(g, AZH + 2 * t + 1, t, 1, down_z, 1).start()

    def stage4(g):
        for t in range(2):
            a_copy(g, AZH + 2 * t, t, 2, up_z, 0).wait_recv()
            a_copy(g, AZH + 2 * t + 1, t, 2, down_z, 1).wait_recv()

    def w_relay(which):
        if which == 0:
            w_copy(WFULL, lax.rem(y + 3, 4), up_y, 0).wait_recv()
            w_copy(WHALF, lax.rem(y + 3, 4), up_y, 0).start()
        else:
            w_copy(WFULL + 3, lax.rem(y + 1, 4), down_y, 1).wait_recv()
            w_copy(WHALF + 1, lax.rem(y + 1, 4), down_y, 1).start()

    def chunk(g, first):
        attend(0, g)
        if not first:
            stage1(g - 1)
        attend(1, g)
        values(g)
        pair_copy(g).start()

    chunk(0, True)
    chunk(1, False)
    w_relay(0)
    w_relay(1)
    chunk(2, False)
    stage2(0)
    chunk(3, False)
    stage3(0)
    stage2(1)
    stage1(3)
    w_copy(WFULL + 1, lax.rem(y + 3, 4), up_y, 1).wait_recv()
    w_pair(lax.rem(y + 3, 4), 1).start()
    w_copy(WFULL + 2, lax.rem(y + 1, 4), down_y, 0).wait_recv()
    w_pair(lax.rem(y + 1, 4), 2).start()
    stage3(1)
    stage2(2)
    w_copy(WHALF, lax.rem(y + 2, 4), up_y, 0).wait_recv()
    w_copy(WHALF + 1, lax.rem(y + 2, 4), down_y, 1).wait_recv()
    w_pair(lax.rem(y + 2, 4), 3).start()
    for k, o in enumerate((0, 3, 1, 2)):
        w_pair_in(lax.rem(y + o, 4), k).wait_recv()

    depth = PER * VD

    def multiply(g):
        def columns(k, carry):
            total = jnp.zeros((8 * HALF, 224), jnp.float32) if g == 0 else part[k]
            for core in range(2):
                total = total + jnp.dot(
                    ag[:, g, core].reshape(8 * HALF, depth),
                    wg[k, core, g * depth : (g + 1) * depth, :],
                    preferred_element_type=jnp.float32,
                )
            if g < CHUNKS - 1:
                part[k] = total
            else:
                rounded = total.astype(jnp.bfloat16)
                for xs in range(2):
                    for zs in range(4):
                        alike = 1 - (xs + c - 2 * xs * c)
                        to = (3 - zs) + alike * (2 * zs - 3)
                        s = xs * 4 + zs
                        outgoing[to, xs, k] = rounded[s * HALF : (s + 1) * HALF]
            return carry

        lax.fori_loop(0, 4, columns, 0)

    stage4(0)
    multiply(0)
    stage3(2)
    stage2(3)
    stage4(1)
    multiply(1)
    stage3(3)
    stage4(2)
    multiply(2)
    stage4(3)
    multiply(3)

    slot = lax.rem(z, 2) * 2 + xl
    for k in range(4):

        @pl.when((mine == 0) | (z != k))
        def _(k=k):
            copy(outgoing.at[k], landed.at[slot], OUT + slot, owners[k], OUT + k).start()

        @pl.when((mine == 1) & (z == k))
        def _(k=k):
            landed[slot] = outgoing[k]

    for k in range(4):
        maker = makers[k]

        @pl.when((mine == 0) | (maker[1] != z) | (maker[3] != xl))
        def _(k=k):
            copy(outgoing.at[k], landed.at[k], OUT + k, owners[k]).wait_recv()

    for zz in range(2):
        for xs in range(2):
            for k in range(4):
                total = landed[2 * zz, xs, k].astype(jnp.float32) + landed[
                    2 * zz + 1, xs, k
                ].astype(jnp.float32)
                out_ref[zz * 4 + k, xs * HALF : (xs + 1) * HALF, :] = total.astype(jnp.bfloat16)

    full = keys.at[0, 0]
    part_key = keys.at[0, 0, pl.ds(0, 32)]

    def sent(ref, number):
        copy(ref, ref, number, partner).wait_send()

    def drain(ref, first, count):
        def one(n, carry):
            sent(ref, first + n)
            return carry

        lax.fori_loop(0, count, one, 0)

    sent(full, CROSS)
    sent(qx.at[0], SWAP)
    drain(full, D1, 4)
    drain(part_key, D1H, 4)
    drain(full, D2, 16)
    drain(part_key, D2H, 16)
    drain(full, PAIR, 32)
    drain(wg.at[0, 0, pl.ds(0, span)], WFULL, 4)
    drain(wg.at[0, 0, pl.ds(0, span)], WHALF, 2)
    drain(wg.at[0, 0], WPAIR, 4)
    for g in range(CHUNKS):
        at = ABASE + ASTRIDE * g
        sent(astage.at[g, 0], at + APAIR)
        sent(ag.at[0, 0], at + AX)
        drain(ag.at[0, 0], at + AZ, 4)
        drain(ag.at[0, 0, 0], at + AZH, 4)
    for k in range(4):

        @pl.when((mine == 0) | (z != k))
        def _(k=k):
            sent(outgoing.at[0], OUT + k)


def local(q_latent, kv_latent, kv_gain, w_q_b, w_kv_b, w_o, prompt_len, response_mask):
    xh, z, y, _, c = (lax.axis_index(a) for a in AXES)
    z_low = z + xh * (3 - 2 * z)
    row = jnp.arange(HALF, dtype=jnp.int32)
    me = xh * 16 + z * 4 + y
    positions = jnp.concatenate(
        [
            me * 128 + c * HALF + row,
            (z_low * 4 + y) * 128 + xh * HALF + row,
            (16 + (3 - z_low) * 4 + y) * 128 + xh * HALF + row,
        ]
    ).astype(jnp.float32)
    lane = jnp.arange(ROPE, dtype=jnp.int32)
    frequency = 10000.0 ** (-(lane % (ROPE // 2)).astype(jnp.float32) * 2.0 / ROPE)
    angles = positions[:, None] * frequency[None, :]
    cos_tab = jnp.cos(angles)
    sin_tab = jnp.sin(angles) * jnp.where(lane < ROPE // 2, -1.0, 1.0)[None, :]
    everywhere = jnp.arange(response_mask.shape[0], dtype=jnp.int32)
    usable = (everywhere < prompt_len[0]) | (response_mask == 1)
    bias = jnp.where(usable, 0.0, -1e30).astype(jnp.float32).reshape(-1, BLOCK)
    vmem = pl.BlockSpec(memory_space=pltpu.VMEM)
    hbm = pl.BlockSpec(memory_space=pl.ANY)
    bf16 = jnp.bfloat16
    depth = PER * VD
    result = pl.pallas_call(
        body,
        out_shape=jax.ShapeDtypeStruct((8, 128, 224), bf16),
        in_specs=[vmem] * 6 + [hbm] * 3,
        out_specs=vmem,
        scratch_shapes=[
            pltpu.SemaphoreType.DMA((NSEM,)),
            pltpu.SemaphoreType.DMA((NSEM,)),
            pltpu.SemaphoreType.DMA((10,)),
            pltpu.VMEM((2, HALF, 1536), bf16),
            pltpu.VMEM((8, 1536, 384), bf16),
            pltpu.VMEM((512, 4096), bf16),
            pltpu.VMEM((32, 2, HALF, WIDE), bf16),
            pltpu.VMEM((2, HEADS, HALF, WIDE), bf16),
            pltpu.VMEM((2, PER, HALF, KVR), bf16),
            pltpu.VMEM((CHUNKS, 2, HALF, depth), bf16),
            pltpu.VMEM((8, CHUNKS, 2, HALF, depth), bf16),
            pltpu.VMEM((4, 2, 2048, 224), bf16),
            pltpu.VMEM((4, 8 * HALF, 224), jnp.float32),
            pltpu.VMEM((4, 2, 4, HALF, 224), bf16),
            pltpu.VMEM((4, 2, 4, HALF, 224), bf16),
            pltpu.VMEM((PER * HALF, 128), jnp.float32),
            pltpu.VMEM((PER * HALF, 128), jnp.float32),
            pltpu.VMEM((PER * HALF, KVR), jnp.float32),
        ],
        compiler_params=pltpu.CompilerParams(
            collective_id=0, has_side_effects=True, vmem_limit_bytes=67000000
        ),
        cost_estimate=pl.CostEstimate(
            flops=20_000_000_000, bytes_accessed=16_000_000, transcendentals=0
        ),
        name="layer",
    )(
        q_latent.reshape(2, HALF, -1),
        kv_latent,
        kv_gain.reshape(1, -1),
        cos_tab,
        sin_tab,
        bias,
        w_q_b,
        w_kv_b,
        w_o,
    )
    return result.transpose(1, 0, 2).reshape(128, -1)


def solution(mesh):
    finer = Mesh(mesh.devices.reshape(2, 4, 4, 2, 2), AXES)
    placed = (
        P(DP, None),
        P(DP, None),
        P(),
        P(None, HEAD),
        P(None, HEAD),
        P(HEAD, DP),
        P(),
        P(),
    )
    return jax.shard_map(
        local, mesh=finer, in_specs=placed, out_specs=P(DP, HEAD), check_vma=False
    )
```

time: 410 us -> 126 us (0.31)
  the two profiles are of different devices: /device:TPU:100 before, /device:TPU:98 now
where the time goes in v1:
time: 126 us
  Pallas kernels  116 us (92%)
  local copies, waits for them, and re-layouts  6.84 us (5%)
  other arithmetic  1.94 us (2%)
    pallas_call x1, Pallas kernels, local(): pl.pallas_call(body, out_shape=jax.ShapeDtypeStruct((8, 128, 224), bf16),...  116 us
    unnamed x2, local copies, waits for them, and re-layouts  3.95 us

profile of v1, /device:TPU:98, one launch (start us, length us, event | category | flops | bytes accessed | tf_op | source)
XLA Modules:
  0.0 125.5 jit_solution(11968984833454777399)
XLA Ops:
  0.7 0.1 add_convert_fusion
  0.8 0.7 fusion.2
  1.5 0.6 reshape.51.bias
  2.1 1.7 %copy.11.kv_lat = bf16[128,576]{1,0:T(8,128)(2,1)} copy(bf16[128,576]{0,1:T(8,128)(2,1)} %param.9) | data formatting | bytes 294912 | tf_op args[1]
  3.8 1.1 fusion
  4.9 2.2 %copy.12.wo_hbm = bf16[2048,224]{1,0:T(8,128)(2,1)} copy(bf16[2048,224]{0,1:T(8,128)(2,1)} %param.13) | data formatting | bytes 1835008 | tf_op args[5]
  7.2 116.1 %layer.1 = bf16[8,128,224]{2,1,0:T(8,128)(2,1)} custom-call(bf16[2,64,1536]{2,1,0:T(8,128)(2,1)} %bitcast.8, bf16[128,576]{1,0:T(8,128)(2,1)} %copy.11.kv_lat, f32[1,512]{1,0:T(1,128)} %bitcast.9, f32[192,64]{1,0:T(8,128)} %get-tuple-element.6.cos_tab, f32[192,64]{1,0:T(8,128)} %get-tuple-element.5.sin_tab, f32[8,512]{1,0:T(8,128)} %reshape.51.bias, ...), custom_call_target="tpu_custom_call" | custom-call | flops 20000000000 | bytes 16000000 | tf_op jit(solution)/shard_map/layer/pallas_call | solution.py:546
  123.2 1.3 %copy.13 = bf16[128,8,224]{0,2,1:T(8,128)(2,1)S(1)} copy(bf16[128,8,224]{2,0,1:T(8,128)(2,1)} %bitcast.7) | data formatting | bytes 917504 | tf_op jit(solution)/shard_map/transpose | solution.py:589
  124.5 1.0 copy.14
  (3 shorter events, 0.0 us)

commit v2 on v1

v2 whole, which is shorter than its diff:
```python
import functools
import math

import jax
import jax.numpy as jnp
import numpy as np
from jax import lax
from jax.experimental import pallas as pl
from jax.experimental.pallas import tpu as pltpu
from jax.sharding import Mesh
from jax.sharding import PartitionSpec as P

KVR = 512
ROPE = 64
NOPE = 128
VD = 128
WIDE = KVR + ROPE
AXES = ("xh", "z", "y", "xl", "c")
DP = ("xh", "z", "y")
HEAD = ("xl", "c")
MESH = pl.DeviceIdType.MESH

HEADS = 16
CHUNKS = 4
PER = HEADS // CHUNKS
SUB = 2
PART = PER // SUB
HALF = 64
BLOCK = 512
LOG2E = 1.4426950408889634
EPS = 1e-06

CROSS = 0
SWAP = 1
D1 = 2
D1H = 6
D2 = 10
D2H = 26
PAIR = 42
WFULL = 74
WHALF = 78
WPAIR = 80
ABASE = 84
APAIR, AX, AZ, AZH = 0, 1, 2, 6
ASTRIDE = 10
OUT = ABASE + ASTRIDE * CHUNKS
XSUM = OUT + 4
NSEM = XSUM + 4


def turn(values, cosine, sine):
    swapped = jnp.concatenate([values[:, ROPE // 2 :], values[:, : ROPE // 2]], axis=1)
    return values * cosine + swapped * sine


def body(
    q_lat,
    kv_lat,
    gain,
    table,
    live,
    prompt,
    wq_hbm,
    wkv_hbm,
    wo_hbm,
    out_ref,
    out_sem,
    in_sem,
    local_sem,
    qx,
    wq,
    wkv,
    keys,
    qs,
    ctx,
    astage,
    ag,
    wg,
    part,
    outgoing,
    summand,
    landed,
    bias,
    m_ref,
    l_ref,
    acc_ref,
):
    xh, z, y, xl, c = (lax.axis_index(a) for a in AXES)
    d1 = y + c * (z - y)
    d2 = z + c * (y - z)

    def place(t, o1, o2):
        a = lax.rem(d1 + o1 + 4, 4)
        b = lax.rem(d2 + o2 + 4, 4)
        zz = b + c * (a - b)
        yy = a + c * (b - a)
        xx = xh + t - 2 * xh * t
        return xx, zz, yy

    def unit(t, o1, o2):
        xx, zz, yy = place(t, o1, o2)
        return xx * 16 + zz * 4 + yy

    def near(o1, o2):
        _, zz, yy = place(0, o1, o2)
        return (xh, zz, yy, xl, c)

    def copy(src, dst, number, device, leaving=None):
        return pltpu.make_async_remote_copy(
            src_ref=src,
            dst_ref=dst,
            send_sem=out_sem.at[number if leaving is None else leaving],
            recv_sem=in_sem.at[number],
            device_id=device,
            device_id_type=MESH,
        )

    me = unit(0, 0, 0)
    partner = (xh, z, y, xl, 1 - c)
    cross = (1 - xh, z, y, 1 - xl, c)
    swap_peer = (1 - xh, 3 - z, y, 1 - xl, c)
    across = (1 - xh, z, y, xl, c)
    up_y = (xh, z, lax.rem(y + 1, 4), xl, c)
    down_y = (xh, z, lax.rem(y + 3, 4), xl, c)
    up_z = (xh, lax.rem(z + 1, 4), y, xl, c)
    down_z = (xh, lax.rem(z + 3, 4), y, xl, c)
    owners = [(c, k, y, xh, z // 2) for k in range(4)]
    makers = [(xl, 2 * c + k, y, xh, xh) for k in range(2)]
    beside = (xh, z, y, 1 - xl, c)
    same = lambda u, v: 1 - jnp.minimum((u - v) * (u - v), 1)
    sums = same(xl, c)
    mine = same(c, xh) * same(xl, xh) * same(z // 2, c)
    z_low = z + xh * (3 - 2 * z)
    shard = (z_low * 4 + y, 16 + (3 - z_low) * 4 + y)

    with jax.named_scope("start"):
        for j in range(8):
            pltpu.make_async_copy(wq_hbm.at[:, pl.ds(j * 384, 384)], wq.at[j], local_sem.at[j]).start()
        pltpu.make_async_copy(wkv_hbm, wkv, local_sem.at[8]).start()
        pltpu.make_async_copy(wo_hbm, wg.at[c, y], local_sem.at[9]).start()

    barrier = pltpu.get_barrier_semaphore()
    for peer in (partner, cross, swap_peer, across, beside, up_y, down_y, up_z, down_z):
        pl.semaphore_signal(barrier, inc=1, device_id=peer, device_id_type=MESH)
    for k in range(2):

        @pl.when((mine == 0) | (2 * c + k != z))
        def _(k=k):
            pl.semaphore_signal(barrier, inc=1, device_id=makers[k], device_id_type=MESH)

    with jax.named_scope("norm"):
        lane = lax.broadcasted_iota(jnp.int32, (1, ROPE), 1)
        sign = jnp.where(lane < ROPE // 2, -1.0, 1.0)

        def angles(m):
            cos_a, sin_a = table[2, pl.ds(m, 1), :], table[3, pl.ds(m, 1), :]
            cos_b, sin_b = table[0], table[1]
            return cos_a * cos_b - sin_a * sin_b, (sin_a * cos_b + cos_a * sin_b) * sign

        turned_rows = kv_lat[...].astype(jnp.float32).T
        rows = jnp.where(c == 0, turned_rows[:HALF], turned_rows[HALF:])
        latent = rows[:, :KVR]
        inverse = lax.rsqrt(jnp.mean(latent * latent, axis=-1, keepdims=True) + EPS)
        keys[me, c, :, :KVR] = (latent * inverse * gain[...]).astype(jnp.bfloat16)
        keys[me, c, :, KVR:] = turn(rows[:, KVR:], *angles(me * 2 + c)).astype(jnp.bfloat16)
        qx[xh] = q_lat[xh]
        spot = lax.broadcasted_iota(jnp.int32, (32, 128), 0) * 128 + lax.broadcasted_iota(
            jnp.int32, (32, 128), 1
        )
        usable = (spot < prompt[0]) | (live[...] == 1)
        masked = jnp.where(usable, 0.0, -1e30)
        for r in range(32):
            b, at = r // (BLOCK // 128), r % (BLOCK // 128)
            bias[b : b + 1, at * 128 : (at + 1) * 128] = masked[r : r + 1]

    with jax.named_scope("barrier"):
        pl.semaphore_wait(barrier, 9 + sums * (4 - mine))

    def key(t, o1, o2, which=None):
        ref = keys.at[unit(t, o1, o2), c]
        if which is None:
            return ref
        return ref.at[pl.ds(32 * which, 32)]

    def key_copy(number, t, o1, o2, device, which=None):
        ref = key(t, o1, o2, which)
        return copy(ref, ref, number, device)

    offsets = (0, 1, 3, 2)

    def spread(k):
        t, o = k % 2, offsets[k // 2]
        key_copy(D2 + 2 * k, t, o, 0, near(0, 1)).start()
        key_copy(D2 + 2 * k + 1, t, o, 0, near(0, -1)).start()
        key_copy(PAIR + k, t, o, 0, partner).start()

    with jax.named_scope("spread"):
        key_copy(CROSS, 0, 0, 0, cross).start()
        swap = copy(q_lat.at[1 - xh], qx.at[xh], SWAP, swap_peer)
        swap_in = copy(q_lat.at[1 - xh], qx.at[1 - xh], SWAP, swap_peer)
        key_copy(D1, 0, 0, 0, near(1, 0)).start()
        key_copy(D1 + 1, 0, 0, 0, near(-1, 0)).start()
        swap.start()
        spread(0)
        with jax.named_scope('cross'):
            key_copy(CROSS, 1, 0, 0, cross).wait_recv()
        key_copy(D1 + 2, 1, 0, 0, near(1, 0)).start()
        key_copy(D1 + 3, 1, 0, 0, near(-1, 0)).start()
        spread(1)
        for t in range(2):
            key_copy(D1 + 2 * t, t, -1, 0, near(1, 0)).wait_recv()
            key_copy(D1H + 2 * t, t, -1, 0, near(1, 0), 0).start()
            spread(4 + t)
            key_copy(D1 + 2 * t + 1, t, 1, 0, near(-1, 0)).wait_recv()
            key_copy(D1H + 2 * t + 1, t, 1, 0, near(-1, 0), 1).start()
            spread(2 + t)
        with jax.named_scope('swap'):
            swap_in.wait_recv()
        with jax.named_scope('wkv'):
            pltpu.make_async_copy(wkv_hbm, wkv, local_sem.at[8]).wait()

    tables = [angles(2 * where + xh) for where in shard]

    def project(j):
        pltpu.make_async_copy(
            wq_hbm.at[:, pl.ds(0, 384)], wq.at[j], local_sem.at[j]
        ).wait()
        both = jnp.dot(
            qx[...].reshape(2 * HALF, -1), wq[j], preferred_element_type=jnp.float32
        ).astype(jnp.bfloat16)
        for e in range(2):
            h = 2 * j + e
            plain = both[:, e * 192 : e * 192 + NOPE]
            roped = both[:, e * 192 + NOPE : (e + 1) * 192].astype(jnp.float32)
            w_key = wkv[:, pl.ds(pl.multiple_of(h * 256, 256), NOPE)]
            absorbed = lax.dot_general(
                plain, w_key, (((1,), (1,)), ((), ())), preferred_element_type=jnp.float32
            ).astype(jnp.bfloat16)
            for half in range(2):
                mine_rows = slice(half * HALF, (half + 1) * HALF)
                qs[half, h, :, :KVR] = absorbed[mine_rows]
                qs[half, h, :, KVR:] = turn(roped[mine_rows], *tables[half]).astype(jnp.bfloat16)

    def relay(k):
        t = lax.rem(k, 2)
        q = k // 2
        o = q + q // 2 - 2 * (q // 3)
        key_copy(D2 + 2 * k, t, o, -1, near(0, 1)).wait_recv()
        key_copy(D2H + 2 * k, t, o, -1, near(0, 1), 0).start()
        key_copy(PAIR + 8 + k, t, o, -1, partner).start()
        key_copy(D2 + 2 * k + 1, t, o, 1, near(0, -1)).wait_recv()
        key_copy(D2H + 2 * k + 1, t, o, 1, near(0, -1), 1).start()
        key_copy(PAIR + 16 + k, t, o, 1, partner).start()

    with jax.named_scope("project"):
        project(0)
    with jax.named_scope("ring1"):
        for t in range(2):
            key_copy(D1H + 2 * t, t, 2, 0, near(1, 0), 0).wait_recv()
            key_copy(D1H + 2 * t + 1, t, 2, 0, near(-1, 0), 1).wait_recv()
            spread(6 + t)

    w_mine = wg.at[c, y]
    pltpu.make_async_copy(wo_hbm, w_mine, local_sem.at[9]).wait()
    span = wo_hbm.shape[0] // 2

    def w_copy(number, row, device, which):
        ref = wg.at[c, row, pl.ds(which * span, span)]
        return copy(ref, ref, number, device)

    def project_step(k, carry):
        with jax.named_scope("relay"):
            relay(k - 1)
        with jax.named_scope("project"):
            project(k)
        return carry

    lax.fori_loop(1, 8, project_step, 0)
    relay(7)
    for which in range(2):
        w_copy(WFULL + which, y, up_y, which).start()
        w_copy(WFULL + 3 - which, y, down_y, 1 - which).start()

    def w_pair(row, number):
        return copy(wg.at[c, row], wg.at[c, row], WPAIR + number, partner)

    def w_pair_in(row, number):
        return copy(wg.at[1 - c, row], wg.at[1 - c, row], WPAIR + number, partner)

    w_pair(y, 0).start()

    def last_in(k, carry):
        t = lax.rem(k, 2)
        q = k // 2
        o = q + q // 2 - 2 * (q // 3)
        key_copy(D2H + 2 * k, t, o, 2, near(0, 1), 0).wait_recv()
        key_copy(D2H + 2 * k + 1, t, o, 2, near(0, -1), 1).wait_recv()
        key_copy(PAIR + 24 + k, t, o, 2, partner).start()
        return carry

    with jax.named_scope("last_in"):
        lax.fori_loop(0, 8, last_in, 0)

    def pair_in(n, carry):
        ref = keys.at[0, 1 - c]
        copy(ref, ref, PAIR + n, partner).wait_recv()
        return carry

    with jax.named_scope("pair_in"):
        lax.fori_loop(0, 32, pair_in, 0)

    scale = LOG2E / math.sqrt(NOPE + ROPE)
    tile_rows = PART * HALF
    reach = BLOCK // 128

    def attend(half, g):
        where = shard[half]
        blocks = where // reach
        m_ref[...] = jnp.full_like(m_ref, -1e30)
        l_ref[...] = jnp.zeros_like(l_ref)
        acc_ref[...] = jnp.zeros_like(acc_ref)

        def step(b, causal):
            block = keys[pl.ds(b * reach, reach)].reshape(BLOCK, WIDE)
            hidden = bias[pl.ds(b, 1), :]
            for n in range(SUB):
                query = qs[half, pl.ds(g * PER + n * PART, PART)].reshape(tile_rows, WIDE)
                scores = lax.dot_general(
                    query, block, (((1,), (1,)), ((), ())), preferred_element_type=jnp.float32
                )
                scores = scores * scale + hidden
                if causal is not None:
                    scores = (scores.reshape(PART, HALF, BLOCK) + causal[None]).reshape(
                        tile_rows, BLOCK
                    )
                before = m_ref[n]
                m_new = jnp.maximum(before, jnp.max(scores, axis=1, keepdims=True))
                alpha = jnp.exp2(before - m_new)
                lifted = jnp.exp2(scores - jnp.concatenate([m_new] * (BLOCK // 128), axis=1))
                total = l_ref[n] * alpha
                for k in range(BLOCK // 128):
                    total = total + lifted[:, k * 128 : (k + 1) * 128]
                l_ref[n] = total
                m_ref[n] = m_new
                acc_ref[n] = acc_ref[n] * jnp.concatenate([alpha] * (KVR // 128), axis=1) + jnp.dot(
                    lifted.astype(jnp.bfloat16), block[:, :KVR], preferred_element_type=jnp.float32
                )

        def open_step(b, carry):
            step(b, None)
            return carry

        lax.fori_loop(0, blocks, open_step, 0)
        token = where * 128 + xh * HALF + lax.broadcasted_iota(jnp.int32, (HALF, BLOCK), 0)
        position = blocks * BLOCK + lax.broadcasted_iota(jnp.int32, (HALF, BLOCK), 1)
        step(blocks, jnp.where(position <= token, 0.0, -1e30))
        for n in range(SUB):
            total = jnp.sum(l_ref[n], axis=1, keepdims=True)
            ctx[half, n * PART : (n + 1) * PART] = (
                (acc_ref[n] / total).astype(jnp.bfloat16).reshape(PART, HALF, KVR)
            )

    here = xh * 4 + z

    def values(g):
        for n in range(PER):
            h = g * PER + n
            context = jnp.concatenate([ctx[0, n], ctx[1, n]], axis=0)
            w_value = wkv[:, pl.ds(pl.multiple_of(h * 256 + NOPE, NOPE), VD)]
            attended = jnp.dot(context, w_value, preferred_element_type=jnp.float32).astype(
                jnp.bfloat16
            )
            astage[g, 0, :, n * VD : (n + 1) * VD] = attended[:HALF]
            astage[g, 1, :, n * VD : (n + 1) * VD] = attended[HALF:]
        ag[here, g, c] = astage[g, c]

    def a_copy(g, number, t, o, device, which=None):
        slot = (xh + t - 2 * xh * t) * 4 + lax.rem(z + o + 4, 4)
        ref = ag.at[slot, g]
        if which is not None:
            ref = ref.at[which]
        return copy(ref, ref, ABASE + ASTRIDE * g + number, device)

    def pair_copy(g):
        return copy(
            astage.at[g, 1 - c], ag.at[here, g, c], ABASE + ASTRIDE * g + APAIR, partner
        )

    def pair_copy_in(g):
        ref = ag.at[here, g, 1 - c]
        return copy(ref, ref, ABASE + ASTRIDE * g + APAIR, partner)

    def stage1(g):
        pair_copy_in(g).wait_recv()
        a_copy(g, AX, 0, 0, across).start()
        a_copy(g, AZ, 0, 0, up_z).start()
        a_copy(g, AZ + 1, 0, 0, down_z).start()

    def stage2(g):
        a_copy(g, AX, 1, 0, across).wait_recv()
        a_copy(g, AZ + 2, 1, 0, up_z).start()
        a_copy(g, AZ + 3, 1, 0, down_z).start()
        for t in range(1):
            a_copy(g, AZ + 2 * t, t, -1, up_z).wait_recv()
            a_copy(g, AZH + 2 * t, t, -1, up_z, 0).start()
            a_copy(g, AZ + 2 * t + 1, t, 1, down_z).wait_recv()
            a_copy(g, AZH + 2 * t + 1, t, 1, down_z, 1).start()

    def stage3(g):
        t = 1
        a_copy(g, AZ + 2 * t, t, -1, up_z).wait_recv()
        a_copy(g, AZH + 2 * t, t, -1, up_z, 0).start()
        a_copy(g, AZ + 2 * t + 1, t, 1, down_z).wait_recv()
        a_copy(g, AZH + 2 * t + 1, t, 1, down_z, 1).start()

    def stage4(g):
        for t in range(2):
            a_copy(g, AZH + 2 * t, t, 2, up_z, 0).wait_recv()
            a_copy(g, AZH + 2 * t + 1, t, 2, down_z, 1).wait_recv()

    def w_relay(which):
        if which == 0:
            w_copy(WFULL, lax.rem(y + 3, 4), up_y, 0).wait_recv()
            w_copy(WHALF, lax.rem(y + 3, 4), up_y, 0).start()
        else:
            w_copy(WFULL + 3, lax.rem(y + 1, 4), down_y, 1).wait_recv()
            w_copy(WHALF + 1, lax.rem(y + 1, 4), down_y, 1).start()

    def chunk(g, first):
        with jax.named_scope("attend_low"):
            attend(0, g)
        if not first:
            with jax.named_scope("stage1"):
                stage1(g - 1)
        with jax.named_scope("attend_high"):
            attend(1, g)
        with jax.named_scope("values"):
            values(g)
        pair_copy(g).start()

    chunk(0, True)
    chunk(1, False)
    with jax.named_scope("w_relay"):
        w_relay(0)
        w_relay(1)
    chunk(2, False)
    with jax.named_scope("stage2_0"):
        stage2(0)
    chunk(3, False)
    with jax.named_scope("stage3_0"):
        stage3(0)
    with jax.named_scope("stage2_1"):
        stage2(1)
    with jax.named_scope("stage1_3"):
        stage1(3)
    with jax.named_scope("w_in"):
        w_copy(WFULL + 1, lax.rem(y + 3, 4), up_y, 1).wait_recv()
        w_pair(lax.rem(y + 3, 4), 1).start()
        w_copy(WFULL + 2, lax.rem(y + 1, 4), down_y, 0).wait_recv()
        w_pair(lax.rem(y + 1, 4), 2).start()
    with jax.named_scope("stage3_1"):
        stage3(1)
    with jax.named_scope("stage2_2"):
        stage2(2)
    with jax.named_scope("w_in2"):
        w_copy(WHALF, lax.rem(y + 2, 4), up_y, 0).wait_recv()
        w_copy(WHALF + 1, lax.rem(y + 2, 4), down_y, 1).wait_recv()
        w_pair(lax.rem(y + 2, 4), 3).start()
        for k, o in enumerate((0, 3, 1, 2)):
            w_pair_in(lax.rem(y + o, 4), k).wait_recv()

    depth = PER * VD

    def multiply(g):
        def product(first):
            total = jnp.zeros((2 * 2 * HALF, 4 * 224), jnp.float32)
            for core in range(2):
                total = total + lax.dot_general(
                    ag[pl.ds(first, 4), g, core].reshape(4 * HALF, depth),
                    wg[core, :, :, g * depth : (g + 1) * depth].reshape(4 * 224, depth),
                    (((1,), (1,)), ((), ())),
                    preferred_element_type=jnp.float32,
                )
            return total

        for xs in range(2):
            total = product(4 * xs)
            if g > 0:
                total = total + part[xs]
            part[xs] = total

    with jax.named_scope("stage4_0"):
        stage4(0)
    with jax.named_scope("multiply"):
        multiply(0)
    with jax.named_scope("stage3_2"):
        stage3(2)
    with jax.named_scope("stage2_3"):
        stage2(3)
    with jax.named_scope("stage4_1"):
        stage4(1)
    with jax.named_scope("multiply"):
        multiply(1)
    with jax.named_scope("stage3_3"):
        stage3(3)
    with jax.named_scope("stage4_2"):
        stage4(2)
    with jax.named_scope("multiply"):
        multiply(2)
    with jax.named_scope("stage4_3"):
        stage4(3)
    with jax.named_scope("multiply"):
        multiply(3)

    def gathered(k):
        first = k + (3 - 2 * k) * c
        second = 3 - first
        low = part[0, pl.ds(pl.multiple_of(first * HALF, HALF), HALF), :]
        high = part[1, pl.ds(pl.multiple_of(second * HALF, HALF), HALF), :]
        return low, high

    with jax.named_scope("half_out"):

        @pl.when(sums == 0)
        def _():
            for k in range(4):
                low, high = gathered(k)
                outgoing[k, :HALF] = low.astype(jnp.bfloat16)
                outgoing[k, HALF:] = high.astype(jnp.bfloat16)
                copy(outgoing.at[k], summand.at[k], XSUM + k, beside).start()

    with jax.named_scope("whole_out"):

        @pl.when(sums == 1)
        def _():
            for k in range(4):
                copy(outgoing.at[k], summand.at[k], XSUM + k, beside).wait_recv()
                low, high = gathered(k)
                outgoing[k, :HALF] = (low + summand[k, :HALF].astype(jnp.float32)).astype(
                    jnp.bfloat16
                )
                outgoing[k, HALF:] = (high + summand[k, HALF:].astype(jnp.float32)).astype(
                    jnp.bfloat16
                )

                @pl.when((mine == 0) | (z != k))
                def _():
                    copy(
                        outgoing.at[k], landed.at[lax.rem(z, 2)], OUT + lax.rem(z, 2), owners[k], OUT + k
                    ).start()

                @pl.when((mine == 1) & (z == k))
                def _():
                    landed[lax.rem(z, 2)] = outgoing[k]

    with jax.named_scope("finish"):
        for k in range(2):

            @pl.when((mine == 0) | (2 * c + k != z))
            def _(k=k):
                copy(outgoing.at[k], landed.at[k], OUT + k, owners[k]).wait_recv()

            out_ref[:, k * 896 : (k + 1) * 896] = landed[k]

    with jax.named_scope("drain"):
        full = keys.at[0, 0]
        part_key = keys.at[0, 0, pl.ds(0, 32)]

        def sent(ref, number):
            copy(ref, ref, number, partner).wait_send()

        def drain(ref, first, count):
            def one(n, carry):
                sent(ref, first + n)
                return carry

            lax.fori_loop(0, count, one, 0)

        sent(full, CROSS)
        sent(qx.at[0], SWAP)
        drain(full, D1, 4)
        drain(part_key, D1H, 4)
        drain(full, D2, 16)
        drain(part_key, D2H, 16)
        drain(full, PAIR, 32)
        drain(wg.at[0, 0, pl.ds(0, span)], WFULL, 4)
        drain(wg.at[0, 0, pl.ds(0, span)], WHALF, 2)
        drain(wg.at[0, 0], WPAIR, 4)
        for g in range(CHUNKS):
            at = ABASE + ASTRIDE * g
            sent(astage.at[g, 0], at + APAIR)
            sent(ag.at[0, 0], at + AX)
            drain(ag.at[0, 0], at + AZ, 4)
            drain(ag.at[0, 0, 0], at + AZH, 4)
        @pl.when(sums == 0)
        def _():
            drain(outgoing.at[0], XSUM, 4)

        for k in range(4):

            @pl.when((sums == 1) & ((mine == 0) | (z != k)))
            def _(k=k):
                sent(outgoing.at[0], OUT + k)


def local(q_latent, kv_latent, kv_gain, w_q_b, w_kv_b, w_o, prompt_len, response_mask):
    frequency = 10000.0 ** (-np.arange(ROPE // 2, dtype=np.float64) * 2.0 / ROPE)
    fine = np.arange(HALF, dtype=np.float64)[:, None] * np.tile(frequency, 2)[None, :]
    table = np.stack([np.cos(fine), np.sin(fine), np.cos(HALF * fine), np.sin(HALF * fine)])
    vmem = pl.BlockSpec(memory_space=pltpu.VMEM)
    hbm = pl.BlockSpec(memory_space=pl.ANY)
    bf16 = jnp.bfloat16
    depth = PER * VD
    result = pl.pallas_call(
        body,
        out_shape=jax.ShapeDtypeStruct((128, 1792), bf16),
        in_specs=[vmem] * 5 + [pl.BlockSpec(memory_space=pltpu.SMEM)] + [hbm] * 3,
        out_specs=vmem,
        scratch_shapes=[
            pltpu.SemaphoreType.DMA((NSEM,)),
            pltpu.SemaphoreType.DMA((NSEM,)),
            pltpu.SemaphoreType.DMA((10,)),
            pltpu.VMEM((2, HALF, 1536), bf16),
            pltpu.VMEM((8, 1536, 384), bf16),
            pltpu.VMEM((512, 4096), bf16),
            pltpu.VMEM((32, 2, HALF, WIDE), bf16),
            pltpu.VMEM((2, HEADS, HALF, WIDE), bf16),
            pltpu.VMEM((2, PER, HALF, KVR), bf16),
            pltpu.VMEM((CHUNKS, 2, HALF, depth), bf16),
            pltpu.VMEM((8, CHUNKS, 2, HALF, depth), bf16),
            pltpu.VMEM((2, 4, 224, 2048), bf16),
            pltpu.VMEM((2, 4 * HALF, 4 * 224), jnp.float32),
            pltpu.VMEM((4, 2 * HALF, 4 * 224), bf16),
            pltpu.VMEM((4, 2 * HALF, 4 * 224), bf16),
            pltpu.VMEM((2, 2 * HALF, 4 * 224), bf16),
            pltpu.VMEM((4096 // BLOCK, BLOCK), jnp.float32),
            pltpu.VMEM((SUB, PART * HALF, 128), jnp.float32),
            pltpu.VMEM((SUB, PART * HALF, 128), jnp.float32),
            pltpu.VMEM((SUB, PART * HALF, KVR), jnp.float32),
        ],
        compiler_params=pltpu.CompilerParams(
            collective_id=0, has_side_effects=True, vmem_limit_bytes=67000000
        ),
        cost_estimate=pl.CostEstimate(
            flops=20_000_000_000, bytes_accessed=16_000_000, transcendentals=0
        ),
        name="layer",
    )(
        q_latent.reshape(2, HALF, -1),
        kv_latent.T,
        kv_gain.reshape(1, -1),
        jnp.asarray(table, jnp.float32),
        response_mask.reshape(32, 128),
        prompt_len,
        w_q_b,
        w_kv_b,
        w_o.T,
    )
    return result


def solution(mesh):
    finer = Mesh(mesh.devices.reshape(2, 4, 4, 2, 2), AXES)
    placed = (
        P(DP, None),
        P(DP, None),
        P(),
        P(None, HEAD),
        P(None, HEAD),
        P(HEAD, DP),
        P(),
        P(),
    )
    return jax.shard_map(
        local, mesh=finer, in_specs=placed, out_specs=P(DP, HEAD), check_vma=False
    )
```

time: 126 us -> 122 us (0.968)
  local copies, waits for them, and re-layouts: 6.84 us -> 1.82 us
  Pallas kernels: 116 us -> 119 us
  other arithmetic: 1.94 us -> 0 us
    pallas_call x1, Pallas kernels: 116 us -> 119 us  [local(): pl.pallas_call(body, out_shape=jax.ShapeDtypeStruct((128, 1792), bf16), i...]
    unnamed x2 -> x1, local copies, waits for them, and re-layouts: 3.95 us -> 1.82 us
    reshape x2 -> x0, local copies, waits for them, and re-layouts: 1.59 us -> none  [the longest x1 0.99 us: local(): return result.transpose(1, 0, 2).reshape(128, -1)]
    transpose x1 -> x0, local copies, waits for them, and re-layouts: 1.3 us -> none  [local(): return result.transpose(1, 0, 2).reshape(128, -1)]
where the time goes in v2:
time: 122 us
  Pallas kernels  119 us (98%)
  local copies, waits for them, and re-layouts  1.82 us (1%)
    pallas_call x1, Pallas kernels, local(): pl.pallas_call(body, out_shape=jax.ShapeDtypeStruct((128, 1792), bf16), i...  119 us

profile of v2, /device:TPU:98, one launch (start us, length us, event | category | flops | bytes accessed | tf_op | source)
XLA Modules:
  0.0 121.9 jit_solution(12450136802879134299)
XLA Ops:
  0.7 119.4 %layer.1 = bf16[128,1792]{1,0:T(8,128)(2,1)} custom-call(bf16[2,64,1536]{2,1,0:T(8,128)(2,1)} %bitcast.6, bf16[576,128]{1,0:T(8,128)(2,1)} %bitcast.7, f32[1,512]{1,0:T(1,128)} %bitcast.9, f32[4,64,64]{2,1,0:T(8,128)} %constant.2.clone.table, s32[32,128]{1,0:T(8,128)} %bitcast.8, s32[1]{0:T(128)S(6)} %copy.11.prompt, bf16[1536,3072]{1,0:T(8,128)(2,1)} %wq_hbm.1, ...), custom_call_target="tpu_custom_call" | custom-call | flops 20000000000 | bytes 16000000 | tf_op jit(solution)/shard_map/layer/pallas_call | solution.py:614
  120.1 1.8 %copy.12 = bf16[128,1792]{1,0:T(8,128)(2,1)} copy(bf16[128,1792]{1,0:T(8,128)(2,1)} %layer.1) | data formatting | bytes 917504

commit v3 on v2

--- a/solution.py
+++ b/solution.py
@@ -22,10 +22,9 @@
 
 HEADS = 16
 CHUNKS = 4
-PER = HEADS // CHUNKS
-SUB = 2
-PART = PER // SUB
+PER = 8
 HALF = 64
+ROWS = 32
 BLOCK = 512
 LOG2E = 1.4426950408889634
 EPS = 1e-06
@@ -41,7 +40,7 @@
 WHALF = 78
 WPAIR = 80
 ABASE = 84
-APAIR, AX, AZ, AZH = 0, 1, 2, 6
+APAIR, AX, AZ, AZH, AX2 = 0, 1, 2, 6, 8
 ASTRIDE = 10
 OUT = ABASE + ASTRIDE * CHUNKS
 XSUM = OUT + 4
@@ -124,11 +123,10 @@
     down_y = (xh, z, lax.rem(y + 3, 4), xl, c)
     up_z = (xh, lax.rem(z + 1, 4), y, xl, c)
     down_z = (xh, lax.rem(z + 3, 4), y, xl, c)
-    owners = [(c, k, y, xh, z // 2) for k in range(4)]
-    makers = [(xl, 2 * c + k, y, xh, xh) for k in range(2)]
+    owners = [[(t, 2 * xl + k, y, xh, z // 2) for k in range(2)] for t in range(2)]
+    makers = [(xl, 2 * c + k % 2, y, z // 2, k // 2) for k in range(4)]
     beside = (xh, z, y, 1 - xl, c)
     same = lambda u, v: 1 - jnp.minimum((u - v) * (u - v), 1)
-    sums = same(xl, c)
     mine = same(c, xh) * same(xl, xh) * same(z // 2, c)
     z_low = z + xh * (3 - 2 * z)
     shard = (z_low * 4 + y, 16 + (3 - z_low) * 4 + y)
@@ -142,9 +140,9 @@
     barrier = pltpu.get_barrier_semaphore()
     for peer in (partner, cross, swap_peer, across, beside, up_y, down_y, up_z, down_z):
         pl.semaphore_signal(barrier, inc=1, device_id=peer, device_id_type=MESH)
-    for k in range(2):
-
-        @pl.when((mine == 0) | (2 * c + k != z))
+    for k in range(4):
+
+        @pl.when((mine == 0) | (makers[k][1] != z) | (k // 2 != c))
         def _(k=k):
             pl.semaphore_signal(barrier, inc=1, device_id=makers[k], device_id_type=MESH)
 
@@ -174,7 +172,7 @@
             bias[b : b + 1, at * 128 : (at + 1) * 128] = masked[r : r + 1]
 
     with jax.named_scope("barrier"):
-        pl.semaphore_wait(barrier, 9 + sums * (4 - mine))
+        pl.semaphore_wait(barrier, 13 - mine)
 
     def key(t, o1, o2, which=None):
         ref = keys.at[unit(t, o1, o2), c]
@@ -289,31 +287,39 @@
 
     w_pair(y, 0).start()
 
-    def last_in(k, carry):
-        t = lax.rem(k, 2)
-        q = k // 2
-        o = q + q // 2 - 2 * (q // 3)
-        key_copy(D2H + 2 * k, t, o, 2, near(0, 1), 0).wait_recv()
-        key_copy(D2H + 2 * k + 1, t, o, 2, near(0, -1), 1).wait_recv()
-        key_copy(PAIR + 24 + k, t, o, 2, partner).start()
-        return carry
+    def last_in(upper):
+        t = xh + upper - 2 * xh * upper
+
+        def one(q, carry):
+            k = 2 * q + t
+            o = q + q // 2 - 2 * (q // 3)
+            key_copy(D2H + 2 * k, t, o, 2, near(0, 1), 0).wait_recv()
+            key_copy(D2H + 2 * k + 1, t, o, 2, near(0, -1), 1).wait_recv()
+            key_copy(PAIR + 24 + k, t, o, 2, partner).start()
+            return carry
+
+        lax.fori_loop(0, 4, one, 0)
+
+    def pair_in(upper):
+        t = xh + upper - 2 * xh * upper
+
+        def one(n, carry):
+            ref = keys.at[0, 1 - c]
+            copy(ref, ref, PAIR + 2 * n + t, partner).wait_recv()
+            return carry
+
+        lax.fori_loop(0, 16, one, 0)
 
     with jax.named_scope("last_in"):
-        lax.fori_loop(0, 8, last_in, 0)
-
-    def pair_in(n, carry):
-        ref = keys.at[0, 1 - c]
-        copy(ref, ref, PAIR + n, partner).wait_recv()
-        return carry
-
+        last_in(0)
     with jax.named_scope("pair_in"):
-        lax.fori_loop(0, 32, pair_in, 0)
+        pair_in(0)
 
     scale = LOG2E / math.sqrt(NOPE + ROPE)
-    tile_rows = PART * HALF
+    tile_rows = HEADS * HALF
     reach = BLOCK // 128
 
-    def attend(half, g):
+    def attend(half, hooks):
         where = shard[half]
         blocks = where // reach
         m_ref[...] = jnp.full_like(m_ref, -1e30)
@@ -322,31 +328,37 @@
 
         def step(b, causal):
             block = keys[pl.ds(b * reach, reach)].reshape(BLOCK, WIDE)
-            hidden = bias[pl.ds(b, 1), :]
-            for n in range(SUB):
-                query = qs[half, pl.ds(g * PER + n * PART, PART)].reshape(tile_rows, WIDE)
-                scores = lax.dot_general(
-                    query, block, (((1,), (1,)), ((), ())), preferred_element_type=jnp.float32
+            scores = lax.dot_general(
+                qs[half].reshape(tile_rows, WIDE),
+                block,
+                (((1,), (1,)), ((), ())),
+                preferred_element_type=jnp.float32,
+            )
+            scores = scores * scale + bias[pl.ds(b, 1), :]
+            if causal is not None:
+                scores = (scores.reshape(HEADS, HALF, BLOCK) + causal[None]).reshape(
+                    tile_rows, BLOCK
                 )
-                scores = scores * scale + hidden
-                if causal is not None:
-                    scores = (scores.reshape(PART, HALF, BLOCK) + causal[None]).reshape(
-                        tile_rows, BLOCK
-                    )
-                before = m_ref[n]
-                m_new = jnp.maximum(before, jnp.max(scores, axis=1, keepdims=True))
-                alpha = jnp.exp2(before - m_new)
-                lifted = jnp.exp2(scores - jnp.concatenate([m_new] * (BLOCK // 128), axis=1))
-                total = l_ref[n] * alpha
-                for k in range(BLOCK // 128):
-                    total = total + lifted[:, k * 128 : (k + 1) * 128]
-                l_ref[n] = total
-                m_ref[n] = m_new
-                acc_ref[n] = acc_ref[n] * jnp.concatenate([alpha] * (KVR // 128), axis=1) + jnp.dot(
-                    lifted.astype(jnp.bfloat16), block[:, :KVR], preferred_element_type=jnp.float32
-                )
+            before = m_ref[...]
+            m_new = jnp.maximum(before, jnp.max(scores, axis=1, keepdims=True))
+            alpha = jnp.exp2(before - m_new)
+            lifted = jnp.exp2(scores - jnp.concatenate([m_new] * (BLOCK // 128), axis=1))
+            total = l_ref[...] * alpha
+            for k in range(BLOCK // 128):
+                total = total + lifted[:, k * 128 : (k + 1) * 128]
+            l_ref[...] = total
+            m_ref[...] = m_new
+            acc_ref[...] = acc_ref[...] * jnp.concatenate([alpha] * (KVR // 128), axis=1) + jnp.dot(
+                lifted.astype(jnp.bfloat16), block[:, :KVR], preferred_element_type=jnp.float32
+            )
 
         def open_step(b, carry):
+            for at, hook in hooks:
+
+                @pl.when(b == at)
+                def _(hook=hook):
+                    hook()
+
             step(b, None)
             return carry
 
@@ -354,25 +366,23 @@
         token = where * 128 + xh * HALF + lax.broadcasted_iota(jnp.int32, (HALF, BLOCK), 0)
         position = blocks * BLOCK + lax.broadcasted_iota(jnp.int32, (HALF, BLOCK), 1)
         step(blocks, jnp.where(position <= token, 0.0, -1e30))
-        for n in range(SUB):
-            total = jnp.sum(l_ref[n], axis=1, keepdims=True)
-            ctx[half, n * PART : (n + 1) * PART] = (
-                (acc_ref[n] / total).astype(jnp.bfloat16).reshape(PART, HALF, KVR)
-            )
+        total = jnp.sum(l_ref[...], axis=1, keepdims=True)
+        ctx[...] = (acc_ref[...] / total).astype(jnp.bfloat16).reshape(HEADS, HALF, KVR)
 
     here = xh * 4 + z
 
-    def values(g):
-        for n in range(PER):
-            h = g * PER + n
-            context = jnp.concatenate([ctx[0, n], ctx[1, n]], axis=0)
-            w_value = wkv[:, pl.ds(pl.multiple_of(h * 256 + NOPE, NOPE), VD)]
-            attended = jnp.dot(context, w_value, preferred_element_type=jnp.float32).astype(
+    def values(half):
+        for h in range(HEADS):
+            w_value = wkv[:, h * 256 + NOPE : (h + 1) * 256]
+            attended = jnp.dot(ctx[h], w_value, preferred_element_type=jnp.float32).astype(
                 jnp.bfloat16
             )
-            astage[g, 0, :, n * VD : (n + 1) * VD] = attended[:HALF]
-            astage[g, 1, :, n * VD : (n + 1) * VD] = attended[HALF:]
-        ag[here, g, c] = astage[g, c]
+            g, at = 2 * half + h // PER, (h % PER) * VD
+            astage[g, 0, :, at : at + VD] = attended[:ROWS]
+            astage[g, 1, :, at : at + VD] = attended[ROWS:]
+        for g in (2 * half, 2 * half + 1):
+            pair_copy(g).start()
+            ag[here, g, c] = astage[g, c]
 
     def a_copy(g, number, t, o, device, which=None):
         slot = (xh + t - 2 * xh * t) * 4 + lax.rem(z + o + 4, 4)
@@ -397,26 +407,25 @@
         a_copy(g, AZ + 1, 0, 0, down_z).start()
 
     def stage2(g):
+        a_copy(g, AZ, 0, -1, up_z).wait_recv()
+        a_copy(g, AZH, 0, -1, up_z, 0).start()
+        a_copy(g, AZ + 1, 0, 1, down_z).wait_recv()
+        a_copy(g, AZH + 1, 0, 1, down_z, 1).start()
+
+    def stage3(g):
         a_copy(g, AX, 1, 0, across).wait_recv()
         a_copy(g, AZ + 2, 1, 0, up_z).start()
         a_copy(g, AZ + 3, 1, 0, down_z).start()
-        for t in range(1):
-            a_copy(g, AZ + 2 * t, t, -1, up_z).wait_recv()
-            a_copy(g, AZH + 2 * t, t, -1, up_z, 0).start()
-            a_copy(g, AZ + 2 * t + 1, t, 1, down_z).wait_recv()
-            a_copy(g, AZH + 2 * t + 1, t, 1, down_z, 1).start()
-
-    def stage3(g):
-        t = 1
-        a_copy(g, AZ + 2 * t, t, -1, up_z).wait_recv()
-        a_copy(g, AZH + 2 * t, t, -1, up_z, 0).start()
-        a_copy(g, AZ + 2 * t + 1, t, 1, down_z).wait_recv()
-        a_copy(g, AZH + 2 * t + 1, t, 1, down_z, 1).start()
 
     def stage4(g):
-        for t in range(2):
-            a_copy(g, AZH + 2 * t, t, 2, up_z, 0).wait_recv()
-            a_copy(g, AZH + 2 * t + 1, t, 2, down_z, 1).wait_recv()
+        a_copy(g, AZH, 0, 2, up_z, 0).wait_recv()
+        a_copy(g, AZH + 1, 0, 2, down_z, 1).wait_recv()
+        a_copy(g, AX2, 0, 2, across).start()
+
+    def stage5(g):
+        a_copy(g, AZ + 2, 1, -1, up_z).wait_recv()
+        a_copy(g, AZ + 3, 1, 1, down_z).wait_recv()
+        a_copy(g, AX2, 1, 2, across).wait_recv()
 
     def w_relay(which):
         if which == 0:
@@ -426,43 +435,13 @@
             w_copy(WFULL + 3, lax.rem(y + 1, 4), down_y, 1).wait_recv()
             w_copy(WHALF + 1, lax.rem(y + 1, 4), down_y, 1).start()
 
-    def chunk(g, first):
-        with jax.named_scope("attend_low"):
-            attend(0, g)
-        if not first:
-            with jax.named_scope("stage1"):
-                stage1(g - 1)
-        with jax.named_scope("attend_high"):
-            attend(1, g)
-        with jax.named_scope("values"):
-            values(g)
-        pair_copy(g).start()
-
-    chunk(0, True)
-    chunk(1, False)
-    with jax.named_scope("w_relay"):
-        w_relay(0)
-        w_relay(1)
-    chunk(2, False)
-    with jax.named_scope("stage2_0"):
-        stage2(0)
-    chunk(3, False)
-    with jax.named_scope("stage3_0"):
-        stage3(0)
-    with jax.named_scope("stage2_1"):
-        stage2(1)
-    with jax.named_scope("stage1_3"):
-        stage1(3)
-    with jax.named_scope("w_in"):
+    def w_middle():
         w_copy(WFULL + 1, lax.rem(y + 3, 4), up_y, 1).wait_recv()
         w_pair(lax.rem(y + 3, 4), 1).start()
         w_copy(WFULL + 2, lax.rem(y + 1, 4), down_y, 0).wait_recv()
         w_pair(lax.rem(y + 1, 4), 2).start()
-    with jax.named_scope("stage3_1"):
-        stage3(1)
-    with jax.named_scope("stage2_2"):
-        stage2(2)
-    with jax.named_scope("w_in2"):
+
+    def w_last():
         w_copy(WHALF, lax.rem(y + 2, 4), up_y, 0).wait_recv()
         w_copy(WHALF + 1, lax.rem(y + 2, 4), down_y, 1).wait_recv()
         w_pair(lax.rem(y + 2, 4), 3).start()
@@ -471,96 +450,144 @@
 
     depth = PER * VD
 
-    def multiply(g):
-        def product(first):
-            total = jnp.zeros((2 * 2 * HALF, 4 * 224), jnp.float32)
-            for core in range(2):
-                total = total + lax.dot_general(
-                    ag[pl.ds(first, 4), g, core].reshape(4 * HALF, depth),
-                    wg[core, :, :, g * depth : (g + 1) * depth].reshape(4 * 224, depth),
-                    (((1,), (1,)), ((), ())),
-                    preferred_element_type=jnp.float32,
-                )
-            return total
-
-        for xs in range(2):
-            total = product(4 * xs)
-            if g > 0:
-                total = total + part[xs]
-            part[xs] = total
-
+    def product(g):
+        total = jnp.zeros((8 * ROWS, 4 * 224), jnp.float32)
+        for core in range(2):
+            total = total + lax.dot_general(
+                ag[:, g, core].reshape(8 * ROWS, depth),
+                wg[core, :, :, (g % 2) * depth : (g % 2 + 1) * depth].reshape(4 * 224, depth),
+                (((1,), (1,)), ((), ())),
+                preferred_element_type=jnp.float32,
+            )
+        return total.reshape(8, ROWS, 4 * 224)
+
+    def slots(half, k):
+        straight, mirrored = k, 3 - k
+        first = straight if half == 0 else mirrored
+        return first, 4 + 3 - first
+
+    def half_out(half):
+        for k in range(2):
+            low, high = slots(half, 2 * (1 - xl) + k)
+            outgoing[half, 0, k, 0] = part[low].astype(jnp.bfloat16)
+            outgoing[half, 0, k, 1] = part[high].astype(jnp.bfloat16)
+            copy(
+                outgoing.at[half, 0, k], summand.at[half, k], XSUM + 2 * half + k, beside
+            ).start()
+
+    def whole_out(half):
+        place_in = lax.rem(z, 2) + 2 * c
+        for k in range(2):
+            row = 2 * xl + k
+            copy(
+                outgoing.at[half, 0, k], summand.at[half, k], XSUM + 2 * half + k, beside
+            ).wait_recv()
+            low, high = slots(half, row)
+            for xs, at in enumerate((low, high)):
+                outgoing[half, 1, k, xs] = (
+                    part[at] + summand[half, k, xs].astype(jnp.float32)
+                ).astype(jnp.bfloat16)
+            own = (mine == 1) & (xh == half) & (z == row)
+
+            @pl.when(jnp.logical_not(own))
+            def _():
+                copy(
+                    outgoing.at[half, 1, k],
+                    landed.at[place_in],
+                    OUT + place_in,
+                    owners[half][k],
+                    OUT + 2 * half + k,
+                ).start()
+
+            @pl.when(own)
+            def _():
+                landed[place_in] = outgoing[half, 1, k]
+
+    def sum_early():
+        part[...] = product(0) + product(1)
+
+    with jax.named_scope("attend_low"):
+        attend(0, ())
+    with jax.named_scope("values"):
+        values(0)
+    with jax.named_scope("last_in"):
+        last_in(1)
+    with jax.named_scope("pair_in"):
+        pair_in(1)
+
+    def hook_a():
+        with jax.named_scope("hook1"):
+            stage1(0)
+            stage1(1)
+
+    def hook_b():
+        with jax.named_scope("hook2"):
+            stage2(0)
+            w_relay(0)
+            w_relay(1)
+
+    def hook_c():
+        with jax.named_scope("hook3"):
+            stage2(1)
+            stage3(0)
+
+    with jax.named_scope("attend_high"):
+        attend(1, ((0, hook_a), (2, hook_b), (3, hook_c)))
+    with jax.named_scope("values"):
+        values(1)
+    with jax.named_scope("stage3_1"):
+        stage3(1)
+    with jax.named_scope("stage1_2"):
+        stage1(2)
+        stage1(3)
     with jax.named_scope("stage4_0"):
         stage4(0)
-    with jax.named_scope("multiply"):
-        multiply(0)
+        stage4(1)
+    with jax.named_scope("stage2_2"):
+        stage2(2)
+    with jax.named_scope("w_middle"):
+        w_middle()
+    with jax.named_scope("stage5_0"):
+        stage5(0)
+        stage5(1)
     with jax.named_scope("stage3_2"):
+        stage2(3)
         stage3(2)
-    with jax.named_scope("stage2_3"):
-        stage2(3)
-    with jax.named_scope("stage4_1"):
-        stage4(1)
-    with jax.named_scope("multiply"):
-        multiply(1)
-    with jax.named_scope("stage3_3"):
         stage3(3)
+    with jax.named_scope("w_last"):
+        w_last()
+    with jax.named_scope("product_low"):
+        sum_early()
+    with jax.named_scope("half_out_low"):
+        half_out(0)
     with jax.named_scope("stage4_2"):
         stage4(2)
-    with jax.named_scope("multiply"):
-        multiply(2)
-    with jax.named_scope("stage4_3"):
         stage4(3)
-    with jax.named_scope("multiply"):
-        multiply(3)
-
-    def gathered(k):
-        first = k + (3 - 2 * k) * c
-        second = 3 - first
-        low = part[0, pl.ds(pl.multiple_of(first * HALF, HALF), HALF), :]
-        high = part[1, pl.ds(pl.multiple_of(second * HALF, HALF), HALF), :]
-        return low, high
-
-    with jax.named_scope("half_out"):
-
-        @pl.when(sums == 0)
-        def _():
-            for k in range(4):
-                low, high = gathered(k)
-                outgoing[k, :HALF] = low.astype(jnp.bfloat16)
-                outgoing[k, HALF:] = high.astype(jnp.bfloat16)
-                copy(outgoing.at[k], summand.at[k], XSUM + k, beside).start()
-
-    with jax.named_scope("whole_out"):
-
-        @pl.when(sums == 1)
-        def _():
-            for k in range(4):
-                copy(outgoing.at[k], summand.at[k], XSUM + k, beside).wait_recv()
-                low, high = gathered(k)
-                outgoing[k, :HALF] = (low + summand[k, :HALF].astype(jnp.float32)).astype(
-                    jnp.bfloat16
-                )
-                outgoing[k, HALF:] = (high + summand[k, HALF:].astype(jnp.float32)).astype(
-                    jnp.bfloat16
-                )
-
-                @pl.when((mine == 0) | (z != k))
-                def _():
-                    copy(
-                        outgoing.at[k], landed.at[lax.rem(z, 2)], OUT + lax.rem(z, 2), owners[k], OUT + k
-                    ).start()
-
-                @pl.when((mine == 1) & (z == k))
-                def _():
-                    landed[lax.rem(z, 2)] = outgoing[k]
+    with jax.named_scope("whole_out_low"):
+        whole_out(0)
+    with jax.named_scope("stage5_2"):
+        stage5(2)
+    with jax.named_scope("product_high"):
+        part[...] = product(2)
+    with jax.named_scope("stage5_3"):
+        stage5(3)
+    with jax.named_scope("product_high"):
+        part[...] = part[...] + product(3)
+    with jax.named_scope("half_out_high"):
+        half_out(1)
+    with jax.named_scope("whole_out_high"):
+        whole_out(1)
 
     with jax.named_scope("finish"):
-        for k in range(2):
-
-            @pl.when((mine == 0) | (2 * c + k != z))
+        for k in range(4):
+
+            @pl.when((mine == 0) | (makers[k][1] != z) | (k // 2 != c))
             def _(k=k):
-                copy(outgoing.at[k], landed.at[k], OUT + k, owners[k]).wait_recv()
-
-            out_ref[:, k * 896 : (k + 1) * 896] = landed[k]
+                copy(landed.at[k], landed.at[k], OUT + k, partner).wait_recv()
+
+            for xs in range(2):
+                at = xs * HALF + (k // 2) * ROWS
+                out_ref[at : at + ROWS, (k % 2) * 896 : (k % 2 + 1) * 896] = landed[k, xs]
 
     with jax.named_scope("drain"):
         full = keys.at[0, 0]
@@ -591,16 +618,16 @@
             sent(astage.at[g, 0], at + APAIR)
             sent(ag.at[0, 0], at + AX)
             drain(ag.at[0, 0], at + AZ, 4)
-            drain(ag.at[0, 0, 0], at + AZH, 4)
-        @pl.when(sums == 0)
-        def _():
-            drain(outgoing.at[0], XSUM, 4)
-
-        for k in range(4):
-
-            @pl.when((sums == 1) & ((mine == 0) | (z != k)))
-            def _(k=k):
-                sent(outgoing.at[0], OUT + k)
+            drain(ag.at[0, 0, 0], at + AZH, 2)
+            sent(ag.at[0, 0], at + AX2)
+        drain(summand.at[0, 0], XSUM, 4)
+        for half in range(2):
+            for k in range(2):
+                own = (mine == 1) & (xh == half) & (z == 2 * xl + k)
+
+                @pl.when(jnp.logical_not(own))
+                def _(half=half, k=k):
+                    sent(landed.at[0], OUT + 2 * half + k)
 
 
 def local(q_latent, kv_latent, kv_gain, w_q_b, w_kv_b, w_o, prompt_len, response_mask):
@@ -625,18 +652,18 @@
             pltpu.VMEM((512, 4096), bf16),
             pltpu.VMEM((32, 2, HALF, WIDE), bf16),
             pltpu.VMEM((2, HEADS, HALF, WIDE), bf16),
-            pltpu.VMEM((2, PER, HALF, KVR), bf16),
-            pltpu.VMEM((CHUNKS, 2, HALF, depth), bf16),
-            pltpu.VMEM((8, CHUNKS, 2, HALF, depth), bf16),
+            pltpu.VMEM((HEADS, HALF, KVR), bf16),
+            pltpu.VMEM((CHUNKS, 2, ROWS, depth), bf16),
+            pltpu.VMEM((8, CHUNKS, 2, ROWS, depth), bf16),
             pltpu.VMEM((2, 4, 224, 2048), bf16),
-            pltpu.VMEM((2, 4 * HALF, 4 * 224), jnp.float32),
-            pltpu.VMEM((4, 2 * HALF, 4 * 224), bf16),
-            pltpu.VMEM((4, 2 * HALF, 4 * 224), bf16),
-            pltpu.VMEM((2, 2 * HALF, 4 * 224), bf16),
+            pltpu.VMEM((8, ROWS, 4 * 224), jnp.float32),
+            pltpu.VMEM((2, 2, 2, 2, ROWS, 4 * 224), bf16),
+            pltpu.VMEM((2, 2, 2, ROWS, 4 * 224), bf16),
+            pltpu.VMEM((4, 2, ROWS, 4 * 224), bf16),
             pltpu.VMEM((4096 // BLOCK, BLOCK), jnp.float32),
-            pltpu.VMEM((SUB, PART * HALF, 128), jnp.float32),
-            pltpu.VMEM((SUB, PART * HALF, 128), jnp.float32),
-            pltpu.VMEM((SUB, PART * HALF, KVR), jnp.float32),
+            pltpu.VMEM((HEADS * HALF, 128), jnp.float32),
+            pltpu.VMEM((HEADS * HALF, 128), jnp.float32),
+            pltpu.VMEM((HEADS * HALF, KVR), jnp.float32),
         ],
         compiler_params=pltpu.CompilerParams(
             collective_id=0, has_side_effects=True, vmem_limit_bytes=67000000

time: 122 us -> 110 us (0.902)
  the two profiles are of different devices: /device:TPU:98 before, /device:TPU:100 now
where the time goes in v3:
time: 110 us; the launch traced here: 109 us
  Pallas kernels  107 us (97%)
  local copies, waits for them, and re-layouts  1.82 us (2%)
    pallas_call x1, Pallas kernels, local(): pl.pallas_call(body, out_shape=jax.ShapeDtypeStruct((128, 1792), bf16), i...  107 us

profile of v3, /device:TPU:100, one launch (start us, length us, event | category | flops | bytes accessed | tf_op | source)
XLA Modules:
  0.0 109.4 jit_solution(17529104749122141401)
XLA Ops:
  0.7 107.0 %layer.1 = bf16[128,1792]{1,0:T(8,128)(2,1)} custom-call(bf16[2,64,1536]{2,1,0:T(8,128)(2,1)} %bitcast.6, bf16[576,128]{1,0:T(8,128)(2,1)} %bitcast.7, f32[1,512]{1,0:T(1,128)} %bitcast.9, f32[4,64,64]{2,1,0:T(8,128)} %constant.2.clone.table, s32[32,128]{1,0:T(8,128)} %bitcast.8, s32[1]{0:T(128)S(6)} %copy.11.prompt, bf16[1536,3072]{1,0:T(8,128)(2,1)} %wq_hbm.1, ...), custom_call_target="tpu_custom_call" | custom-call | flops 20000000000 | bytes 16000000 | tf_op jit(solution)/shard_map/layer/pallas_call | solution.py:641
  107.6 1.8 %copy.12 = bf16[128,1792]{1,0:T(8,128)(2,1)} copy(bf16[128,1792]{1,0:T(8,128)(2,1)} %layer.1) | data formatting | bytes 917504

commit v4 on v3

--- a/solution.py
+++ b/solution.py
@@ -22,9 +22,8 @@
 
 HEADS = 16
 CHUNKS = 4
-PER = 8
 HALF = 64
-ROWS = 32
+ROWS = 16
 BLOCK = 512
 LOG2E = 1.4426950408889634
 EPS = 1e-06
@@ -43,8 +42,8 @@
 APAIR, AX, AZ, AZH, AX2 = 0, 1, 2, 6, 8
 ASTRIDE = 10
 OUT = ABASE + ASTRIDE * CHUNKS
-XSUM = OUT + 4
-NSEM = XSUM + 4
+XSUM = OUT + 8
+NSEM = XSUM + 8
 
 
 def turn(values, cosine, sine):
@@ -132,13 +131,16 @@
     shard = (z_low * 4 + y, 16 + (3 - z_low) * 4 + y)
 
     with jax.named_scope("start"):
+        pltpu.make_async_copy(wkv_hbm, wkv, local_sem.at[8]).start()
         for j in range(8):
-            pltpu.make_async_copy(wq_hbm.at[:, pl.ds(j * 384, 384)], wq.at[j], local_sem.at[j]).start()
-        pltpu.make_async_copy(wkv_hbm, wkv, local_sem.at[8]).start()
+            pltpu.make_async_copy(
+                wq_hbm.at[:, pl.ds(j * 384, 384)], wq.at[j], local_sem.at[j]
+            ).start()
         pltpu.make_async_copy(wo_hbm, wg.at[c, y], local_sem.at[9]).start()
 
     barrier = pltpu.get_barrier_semaphore()
-    for peer in (partner, cross, swap_peer, across, beside, up_y, down_y, up_z, down_z):
+    far = near(2, 0)
+    for peer in (partner, cross, swap_peer, across, beside, far, up_y, down_y, up_z, down_z):
         pl.semaphore_signal(barrier, inc=1, device_id=peer, device_id_type=MESH)
     for k in range(4):
 
@@ -172,7 +174,7 @@
             bias[b : b + 1, at * 128 : (at + 1) * 128] = masked[r : r + 1]
 
     with jax.named_scope("barrier"):
-        pl.semaphore_wait(barrier, 13 - mine)
+        pl.semaphore_wait(barrier, 14 - mine)
 
     def key(t, o1, o2, which=None):
         ref = keys.at[unit(t, o1, o2), c]
@@ -192,30 +194,32 @@
         key_copy(D2 + 2 * k + 1, t, o, 0, near(0, -1)).start()
         key_copy(PAIR + k, t, o, 0, partner).start()
 
+    def first_in(t):
+        key_copy(D1 + 2 * t, t, -1, 0, near(1, 0)).wait_recv()
+        spread(4 + t)
+        key_copy(D1 + 2 * t + 1, t, 1, 0, near(-1, 0)).wait_recv()
+        spread(2 + t)
+
+    def first_out(t):
+        key_copy(D1 + 2 * t, t, 0, 0, near(1, 0)).start()
+        key_copy(D1 + 2 * t + 1, t, 0, 0, near(-1, 0)).start()
+        spread(t)
+        key_copy(D1H + t, t, 0, 0, far).start()
+
+    def far_in(t):
+        key_copy(D1H + t, t, 2, 0, far).wait_recv()
+        spread(6 + t)
+
     with jax.named_scope("spread"):
         key_copy(CROSS, 0, 0, 0, cross).start()
+        first_out(0)
         swap = copy(q_lat.at[1 - xh], qx.at[xh], SWAP, swap_peer)
         swap_in = copy(q_lat.at[1 - xh], qx.at[1 - xh], SWAP, swap_peer)
-        key_copy(D1, 0, 0, 0, near(1, 0)).start()
-        key_copy(D1 + 1, 0, 0, 0, near(-1, 0)).start()
         swap.start()
-        spread(0)
-        with jax.named_scope('cross'):
-            key_copy(CROSS, 1, 0, 0, cross).wait_recv()
-        key_copy(D1 + 2, 1, 0, 0, near(1, 0)).start()
-        key_copy(D1 + 3, 1, 0, 0, near(-1, 0)).start()
-        spread(1)
-        for t in range(2):
-            key_copy(D1 + 2 * t, t, -1, 0, near(1, 0)).wait_recv()
-            key_copy(D1H + 2 * t, t, -1, 0, near(1, 0), 0).start()
-            spread(4 + t)
-            key_copy(D1 + 2 * t + 1, t, 1, 0, near(-1, 0)).wait_recv()
-            key_copy(D1H + 2 * t + 1, t, 1, 0, near(-1, 0), 1).start()
-            spread(2 + t)
-        with jax.named_scope('swap'):
-            swap_in.wait_recv()
-        with jax.named_scope('wkv'):
-            pltpu.make_async_copy(wkv_hbm, wkv, local_sem.at[8]).wait()
+        first_in(0)
+    with jax.named_scope("cross"):
+        key_copy(CROSS, 1, 0, 0, cross).wait_recv()
+        first_out(1)
 
     tables = [angles(2 * where + xh) for where in shard]
 
@@ -250,31 +254,37 @@
         key_copy(D2H + 2 * k + 1, t, o, 1, near(0, -1), 1).start()
         key_copy(PAIR + 16 + k, t, o, 1, partner).start()
 
-    with jax.named_scope("project"):
-        project(0)
-    with jax.named_scope("ring1"):
-        for t in range(2):
-            key_copy(D1H + 2 * t, t, 2, 0, near(1, 0), 0).wait_recv()
-            key_copy(D1H + 2 * t + 1, t, 2, 0, near(-1, 0), 1).wait_recv()
-            spread(6 + t)
-
-    w_mine = wg.at[c, y]
-    pltpu.make_async_copy(wo_hbm, w_mine, local_sem.at[9]).wait()
     span = wo_hbm.shape[0] // 2
 
     def w_copy(number, row, device, which):
         ref = wg.at[c, row, pl.ds(which * span, span)]
         return copy(ref, ref, number, device)
 
-    def project_step(k, carry):
-        with jax.named_scope("relay"):
-            relay(k - 1)
+    with jax.named_scope("relay0"):
+        relay(0)
+    with jax.named_scope("far0"):
+        far_in(0)
+    with jax.named_scope("swap"):
+        swap_in.wait_recv()
+    with jax.named_scope("wkv"):
+        pltpu.make_async_copy(wkv_hbm, wkv, local_sem.at[8]).wait()
+    with jax.named_scope("project"):
+        project(0)
+    with jax.named_scope("first1"):
+        first_in(1)
+    with jax.named_scope("relay42"):
+        relay(4)
+        relay(2)
+    with jax.named_scope("project"):
+        project(1)
+    with jax.named_scope("far1"):
+        far_in(1)
+    for at, k in enumerate((1, 5, 3, 6, 7)):
+        with jax.named_scope("relays"):
+            relay(k)
         with jax.named_scope("project"):
-            project(k)
-        return carry
-
-    lax.fori_loop(1, 8, project_step, 0)
-    relay(7)
+            project(2 + at)
+    pltpu.make_async_copy(wo_hbm, wg.at[c, y], local_sem.at[9]).wait()
     for which in range(2):
         w_copy(WFULL + which, y, up_y, which).start()
         w_copy(WFULL + 3 - which, y, down_y, 1 - which).start()
@@ -286,6 +296,8 @@
         return copy(wg.at[1 - c, row], wg.at[1 - c, row], WPAIR + number, partner)
 
     w_pair(y, 0).start()
+    with jax.named_scope("project"):
+        project(7)
 
     def last_in(upper):
         t = xh + upper - 2 * xh * upper
@@ -353,12 +365,7 @@
             )
 
         def open_step(b, carry):
-            for at, hook in hooks:
-
-                @pl.when(b == at)
-                def _(hook=hook):
-                    hook()
-
+            hooks(b, blocks)
             step(b, None)
             return carry
 
@@ -377,9 +384,10 @@
             attended = jnp.dot(ctx[h], w_value, preferred_element_type=jnp.float32).astype(
                 jnp.bfloat16
             )
-            g, at = 2 * half + h // PER, (h % PER) * VD
-            astage[g, 0, :, at : at + VD] = attended[:ROWS]
-            astage[g, 1, :, at : at + VD] = attended[ROWS:]
+            for r in range(2):
+                for to in range(2):
+                    at = to * 2 * ROWS + r * ROWS
+                    astage[2 * half + r, to, :, h * VD : (h + 1) * VD] = attended[at : at + ROWS]
         for g in (2 * half, 2 * half + 1):
             pair_copy(g).start()
             ag[here, g, c] = astage[g, c]
@@ -448,66 +456,61 @@
         for k, o in enumerate((0, 3, 1, 2)):
             w_pair_in(lax.rem(y + o, 4), k).wait_recv()
 
-    depth = PER * VD
-
-    def product(g):
-        total = jnp.zeros((8 * ROWS, 4 * 224), jnp.float32)
+    def product(first, count):
+        rows = 8 * count * ROWS
+        total = jnp.zeros((rows, 4 * 224), jnp.float32)
         for core in range(2):
             total = total + lax.dot_general(
-                ag[:, g, core].reshape(8 * ROWS, depth),
-                wg[core, :, :, (g % 2) * depth : (g % 2 + 1) * depth].reshape(4 * 224, depth),
+                ag[:, first : first + count, core].reshape(rows, HEADS * VD),
+                wg[core].reshape(4 * 224, HEADS * VD),
                 (((1,), (1,)), ((), ())),
                 preferred_element_type=jnp.float32,
             )
-        return total.reshape(8, ROWS, 4 * 224)
+        total = total.reshape(8, count * ROWS, 4 * 224)
+        for n in range(count):
+            part[first + n] = total[:, n * ROWS : (n + 1) * ROWS]
 
     def slots(half, k):
         straight, mirrored = k, 3 - k
         first = straight if half == 0 else mirrored
         return first, 4 + 3 - first
 
-    def half_out(half):
+    def half_out(g):
         for k in range(2):
-            low, high = slots(half, 2 * (1 - xl) + k)
-            outgoing[half, 0, k, 0] = part[low].astype(jnp.bfloat16)
-            outgoing[half, 0, k, 1] = part[high].astype(jnp.bfloat16)
-            copy(
-                outgoing.at[half, 0, k], summand.at[half, k], XSUM + 2 * half + k, beside
-            ).start()
-
-    def whole_out(half):
-        place_in = lax.rem(z, 2) + 2 * c
+            low, high = slots(g // 2, 2 * (1 - xl) + k)
+            outgoing[g, 0, k, 0] = part[g, low].astype(jnp.bfloat16)
+            outgoing[g, 0, k, 1] = part[g, high].astype(jnp.bfloat16)
+            copy(outgoing.at[g, 0, k], summand.at[g, k], XSUM + 2 * g + k, beside).start()
+
+    def whole_out(g):
+        half = g // 2
+        place_in = lax.rem(z, 2) + 2 * c + 4 * (g % 2)
         for k in range(2):
             row = 2 * xl + k
-            copy(
-                outgoing.at[half, 0, k], summand.at[half, k], XSUM + 2 * half + k, beside
-            ).wait_recv()
+            copy(outgoing.at[g, 0, k], summand.at[g, k], XSUM + 2 * g + k, beside).wait_recv()
             low, high = slots(half, row)
             for xs, at in enumerate((low, high)):
-                outgoing[half, 1, k, xs] = (
-                    part[at] + summand[half, k, xs].astype(jnp.float32)
+                outgoing[g, 1, k, xs] = (
+                    part[g, at] + summand[g, k, xs].astype(jnp.float32)
                 ).astype(jnp.bfloat16)
             own = (mine == 1) & (xh == half) & (z == row)
 
             @pl.when(jnp.logical_not(own))
             def _():
                 copy(
-                    outgoing.at[half, 1, k],
+                    outgoing.at[g, 1, k],
                     landed.at[place_in],
                     OUT + place_in,
                     owners[half][k],
-                    OUT + 2 * half + k,
+                    OUT + 2 * g + k,
                 ).start()
 
             @pl.when(own)
             def _():
-                landed[place_in] = outgoing[half, 1, k]
-
-    def sum_early():
-        part[...] = product(0) + product(1)
+                landed[place_in] = outgoing[g, 1, k]
 
     with jax.named_scope("attend_low"):
-        attend(0, ())
+        attend(0, lambda b, blocks: None)
     with jax.named_scope("values"):
         values(0)
     with jax.named_scope("last_in"):
@@ -515,79 +518,87 @@
     with jax.named_scope("pair_in"):
         pair_in(1)
 
-    def hook_a():
-        with jax.named_scope("hook1"):
-            stage1(0)
-            stage1(1)
-
-    def hook_b():
-        with jax.named_scope("hook2"):
-            stage2(0)
-            w_relay(0)
-            w_relay(1)
-
-    def hook_c():
-        with jax.named_scope("hook3"):
-            stage2(1)
-            stage3(0)
+    def late_hooks(b, blocks):
+        @pl.when(b == 0)
+        def _():
+            with jax.named_scope("hook1"):
+                stage1(0)
+                stage1(1)
+
+        @pl.when(b == blocks - 1)
+        def _():
+            with jax.named_scope("hook2"):
+                stage2(0)
+                stage3(0)
+                w_relay(0)
+                w_relay(1)
 
     with jax.named_scope("attend_high"):
-        attend(1, ((0, hook_a), (2, hook_b), (3, hook_c)))
+        attend(1, late_hooks)
     with jax.named_scope("values"):
         values(1)
-    with jax.named_scope("stage3_1"):
+    with jax.named_scope("stage23_1"):
+        stage2(1)
         stage3(1)
-    with jax.named_scope("stage1_2"):
+    with jax.named_scope("stage1_23"):
         stage1(2)
         stage1(3)
-    with jax.named_scope("stage4_0"):
+    with jax.named_scope("stage4_01"):
         stage4(0)
         stage4(1)
+    with jax.named_scope("w_middle"):
+        w_middle()
+    with jax.named_scope("stage5_01"):
+        stage5(0)
+        stage5(1)
     with jax.named_scope("stage2_2"):
         stage2(2)
-    with jax.named_scope("w_middle"):
-        w_middle()
-    with jax.named_scope("stage5_0"):
-        stage5(0)
-        stage5(1)
-    with jax.named_scope("stage3_2"):
-        stage2(3)
-        stage3(2)
-        stage3(3)
     with jax.named_scope("w_last"):
         w_last()
     with jax.named_scope("product_low"):
-        sum_early()
+        product(0, 2)
     with jax.named_scope("half_out_low"):
         half_out(0)
-    with jax.named_scope("stage4_2"):
+        half_out(1)
+    with jax.named_scope("stage3_2"):
+        stage3(2)
+    with jax.named_scope("stage23_3"):
+        stage2(3)
+        stage3(3)
+    with jax.named_scope("whole_out_low"):
+        whole_out(0)
+        whole_out(1)
+    with jax.named_scope("stage4_23"):
         stage4(2)
         stage4(3)
-    with jax.named_scope("whole_out_low"):
-        whole_out(0)
     with jax.named_scope("stage5_2"):
         stage5(2)
-    with jax.named_scope("product_high"):
-        part[...] = product(2)
+    with jax.named_scope("product_2"):
+        product(2, 1)
+    with jax.named_scope("half_out_2"):
+        half_out(2)
     with jax.named_scope("stage5_3"):
         stage5(3)
-    with jax.named_scope("product_high"):
-        part[...] = part[...] + product(3)
-    with jax.named_scope("half_out_high"):
-        half_out(1)
-    with jax.named_scope("whole_out_high"):
-        whole_out(1)
+    with jax.named_scope("product_3"):
+        product(3, 1)
+    with jax.named_scope("half_out_3"):
+        half_out(3)
+    with jax.named_scope("whole_out_2"):
+        whole_out(2)
+    with jax.named_scope("whole_out_3"):
+        whole_out(3)
 
     with jax.named_scope("finish"):
-        for k in range(4):
+        for n in range(8):
+            r, k = n // 4, n % 4
 
             @pl.when((mine == 0) | (makers[k][1] != z) | (k // 2 != c))
-            def _(k=k):
-                copy(landed.at[k], landed.at[k], OUT + k, partner).wait_recv()
+            def _(n=n):
+                copy(landed.at[n], landed.at[n], OUT + n, partner).wait_recv()
 
             for xs in range(2):
-                at = xs * HALF + (k // 2) * ROWS
-                out_ref[at : at + ROWS, (k % 2) * 896 : (k % 2 + 1) * 896] = landed[k, xs]
+                at = xs * HALF + (k // 2) * 2 * ROWS + r * ROWS
+                out_ref[at : at + ROWS, (k % 2) * 896 : (k % 2 + 1) * 896] = landed[n, xs]
 
     with jax.named_scope("drain"):
         full = keys.at[0, 0]
@@ -606,7 +617,7 @@
         sent(full, CROSS)
         sent(qx.at[0], SWAP)
         drain(full, D1, 4)
-        drain(part_key, D1H, 4)
+        drain(full, D1H, 2)
         drain(full, D2, 16)
         drain(part_key, D2H, 16)
         drain(full, PAIR, 32)
@@ -620,14 +631,14 @@
             drain(ag.at[0, 0], at + AZ, 4)
             drain(ag.at[0, 0, 0], at + AZH, 2)
             sent(ag.at[0, 0], at + AX2)
-        drain(summand.at[0, 0], XSUM, 4)
-        for half in range(2):
+        drain(summand.at[0, 0], XSUM, 8)
+        for g in range(CHUNKS):
             for k in range(2):
-                own = (mine == 1) & (xh == half) & (z == 2 * xl + k)
+                own = (mine == 1) & (xh == g // 2) & (z == 2 * xl + k)
 
                 @pl.when(jnp.logical_not(own))
-                def _(half=half, k=k):
-                    sent(landed.at[0], OUT + 2 * half + k)
+                def _(g=g, k=k):
+                    sent(landed.at[0], OUT + 2 * g + k)
 
 
 def local(q_latent, kv_latent, kv_gain, w_q_b, w_kv_b, w_o, prompt_len, response_mask):
@@ -637,7 +648,7 @@
     vmem = pl.BlockSpec(memory_space=pltpu.VMEM)
     hbm = pl.BlockSpec(memory_space=pl.ANY)
     bf16 = jnp.bfloat16
-    depth = PER * VD
+    depth = HEADS * VD
     result = pl.pallas_call(
         body,
         out_shape=jax.ShapeDtypeStruct((128, 1792), bf16),
@@ -656,10 +667,10 @@
             pltpu.VMEM((CHUNKS, 2, ROWS, depth), bf16),
             pltpu.VMEM((8, CHUNKS, 2, ROWS, depth), bf16),
             pltpu.VMEM((2, 4, 224, 2048), bf16),
-            pltpu.VMEM((8, ROWS, 4 * 224), jnp.float32),
-            pltpu.VMEM((2, 2, 2, 2, ROWS, 4 * 224), bf16),
-            pltpu.VMEM((2, 2, 2, ROWS, 4 * 224), bf16),
-            pltpu.VMEM((4, 2, ROWS, 4 * 224), bf16),
+            pltpu.VMEM((CHUNKS, 8, ROWS, 4 * 224), jnp.float32),
+            pltpu.VMEM((CHUNKS, 2, 2, 2, ROWS, 4 * 224), bf16),
+            pltpu.VMEM((CHUNKS, 2, 2, ROWS, 4 * 224), bf16),
+            pltpu.VMEM((8, 2, ROWS, 4 * 224), bf16),
             pltpu.VMEM((4096 // BLOCK, BLOCK), jnp.float32),
             pltpu.VMEM((HEADS * HALF, 128), jnp.float32),
             pltpu.VMEM((HEADS * HALF, 128), jnp.float32),

time: 110 us -> 107 us (0.973)
  Pallas kernels: 107 us -> 104 us
    pallas_call x1, Pallas kernels: 107 us -> 104 us  [local(): pl.pallas_call(body, out_shape=jax.ShapeDtypeStruct((128, 1792), bf16), i...]
where the time goes in v4:
time: 107 us
  Pallas kernels  104 us (97%)
  local copies, waits for them, and re-layouts  1.82 us (2%)
    pallas_call x1, Pallas kernels, local(): pl.pallas_call(body, out_shape=jax.ShapeDtypeStruct((128, 1792), bf16), i...  104 us

profile of v4, /device:TPU:100, one launch (start us, length us, event | category | flops | bytes accessed | tf_op | source)
XLA Modules:
  0.0 106.8 jit_solution(7488760431382428005)
XLA Ops:
  0.7 104.3 %layer.1 = bf16[128,1792]{1,0:T(8,128)(2,1)} custom-call(bf16[2,64,1536]{2,1,0:T(8,128)(2,1)} %bitcast.6, bf16[576,128]{1,0:T(8,128)(2,1)} %bitcast.7, f32[1,512]{1,0:T(1,128)} %bitcast.9, f32[4,64,64]{2,1,0:T(8,128)} %constant.2.clone.table, s32[32,128]{1,0:T(8,128)} %bitcast.8, s32[1]{0:T(128)S(6)} %copy.11.prompt, bf16[1536,3072]{1,0:T(8,128)(2,1)} %wq_hbm.1, ...), custom_call_target="tpu_custom_call" | custom-call | flops 20000000000 | bytes 16000000 | tf_op jit(solution)/shard_map/layer/pallas_call | solution.py:652
  105.0 1.8 %copy.12 = bf16[128,1792]{1,0:T(8,128)(2,1)} copy(bf16[128,1792]{1,0:T(8,128)(2,1)} %layer.1) | data formatting | bytes 917504

commit v5 on v4

--- a/solution.py
+++ b/solution.py
@@ -77,7 +77,6 @@
     part,
     outgoing,
     summand,
-    landed,
     bias,
     m_ref,
     l_ref,
@@ -187,39 +186,42 @@
         return copy(ref, ref, number, device)
 
     offsets = (0, 1, 3, 2)
-
-    def spread(k):
-        t, o = k % 2, offsets[k // 2]
+    lower, upper = xh, 1 - xh
+
+    def spread(q, t):
+        k, o = 2 * q + t, offsets[q]
         key_copy(D2 + 2 * k, t, o, 0, near(0, 1)).start()
         key_copy(D2 + 2 * k + 1, t, o, 0, near(0, -1)).start()
         key_copy(PAIR + k, t, o, 0, partner).start()
 
-    def first_in(t):
-        key_copy(D1 + 2 * t, t, -1, 0, near(1, 0)).wait_recv()
-        spread(4 + t)
-        key_copy(D1 + 2 * t + 1, t, 1, 0, near(-1, 0)).wait_recv()
-        spread(2 + t)
-
     def first_out(t):
         key_copy(D1 + 2 * t, t, 0, 0, near(1, 0)).start()
         key_copy(D1 + 2 * t + 1, t, 0, 0, near(-1, 0)).start()
-        spread(t)
+        spread(0, t)
         key_copy(D1H + t, t, 0, 0, far).start()
+
+    def first_in(t):
+        key_copy(D1 + 2 * t, t, -1, 0, near(1, 0)).wait_recv()
+        spread(2, t)
+        key_copy(D1 + 2 * t + 1, t, 1, 0, near(-1, 0)).wait_recv()
+        spread(1, t)
 
     def far_in(t):
         key_copy(D1H + t, t, 2, 0, far).wait_recv()
-        spread(6 + t)
+        spread(3, t)
+
+    def cross_in():
+        key_copy(CROSS, 1, 0, 0, cross).wait_recv()
 
     with jax.named_scope("spread"):
         key_copy(CROSS, 0, 0, 0, cross).start()
-        first_out(0)
+        pl.when(xh == 1)(cross_in)
+        first_out(lower)
         swap = copy(q_lat.at[1 - xh], qx.at[xh], SWAP, swap_peer)
         swap_in = copy(q_lat.at[1 - xh], qx.at[1 - xh], SWAP, swap_peer)
         swap.start()
-        first_in(0)
-    with jax.named_scope("cross"):
-        key_copy(CROSS, 1, 0, 0, cross).wait_recv()
-        first_out(1)
+        pl.when(xh == 0)(cross_in)
+        first_out(upper)
 
     tables = [angles(2 * where + xh) for where in shard]
 
@@ -243,10 +245,8 @@
                 qs[half, h, :, :KVR] = absorbed[mine_rows]
                 qs[half, h, :, KVR:] = turn(roped[mine_rows], *tables[half]).astype(jnp.bfloat16)
 
-    def relay(k):
-        t = lax.rem(k, 2)
-        q = k // 2
-        o = q + q // 2 - 2 * (q // 3)
+    def relay(q, t):
+        k, o = 2 * q + t, offsets[q]
         key_copy(D2 + 2 * k, t, o, -1, near(0, 1)).wait_recv()
         key_copy(D2H + 2 * k, t, o, -1, near(0, 1), 0).start()
         key_copy(PAIR + 8 + k, t, o, -1, partner).start()
@@ -254,78 +254,78 @@
         key_copy(D2H + 2 * k + 1, t, o, 1, near(0, -1), 1).start()
         key_copy(PAIR + 16 + k, t, o, 1, partner).start()
 
+    def last_in(q, t):
+        k, o = 2 * q + t, offsets[q]
+        key_copy(D2H + 2 * k, t, o, 2, near(0, 1), 0).wait_recv()
+        key_copy(D2H + 2 * k + 1, t, o, 2, near(0, -1), 1).wait_recv()
+        key_copy(PAIR + 24 + k, t, o, 2, partner).start()
+
+    def pair_in(t):
+        def one(n, carry):
+            ref = keys.at[0, 1 - c]
+            copy(ref, ref, PAIR + 2 * n + t, partner).wait_recv()
+            return carry
+
+        lax.fori_loop(0, 16, one, 0)
+
     span = wo_hbm.shape[0] // 2
 
     def w_copy(number, row, device, which):
         ref = wg.at[c, row, pl.ds(which * span, span)]
         return copy(ref, ref, number, device)
 
-    with jax.named_scope("relay0"):
-        relay(0)
-    with jax.named_scope("far0"):
-        far_in(0)
+    def w_pair(row, number):
+        return copy(wg.at[c, row], wg.at[c, row], WPAIR + number, partner)
+
+    def w_pair_in(row, number):
+        return copy(wg.at[1 - c, row], wg.at[1 - c, row], WPAIR + number, partner)
+
+    with jax.named_scope("first_in_l"):
+        first_in(lower)
+    with jax.named_scope("relay_l0"):
+        relay(0, lower)
+    with jax.named_scope("far_l"):
+        far_in(lower)
     with jax.named_scope("swap"):
         swap_in.wait_recv()
     with jax.named_scope("wkv"):
         pltpu.make_async_copy(wkv_hbm, wkv, local_sem.at[8]).wait()
     with jax.named_scope("project"):
         project(0)
-    with jax.named_scope("first1"):
-        first_in(1)
-    with jax.named_scope("relay42"):
-        relay(4)
-        relay(2)
+    with jax.named_scope("relay_l21"):
+        relay(2, lower)
+        relay(1, lower)
     with jax.named_scope("project"):
         project(1)
-    with jax.named_scope("far1"):
-        far_in(1)
-    for at, k in enumerate((1, 5, 3, 6, 7)):
-        with jax.named_scope("relays"):
-            relay(k)
-        with jax.named_scope("project"):
-            project(2 + at)
-    pltpu.make_async_copy(wo_hbm, wg.at[c, y], local_sem.at[9]).wait()
-    for which in range(2):
-        w_copy(WFULL + which, y, up_y, which).start()
-        w_copy(WFULL + 3 - which, y, down_y, 1 - which).start()
-
-    def w_pair(row, number):
-        return copy(wg.at[c, row], wg.at[c, row], WPAIR + number, partner)
-
-    def w_pair_in(row, number):
-        return copy(wg.at[1 - c, row], wg.at[1 - c, row], WPAIR + number, partner)
-
-    w_pair(y, 0).start()
+    with jax.named_scope("first_in_u"):
+        first_in(upper)
+    with jax.named_scope("project"):
+        project(2)
+    with jax.named_scope("relay_l3"):
+        relay(3, lower)
+    with jax.named_scope("project"):
+        project(3)
+    with jax.named_scope("far_u"):
+        far_in(upper)
+    with jax.named_scope("relay_u0"):
+        relay(0, upper)
+    with jax.named_scope("project"):
+        project(4)
+    with jax.named_scope("last_in_l"):
+        for q in (0, 2, 1):
+            last_in(q, lower)
+    with jax.named_scope("project"):
+        project(5)
+        project(6)
+    with jax.named_scope("last_in_l3"):
+        last_in(3, lower)
+    with jax.named_scope("relay_u21"):
+        relay(2, upper)
+        relay(1, upper)
     with jax.named_scope("project"):
         project(7)
-
-    def last_in(upper):
-        t = xh + upper - 2 * xh * upper
-
-        def one(q, carry):
-            k = 2 * q + t
-            o = q + q // 2 - 2 * (q // 3)
-            key_copy(D2H + 2 * k, t, o, 2, near(0, 1), 0).wait_recv()
-            key_copy(D2H + 2 * k + 1, t, o, 2, near(0, -1), 1).wait_recv()
-            key_copy(PAIR + 24 + k, t, o, 2, partner).start()
-            return carry
-
-        lax.fori_loop(0, 4, one, 0)
-
-    def pair_in(upper):
-        t = xh + upper - 2 * xh * upper
-
-        def one(n, carry):
-            ref = keys.at[0, 1 - c]
-            copy(ref, ref, PAIR + 2 * n + t, partner).wait_recv()
-            return carry
-
-        lax.fori_loop(0, 16, one, 0)
-
-    with jax.named_scope("last_in"):
-        last_in(0)
-    with jax.named_scope("pair_in"):
-        pair_in(0)
+    with jax.named_scope("pair_in_l"):
+        pair_in(lower)
 
     scale = LOG2E / math.sqrt(NOPE + ROPE)
     tile_rows = HEADS * HALF
@@ -370,6 +370,7 @@
             return carry
 
         lax.fori_loop(0, blocks, open_step, 0)
+        hooks(blocks, blocks)
         token = where * 128 + xh * HALF + lax.broadcasted_iota(jnp.int32, (HALF, BLOCK), 0)
         position = blocks * BLOCK + lax.broadcasted_iota(jnp.int32, (HALF, BLOCK), 1)
         step(blocks, jnp.where(position <= token, 0.0, -1e30))
@@ -453,6 +454,8 @@
         w_copy(WHALF, lax.rem(y + 2, 4), up_y, 0).wait_recv()
         w_copy(WHALF + 1, lax.rem(y + 2, 4), down_y, 1).wait_recv()
         w_pair(lax.rem(y + 2, 4), 3).start()
+
+    def w_all():
         for k, o in enumerate((0, 3, 1, 2)):
             w_pair_in(lax.rem(y + o, 4), k).wait_recv()
 
@@ -484,7 +487,7 @@
 
     def whole_out(g):
         half = g // 2
-        place_in = lax.rem(z, 2) + 2 * c + 4 * (g % 2)
+        number = lax.rem(z, 2) + 2 * c + 4 * (g % 2)
         for k in range(2):
             row = 2 * xl + k
             copy(outgoing.at[g, 0, k], summand.at[g, k], XSUM + 2 * g + k, beside).wait_recv()
@@ -494,45 +497,64 @@
                     part[g, at] + summand[g, k, xs].astype(jnp.float32)
                 ).astype(jnp.bfloat16)
             own = (mine == 1) & (xh == half) & (z == row)
+            target = out_ref.at[:, 2 * c + g % 2, :, pl.ds(lax.rem(z, 2) * 896, 896)]
 
             @pl.when(jnp.logical_not(own))
             def _():
                 copy(
-                    outgoing.at[g, 1, k],
-                    landed.at[place_in],
-                    OUT + place_in,
-                    owners[half][k],
-                    OUT + 2 * g + k,
+                    outgoing.at[g, 1, k], target, OUT + number, owners[half][k], OUT + 2 * g + k
                 ).start()
 
             @pl.when(own)
             def _():
-                landed[place_in] = outgoing[g, 1, k]
-
-    with jax.named_scope("attend_low"):
-        attend(0, lambda b, blocks: None)
-    with jax.named_scope("values"):
-        values(0)
-    with jax.named_scope("last_in"):
-        last_in(1)
-    with jax.named_scope("pair_in"):
-        pair_in(1)
+                pltpu.make_async_copy(
+                    outgoing.at[g, 1, k], target, local_sem.at[10 + g % 2]
+                ).start()
+
+    def start_w():
+        pltpu.make_async_copy(wo_hbm, wg.at[c, y], local_sem.at[9]).wait()
+        for which in range(2):
+            w_copy(WFULL + which, y, up_y, which).start()
+            w_copy(WFULL + 3 - which, y, down_y, 1 - which).start()
+        w_pair(y, 0).start()
+
+    def early_hooks(b, blocks):
+        @pl.when(b == jnp.minimum(1, blocks))
+        def _():
+            with jax.named_scope("relay_u3"):
+                relay(3, upper)
+                start_w()
 
     def late_hooks(b, blocks):
         @pl.when(b == 0)
         def _():
-            with jax.named_scope("hook1"):
+            with jax.named_scope("last_in_u"):
+                for q in (0, 2, 1, 3):
+                    last_in(q, upper)
+
+        @pl.when(b == 1)
+        def _():
+            with jax.named_scope("stage1_01"):
                 stage1(0)
                 stage1(1)
 
-        @pl.when(b == blocks - 1)
+        @pl.when(b == 4)
         def _():
-            with jax.named_scope("hook2"):
+            with jax.named_scope("pair_in_u"):
+                pair_in(upper)
+
+        @pl.when(b == blocks)
+        def _():
+            with jax.named_scope("stage23_0"):
                 stage2(0)
                 stage3(0)
                 w_relay(0)
                 w_relay(1)
 
+    with jax.named_scope("attend_low"):
+        attend(0, early_hooks)
+    with jax.named_scope("values"):
+        values(0)
     with jax.named_scope("attend_high"):
         attend(1, late_hooks)
     with jax.named_scope("values"):
@@ -540,65 +562,66 @@
     with jax.named_scope("stage23_1"):
         stage2(1)
         stage3(1)
+    with jax.named_scope("stage4_0"):
+        stage4(0)
+    with jax.named_scope("stage4_1"):
+        stage4(1)
     with jax.named_scope("stage1_23"):
         stage1(2)
         stage1(3)
-    with jax.named_scope("stage4_01"):
-        stage4(0)
-        stage4(1)
     with jax.named_scope("w_middle"):
         w_middle()
-    with jax.named_scope("stage5_01"):
+    with jax.named_scope("stage5_0"):
         stage5(0)
+    with jax.named_scope("stage5_1"):
         stage5(1)
-    with jax.named_scope("stage2_2"):
+    with jax.named_scope("stage23_2"):
         stage2(2)
+        stage3(2)
     with jax.named_scope("w_last"):
         w_last()
+        w_all()
     with jax.named_scope("product_low"):
         product(0, 2)
     with jax.named_scope("half_out_low"):
         half_out(0)
         half_out(1)
-    with jax.named_scope("stage3_2"):
-        stage3(2)
     with jax.named_scope("stage23_3"):
         stage2(3)
         stage3(3)
+    with jax.named_scope("stage4_2"):
+        stage4(2)
     with jax.named_scope("whole_out_low"):
         whole_out(0)
         whole_out(1)
-    with jax.named_scope("stage4_23"):
-        stage4(2)
+    with jax.named_scope("stage4_3"):
         stage4(3)
     with jax.named_scope("stage5_2"):
         stage5(2)
-    with jax.named_scope("product_2"):
-        product(2, 1)
-    with jax.named_scope("half_out_2"):
-        half_out(2)
     with jax.named_scope("stage5_3"):
         stage5(3)
-    with jax.named_scope("product_3"):
-        product(3, 1)
-    with jax.named_scope("half_out_3"):
+    with jax.named_scope("product_high"):
+        product(2, 2)
+    with jax.named_scope("half_out_high"):
+        half_out(2)
         half_out(3)
-    with jax.named_scope("whole_out_2"):
+    with jax.named_scope("whole_out_high"):
         whole_out(2)
-    with jax.named_scope("whole_out_3"):
         whole_out(3)
 
     with jax.named_scope("finish"):
         for n in range(8):
             r, k = n // 4, n % 4
-
-            @pl.when((mine == 0) | (makers[k][1] != z) | (k // 2 != c))
-            def _(n=n):
-                copy(landed.at[n], landed.at[n], OUT + n, partner).wait_recv()
-
-            for xs in range(2):
-                at = xs * HALF + (k // 2) * 2 * ROWS + r * ROWS
-                out_ref[at : at + ROWS, (k % 2) * 896 : (k % 2 + 1) * 896] = landed[n, xs]
+            piece = out_ref.at[:, 2 * (k // 2) + r, :, (k % 2) * 896 : (k % 2 + 1) * 896]
+            self_made = (mine == 1) & (makers[k][1] == z) & (k // 2 == c)
+
+            @pl.when(jnp.logical_not(self_made))
+            def _(n=n, piece=piece):
+                copy(piece, piece, OUT + n, partner).wait_recv()
+
+            @pl.when(self_made)
+            def _(r=r, piece=piece):
+                pltpu.make_async_copy(outgoing.at[0, 1, 0], piece, local_sem.at[10 + r]).wait()
 
     with jax.named_scope("drain"):
         full = keys.at[0, 0]
@@ -638,7 +661,7 @@
 
                 @pl.when(jnp.logical_not(own))
                 def _(g=g, k=k):
-                    sent(landed.at[0], OUT + 2 * g + k)
+                    sent(summand.at[0, 0], OUT + 2 * g + k)
 
 
 def local(q_latent, kv_latent, kv_gain, w_q_b, w_kv_b, w_o, prompt_len, response_mask):
@@ -651,13 +674,13 @@
     depth = HEADS * VD
     result = pl.pallas_call(
         body,
-        out_shape=jax.ShapeDtypeStruct((128, 1792), bf16),
+        out_shape=jax.ShapeDtypeStruct((2, 4, ROWS, 1792), bf16),
         in_specs=[vmem] * 5 + [pl.BlockSpec(memory_space=pltpu.SMEM)] + [hbm] * 3,
-        out_specs=vmem,
+        out_specs=hbm,
         scratch_shapes=[
             pltpu.SemaphoreType.DMA((NSEM,)),
             pltpu.SemaphoreType.DMA((NSEM,)),
-            pltpu.SemaphoreType.DMA((10,)),
+            pltpu.SemaphoreType.DMA((12,)),
             pltpu.VMEM((2, HALF, 1536), bf16),
             pltpu.VMEM((8, 1536, 384), bf16),
             pltpu.VMEM((512, 4096), bf16),
@@ -670,7 +693,6 @@
             pltpu.VMEM((CHUNKS, 8, ROWS, 4 * 224), jnp.float32),
             pltpu.VMEM((CHUNKS, 2, 2, 2, ROWS, 4 * 224), bf16),
             pltpu.VMEM((CHUNKS, 2, 2, ROWS, 4 * 224), bf16),
-            pltpu.VMEM((8, 2, ROWS, 4 * 224), bf16),
             pltpu.VMEM((4096 // BLOCK, BLOCK), jnp.float32),
             pltpu.VMEM((HEADS * HALF, 128), jnp.float32),
             pltpu.VMEM((HEADS * HALF, 128), jnp.float32),
@@ -694,7 +716,7 @@
         w_kv_b,
         w_o.T,
     )
-    return result
+    return result.reshape(128, 1792)
 
 
 def solution(mesh):

time: 107 us -> 107 us (level)
  no operation moved by 1% of the time
where the time goes in v5:
time: 107 us; the launch traced here: 106 us
  Pallas kernels  104 us (97%)
  local copies, waits for them, and re-layouts  1.82 us (2%)
    pallas_call x1, Pallas kernels, local(): pl.pallas_call(body, out_shape=jax.ShapeDtypeStruct((2, 4, ROWS, 1792), b...  104 us

profile of v5, /device:TPU:100, one launch (start us, length us, event | category | flops | bytes accessed | tf_op | source)
XLA Modules:
  0.0 106.1 jit_solution(12487888763454815830)
XLA Ops:
  0.7 103.6 %layer.1 = bf16[2,4,16,1792]{3,2,1,0:T(8,128)(2,1)} custom-call(bf16[2,64,1536]{2,1,0:T(8,128)(2,1)} %bitcast.8, bf16[576,128]{1,0:T(8,128)(2,1)} %bitcast.9, f32[1,512]{1,0:T(1,128)} %bitcast.11, f32[4,64,64]{2,1,0:T(8,128)} %constant.2.clone.table, s32[32,128]{1,0:T(8,128)} %bitcast.10, s32[1]{0:T(128)S(6)} %copy.11.prompt, bf16[1536,3072]{1,0:T(8,128)(2,1)} %wq_hbm.1, ...), custom_call_target="tpu_custom_call" | custom-call | flops 20000000000 | bytes 16000000 | tf_op jit(solution)/shard_map/layer/pallas_call | solution.py:675
  104.3 1.8 %copy.12 = bf16[128,1792]{1,0:T(8,128)(2,1)} copy(bf16[128,1792]{1,0:T(8,128)(2,1)} %bitcast.6) | data formatting | bytes 917504

commit v6 on v5

--- a/solution.py
+++ b/solution.py
@@ -32,6 +32,7 @@
 SWAP = 1
 D1 = 2
 D1H = 6
+SWAP2 = 8
 D2 = 10
 D2H = 26
 PAIR = 42
@@ -52,11 +53,11 @@
 
 
 def body(
-    q_lat,
-    kv_lat,
-    gain,
-    table,
-    live,
+    q_hbm,
+    kv_hbm,
+    gain_hbm,
+    table_hbm,
+    live_hbm,
     prompt,
     wq_hbm,
     wkv_hbm,
@@ -65,6 +66,10 @@
     out_sem,
     in_sem,
     local_sem,
+    kv_lat,
+    gain,
+    table,
+    live,
     qx,
     wq,
     wkv,
@@ -129,14 +134,6 @@
     z_low = z + xh * (3 - 2 * z)
     shard = (z_low * 4 + y, 16 + (3 - z_low) * 4 + y)
 
-    with jax.named_scope("start"):
-        pltpu.make_async_copy(wkv_hbm, wkv, local_sem.at[8]).start()
-        for j in range(8):
-            pltpu.make_async_copy(
-                wq_hbm.at[:, pl.ds(j * 384, 384)], wq.at[j], local_sem.at[j]
-            ).start()
-        pltpu.make_async_copy(wo_hbm, wg.at[c, y], local_sem.at[9]).start()
-
     barrier = pltpu.get_barrier_semaphore()
     far = near(2, 0)
     for peer in (partner, cross, swap_peer, across, beside, far, up_y, down_y, up_z, down_z):
@@ -147,7 +144,19 @@
         def _(k=k):
             pl.semaphore_signal(barrier, inc=1, device_id=makers[k], device_id_type=MESH)
 
+    inputs = ((kv_hbm, kv_lat), (gain_hbm, gain), (table_hbm, table), (live_hbm, live))
+    for n, (far_away, close) in enumerate(inputs):
+        pltpu.make_async_copy(far_away, close, local_sem.at[12 + n]).start()
+    own_rows = pltpu.make_async_copy(q_hbm.at[xh], qx.at[xh], local_sem.at[16])
+    own_rows.start()
+    pltpu.make_async_copy(wkv_hbm, wkv, local_sem.at[8]).start()
+    for j in range(8):
+        pltpu.make_async_copy(wq_hbm.at[:, pl.ds(j * 384, 384)], wq.at[j], local_sem.at[j]).start()
+    pltpu.make_async_copy(wo_hbm, wg.at[c, y], local_sem.at[9]).start()
+
     with jax.named_scope("norm"):
+        for n, (far_away, close) in enumerate(inputs):
+            pltpu.make_async_copy(far_away, close, local_sem.at[12 + n]).wait()
         lane = lax.broadcasted_iota(jnp.int32, (1, ROPE), 1)
         sign = jnp.where(lane < ROPE // 2, -1.0, 1.0)
 
@@ -162,7 +171,6 @@
         inverse = lax.rsqrt(jnp.mean(latent * latent, axis=-1, keepdims=True) + EPS)
         keys[me, c, :, :KVR] = (latent * inverse * gain[...]).astype(jnp.bfloat16)
         keys[me, c, :, KVR:] = turn(rows[:, KVR:], *angles(me * 2 + c)).astype(jnp.bfloat16)
-        qx[xh] = q_lat[xh]
         spot = lax.broadcasted_iota(jnp.int32, (32, 128), 0) * 128 + lax.broadcasted_iota(
             jnp.int32, (32, 128), 1
         )
@@ -215,11 +223,9 @@
 
     with jax.named_scope("spread"):
         key_copy(CROSS, 0, 0, 0, cross).start()
+        copy(q_hbm.at[1 - xh, c], qx.at[xh, c], SWAP, swap_peer).start()
         pl.when(xh == 1)(cross_in)
         first_out(lower)
-        swap = copy(q_lat.at[1 - xh], qx.at[xh], SWAP, swap_peer)
-        swap_in = copy(q_lat.at[1 - xh], qx.at[1 - xh], SWAP, swap_peer)
-        swap.start()
         pl.when(xh == 0)(cross_in)
         first_out(upper)
 
@@ -230,7 +236,7 @@
             wq_hbm.at[:, pl.ds(0, 384)], wq.at[j], local_sem.at[j]
         ).wait()
         both = jnp.dot(
-            qx[...].reshape(2 * HALF, -1), wq[j], preferred_element_type=jnp.float32
+            qx[...].reshape(2 * HALF, 1536), wq[j], preferred_element_type=jnp.float32
         ).astype(jnp.bfloat16)
         for e in range(2):
             h = 2 * j + e
@@ -280,6 +286,18 @@
     def w_pair_in(row, number):
         return copy(wg.at[1 - c, row], wg.at[1 - c, row], WPAIR + number, partner)
 
+    def project_in(*order):
+        with jax.named_scope("project"):
+            for j in order:
+                project(j)
+
+    def start_w():
+        pltpu.make_async_copy(wo_hbm, wg.at[c, y], local_sem.at[9]).wait()
+        for which in range(2):
+            w_copy(WFULL + which, y, up_y, which).start()
+            w_copy(WFULL + 3 - which, y, down_y, 1 - which).start()
+        w_pair(y, 0).start()
+
     with jax.named_scope("first_in_l"):
         first_in(lower)
     with jax.named_scope("relay_l0"):
@@ -287,43 +305,40 @@
     with jax.named_scope("far_l"):
         far_in(lower)
     with jax.named_scope("swap"):
-        swap_in.wait_recv()
-    with jax.named_scope("wkv"):
-        pltpu.make_async_copy(wkv_hbm, wkv, local_sem.at[8]).wait()
-    with jax.named_scope("project"):
-        project(0)
+        copy(qx.at[1 - xh, c], qx.at[1 - xh, c], SWAP, swap_peer).wait_recv()
+        copy(qx.at[1 - xh, c], qx.at[1 - xh, c], SWAP2, partner).start()
     with jax.named_scope("relay_l21"):
         relay(2, lower)
         relay(1, lower)
-    with jax.named_scope("project"):
-        project(1)
+    with jax.named_scope("swap2"):
+        copy(qx.at[1 - xh, 1 - c], qx.at[1 - xh, 1 - c], SWAP2, partner).wait_recv()
+        own_rows.wait()
+        pltpu.make_async_copy(wkv_hbm, wkv, local_sem.at[8]).wait()
+    project_in(0)
+    with jax.named_scope("relay_l3"):
+        relay(3, lower)
     with jax.named_scope("first_in_u"):
         first_in(upper)
-    with jax.named_scope("project"):
-        project(2)
-    with jax.named_scope("relay_l3"):
-        relay(3, lower)
-    with jax.named_scope("project"):
-        project(3)
+    project_in(1)
     with jax.named_scope("far_u"):
         far_in(upper)
-    with jax.named_scope("relay_u0"):
-        relay(0, upper)
-    with jax.named_scope("project"):
-        project(4)
     with jax.named_scope("last_in_l"):
         for q in (0, 2, 1):
             last_in(q, lower)
-    with jax.named_scope("project"):
-        project(5)
-        project(6)
+    project_in(2)
     with jax.named_scope("last_in_l3"):
         last_in(3, lower)
+    project_in(3)
+    with jax.named_scope("relay_u0"):
+        relay(0, upper)
+    project_in(4)
     with jax.named_scope("relay_u21"):
         relay(2, upper)
         relay(1, upper)
-    with jax.named_scope("project"):
-        project(7)
+    project_in(5)
+    with jax.named_scope("start_w"):
+        start_w()
+    project_in(6, 7)
     with jax.named_scope("pair_in_l"):
         pair_in(lower)
 
@@ -511,19 +526,11 @@
                     outgoing.at[g, 1, k], target, local_sem.at[10 + g % 2]
                 ).start()
 
-    def start_w():
-        pltpu.make_async_copy(wo_hbm, wg.at[c, y], local_sem.at[9]).wait()
-        for which in range(2):
-            w_copy(WFULL + which, y, up_y, which).start()
-            w_copy(WFULL + 3 - which, y, down_y, 1 - which).start()
-        w_pair(y, 0).start()
-
     def early_hooks(b, blocks):
         @pl.when(b == jnp.minimum(1, blocks))
         def _():
             with jax.named_scope("relay_u3"):
                 relay(3, upper)
-                start_w()
 
     def late_hooks(b, blocks):
         @pl.when(b == 0)
@@ -580,22 +587,23 @@
         stage3(2)
     with jax.named_scope("w_last"):
         w_last()
+    with jax.named_scope("stage23_3"):
+        stage2(3)
+        stage3(3)
+    with jax.named_scope("w_all"):
         w_all()
+    with jax.named_scope("stage4_2"):
+        stage4(2)
     with jax.named_scope("product_low"):
         product(0, 2)
     with jax.named_scope("half_out_low"):
         half_out(0)
         half_out(1)
-    with jax.named_scope("stage23_3"):
-        stage2(3)
-        stage3(3)
-    with jax.named_scope("stage4_2"):
-        stage4(2)
+    with jax.named_scope("stage4_3"):
+        stage4(3)
     with jax.named_scope("whole_out_low"):
         whole_out(0)
         whole_out(1)
-    with jax.named_scope("stage4_3"):
-        stage4(3)
     with jax.named_scope("stage5_2"):
         stage5(2)
     with jax.named_scope("stage5_3"):
@@ -638,7 +646,8 @@
             lax.fori_loop(0, count, one, 0)
 
         sent(full, CROSS)
-        sent(qx.at[0], SWAP)
+        sent(qx.at[0, 0], SWAP)
+        sent(qx.at[0, 0], SWAP2)
         drain(full, D1, 4)
         drain(full, D1H, 2)
         drain(full, D2, 16)
@@ -668,20 +677,23 @@
     frequency = 10000.0 ** (-np.arange(ROPE // 2, dtype=np.float64) * 2.0 / ROPE)
     fine = np.arange(HALF, dtype=np.float64)[:, None] * np.tile(frequency, 2)[None, :]
     table = np.stack([np.cos(fine), np.sin(fine), np.cos(HALF * fine), np.sin(HALF * fine)])
-    vmem = pl.BlockSpec(memory_space=pltpu.VMEM)
-    hbm = pl.BlockSpec(memory_space=pl.ANY)
+    hbm = pl.BlockSpec(memory_space=pltpu.HBM)
     bf16 = jnp.bfloat16
     depth = HEADS * VD
     result = pl.pallas_call(
         body,
         out_shape=jax.ShapeDtypeStruct((2, 4, ROWS, 1792), bf16),
-        in_specs=[vmem] * 5 + [pl.BlockSpec(memory_space=pltpu.SMEM)] + [hbm] * 3,
+        in_specs=[hbm] * 5 + [pl.BlockSpec(memory_space=pltpu.SMEM)] + [hbm] * 3,
         out_specs=hbm,
         scratch_shapes=[
             pltpu.SemaphoreType.DMA((NSEM,)),
             pltpu.SemaphoreType.DMA((NSEM,)),
-            pltpu.SemaphoreType.DMA((12,)),
-            pltpu.VMEM((2, HALF, 1536), bf16),
+            pltpu.SemaphoreType.DMA((17,)),
+            pltpu.VMEM((WIDE, 128), bf16),
+            pltpu.VMEM((1, KVR), jnp.float32),
+            pltpu.VMEM((4, HALF, ROPE), jnp.float32),
+            pltpu.VMEM((32, 128), jnp.int32),
+            pltpu.VMEM((2, 2, HALF // 2, 1536), bf16),
             pltpu.VMEM((8, 1536, 384), bf16),
             pltpu.VMEM((512, 4096), bf16),
             pltpu.VMEM((32, 2, HALF, WIDE), bf16),
@@ -706,7 +718,7 @@
         ),
         name="layer",
     )(
-        q_latent.reshape(2, HALF, -1),
+        q_latent.reshape(2, 2, HALF // 2, 1536),
         kv_latent.T,
         kv_gain.reshape(1, -1),
         jnp.asarray(table, jnp.float32),

time: 107 us -> 112 us (1.047)
  Pallas kernels: 104 us -> 109 us
    pallas_call x1, Pallas kernels: 104 us -> 109 us  [local(): pl.pallas_call(body, out_shape=jax.ShapeDtypeStruct((2, 4, ROWS, 1792), b...]
where the time goes in v6:
time: 112 us
  Pallas kernels  109 us (97%)
  local copies, waits for them, and re-layouts  1.82 us (2%)
    pallas_call x1, Pallas kernels, local(): pl.pallas_call(body, out_shape=jax.ShapeDtypeStruct((2, 4, ROWS, 1792), b...  109 us

profile of v6, /device:TPU:100, one launch (start us, length us, event | category | flops | bytes accessed | tf_op | source)
XLA Modules:
  0.0 111.8 jit_solution(10413378575946880678)
XLA Ops:
  0.7 109.3 %layer.1 = bf16[2,4,16,1792]{3,2,1,0:T(8,128)(2,1)} custom-call(bf16[2,2,32,1536]{3,2,1,0:T(8,128)(2,1)} %bitcast.8, bf16[576,128]{1,0:T(8,128)(2,1)} %bitcast.9, f32[1,512]{1,0:T(1,128)} %bitcast.11, f32[4,64,64]{2,1,0:T(8,128)} %constant.2.clone.table_hbm, s32[32,128]{1,0:T(8,128)} %bitcast.10, s32[1]{0:T(128)S(6)} %copy.11.prompt, ...), custom_call_target="tpu_custom_call" | custom-call | flops 20000000000 | bytes 16000000 | tf_op jit(solution)/shard_map/layer/pallas_call | solution.py:683
  109.9 1.8 %copy.12 = bf16[128,1792]{1,0:T(8,128)(2,1)} copy(bf16[128,1792]{1,0:T(8,128)(2,1)} %bitcast.6) | data formatting | bytes 917504

commit v7 on v6

--- a/solution.py
+++ b/solution.py
@@ -335,10 +335,12 @@
     with jax.named_scope("relay_u21"):
         relay(2, upper)
         relay(1, upper)
-    project_in(5)
+    project_in(5, 6)
+    with jax.named_scope("relay_u3"):
+        relay(3, upper)
     with jax.named_scope("start_w"):
         start_w()
-    project_in(6, 7)
+    project_in(7)
     with jax.named_scope("pair_in_l"):
         pair_in(lower)
 
@@ -529,15 +531,15 @@
     def early_hooks(b, blocks):
         @pl.when(b == jnp.minimum(1, blocks))
         def _():
-            with jax.named_scope("relay_u3"):
-                relay(3, upper)
+            with jax.named_scope("last_in_u"):
+                for q in (0, 2, 1):
+                    last_in(q, upper)
 
     def late_hooks(b, blocks):
         @pl.when(b == 0)
         def _():
-            with jax.named_scope("last_in_u"):
-                for q in (0, 2, 1, 3):
-                    last_in(q, upper)
+            with jax.named_scope("last_in_u3"):
+                last_in(3, upper)
 
         @pl.when(b == 1)
         def _():

time: 112 us -> 97.5 us (0.87)
  Pallas kernels: 109 us -> 94.3 us
    pallas_call x1, Pallas kernels: 109 us -> 94.3 us  [local(): pl.pallas_call(body, out_shape=jax.ShapeDtypeStruct((2, 4, ROWS, 1792), b...]
where the time goes in v7:
time: 97.5 us; the launch traced here: 96.8 us
  Pallas kernels  94.3 us (97%)
  local copies, waits for them, and re-layouts  1.82 us (2%)
    pallas_call x1, Pallas kernels, local(): pl.pallas_call(body, out_shape=jax.ShapeDtypeStruct((2, 4, ROWS, 1792), b...  94.3 us

profile of v7, /device:TPU:100, one launch (start us, length us, event | category | flops | bytes accessed | tf_op | source)
XLA Modules:
  0.0 96.8 jit_solution(5195090115854767271)
XLA Ops:
  0.7 94.3 %layer.1 = bf16[2,4,16,1792]{3,2,1,0:T(8,128)(2,1)} custom-call(bf16[2,2,32,1536]{3,2,1,0:T(8,128)(2,1)} %bitcast.8, bf16[576,128]{1,0:T(8,128)(2,1)} %bitcast.9, f32[1,512]{1,0:T(1,128)} %bitcast.11, f32[4,64,64]{2,1,0:T(8,128)} %constant.2.clone.table_hbm, s32[32,128]{1,0:T(8,128)} %bitcast.10, s32[1]{0:T(128)S(6)} %copy.11.prompt, ...), custom_call_target="tpu_custom_call" | custom-call | flops 20000000000 | bytes 16000000 | tf_op jit(solution)/shard_map/layer/pallas_call | solution.py:685
  95.0 1.8 %copy.12 = bf16[128,1792]{1,0:T(8,128)(2,1)} copy(bf16[128,1792]{1,0:T(8,128)(2,1)} %bitcast.6) | data formatting | bytes 917504

commit v8 on v6

--- a/solution.py
+++ b/solution.py
@@ -30,18 +30,18 @@
 
 CROSS = 0
 SWAP = 1
-D1 = 2
-D1H = 6
-SWAP2 = 8
-D2 = 10
-D2H = 26
-PAIR = 42
-WFULL = 74
-WHALF = 78
-WPAIR = 80
-ABASE = 84
-APAIR, AX, AZ, AZH, AX2 = 0, 1, 2, 6, 8
-ASTRIDE = 10
+SWAP2 = 2
+D1 = 3
+FAR = 7
+D2 = 9
+D2H = 25
+PAIR = 33
+WFULL = 35
+WHALF = 39
+WPAIR = 40
+ABASE = 44
+APAIR, AX, AZ, AZH, AX2 = 0, 1, 2, 6, 7
+ASTRIDE = 8
 OUT = ABASE + ASTRIDE * CHUNKS
 XSUM = OUT + 8
 NSEM = XSUM + 8
@@ -200,13 +200,13 @@
         k, o = 2 * q + t, offsets[q]
         key_copy(D2 + 2 * k, t, o, 0, near(0, 1)).start()
         key_copy(D2 + 2 * k + 1, t, o, 0, near(0, -1)).start()
-        key_copy(PAIR + k, t, o, 0, partner).start()
+        key_copy(PAIR + t, t, o, 0, partner).start()
 
     def first_out(t):
         key_copy(D1 + 2 * t, t, 0, 0, near(1, 0)).start()
         key_copy(D1 + 2 * t + 1, t, 0, 0, near(-1, 0)).start()
         spread(0, t)
-        key_copy(D1H + t, t, 0, 0, far).start()
+        key_copy(FAR + t, t, 0, 0, far).start()
 
     def first_in(t):
         key_copy(D1 + 2 * t, t, -1, 0, near(1, 0)).wait_recv()
@@ -215,7 +215,7 @@
         spread(1, t)
 
     def far_in(t):
-        key_copy(D1H + t, t, 2, 0, far).wait_recv()
+        key_copy(FAR + t, t, 2, 0, far).wait_recv()
         spread(3, t)
 
     def cross_in():
@@ -254,25 +254,20 @@
     def relay(q, t):
         k, o = 2 * q + t, offsets[q]
         key_copy(D2 + 2 * k, t, o, -1, near(0, 1)).wait_recv()
-        key_copy(D2H + 2 * k, t, o, -1, near(0, 1), 0).start()
-        key_copy(PAIR + 8 + k, t, o, -1, partner).start()
+        key_copy(D2H + k, t, o, -1, near(0, 1), 0).start()
+        key_copy(PAIR + t, t, o, -1, partner).start()
         key_copy(D2 + 2 * k + 1, t, o, 1, near(0, -1)).wait_recv()
-        key_copy(D2H + 2 * k + 1, t, o, 1, near(0, -1), 1).start()
-        key_copy(PAIR + 16 + k, t, o, 1, partner).start()
+        key_copy(D2H + k, t, o, 1, near(0, -1), 1).start()
+        key_copy(PAIR + t, t, o, 1, partner).start()
 
     def last_in(q, t):
         k, o = 2 * q + t, offsets[q]
-        key_copy(D2H + 2 * k, t, o, 2, near(0, 1), 0).wait_recv()
-        key_copy(D2H + 2 * k + 1, t, o, 2, near(0, -1), 1).wait_recv()
-        key_copy(PAIR + 24 + k, t, o, 2, partner).start()
+        key_copy(D2H + k, t, o, 2, near(0, 1)).wait_recv()
+        key_copy(PAIR + t, t, o, 2, partner).start()
 
     def pair_in(t):
-        def one(n, carry):
-            ref = keys.at[0, 1 - c]
-            copy(ref, ref, PAIR + 2 * n + t, partner).wait_recv()
-            return carry
-
-        lax.fori_loop(0, 16, one, 0)
+        ref = keys.at[pl.ds(0, 16), 1 - c]
+        copy(ref, ref, PAIR + t, partner).wait_recv()
 
     span = wo_hbm.shape[0] // 2
 
@@ -298,6 +293,12 @@
             w_copy(WFULL + 3 - which, y, down_y, 1 - which).start()
         w_pair(y, 0).start()
 
+    def swap_on():
+        copy(qx.at[1 - xh, c], qx.at[1 - xh, c], SWAP, swap_peer).wait_recv()
+        copy(qx.at[1 - xh, c], qx.at[1 - xh, c], SWAP2, partner).start()
+
+    with jax.named_scope("swap"):
+        pl.when(xh == 1)(swap_on)
     with jax.named_scope("first_in_l"):
         first_in(lower)
     with jax.named_scope("relay_l0"):
@@ -305,40 +306,32 @@
     with jax.named_scope("far_l"):
         far_in(lower)
     with jax.named_scope("swap"):
-        copy(qx.at[1 - xh, c], qx.at[1 - xh, c], SWAP, swap_peer).wait_recv()
-        copy(qx.at[1 - xh, c], qx.at[1 - xh, c], SWAP2, partner).start()
+        pl.when(xh == 0)(swap_on)
+    with jax.named_scope("swap2"):
+        own_rows.wait()
+        pltpu.make_async_copy(wkv_hbm, wkv, local_sem.at[8]).wait()
+        copy(qx.at[1 - xh, 1 - c], qx.at[1 - xh, 1 - c], SWAP2, partner).wait_recv()
+    project_in(0, 1)
     with jax.named_scope("relay_l21"):
         relay(2, lower)
         relay(1, lower)
-    with jax.named_scope("swap2"):
-        copy(qx.at[1 - xh, 1 - c], qx.at[1 - xh, 1 - c], SWAP2, partner).wait_recv()
-        own_rows.wait()
-        pltpu.make_async_copy(wkv_hbm, wkv, local_sem.at[8]).wait()
-    project_in(0)
+    project_in(2)
     with jax.named_scope("relay_l3"):
         relay(3, lower)
     with jax.named_scope("first_in_u"):
         first_in(upper)
-    project_in(1)
+    project_in(3)
     with jax.named_scope("far_u"):
         far_in(upper)
     with jax.named_scope("last_in_l"):
         for q in (0, 2, 1):
             last_in(q, lower)
-    project_in(2)
+    project_in(4)
     with jax.named_scope("last_in_l3"):
         last_in(3, lower)
-    project_in(3)
     with jax.named_scope("relay_u0"):
         relay(0, upper)
-    project_in(4)
-    with jax.named_scope("relay_u21"):
-        relay(2, upper)
-        relay(1, upper)
-    project_in(5)
-    with jax.named_scope("start_w"):
-        start_w()
-    project_in(6, 7)
+    project_in(5, 6, 7)
     with jax.named_scope("pair_in_l"):
         pair_in(lower)
 
@@ -434,7 +427,7 @@
         a_copy(g, AZ, 0, -1, up_z).wait_recv()
         a_copy(g, AZH, 0, -1, up_z, 0).start()
         a_copy(g, AZ + 1, 0, 1, down_z).wait_recv()
-        a_copy(g, AZH + 1, 0, 1, down_z, 1).start()
+        a_copy(g, AZH, 0, 1, down_z, 1).start()
 
     def stage3(g):
         a_copy(g, AX, 1, 0, across).wait_recv()
@@ -442,8 +435,7 @@
         a_copy(g, AZ + 3, 1, 0, down_z).start()
 
     def stage4(g):
-        a_copy(g, AZH, 0, 2, up_z, 0).wait_recv()
-        a_copy(g, AZH + 1, 0, 2, down_z, 1).wait_recv()
+        a_copy(g, AZH, 0, 2, up_z).wait_recv()
         a_copy(g, AX2, 0, 2, across).start()
 
     def stage5(g):
@@ -457,7 +449,7 @@
             w_copy(WHALF, lax.rem(y + 3, 4), up_y, 0).start()
         else:
             w_copy(WFULL + 3, lax.rem(y + 1, 4), down_y, 1).wait_recv()
-            w_copy(WHALF + 1, lax.rem(y + 1, 4), down_y, 1).start()
+            w_copy(WHALF, lax.rem(y + 1, 4), down_y, 1).start()
 
     def w_middle():
         w_copy(WFULL + 1, lax.rem(y + 3, 4), up_y, 1).wait_recv()
@@ -466,8 +458,8 @@
         w_pair(lax.rem(y + 1, 4), 2).start()
 
     def w_last():
-        w_copy(WHALF, lax.rem(y + 2, 4), up_y, 0).wait_recv()
-        w_copy(WHALF + 1, lax.rem(y + 2, 4), down_y, 1).wait_recv()
+        ref = wg.at[c, lax.rem(y + 2, 4)]
+        copy(ref, ref, WHALF, up_y).wait_recv()
         w_pair(lax.rem(y + 2, 4), 3).start()
 
     def w_all():
@@ -527,13 +519,21 @@
                 ).start()
 
     def early_hooks(b, blocks):
-        @pl.when(b == jnp.minimum(1, blocks))
+        @pl.when(b == 0)
         def _():
-            with jax.named_scope("relay_u3"):
-                relay(3, upper)
+            with jax.named_scope("relay_u"):
+                for q in (2, 1, 3):
+                    relay(q, upper)
+                start_w()
+
+        @pl.when((b == blocks) & (blocks > 0))
+        def _():
+            with jax.named_scope("last_in_u"):
+                for q in (0, 2, 1, 3):
+                    last_in(q, upper)
 
     def late_hooks(b, blocks):
-        @pl.when(b == 0)
+        @pl.when((b == 0) & (shard[0] < reach))
         def _():
             with jax.named_scope("last_in_u"):
                 for q in (0, 2, 1, 3):
@@ -566,55 +566,61 @@
         attend(1, late_hooks)
     with jax.named_scope("values"):
         values(1)
+    with jax.named_scope("stage1_23"):
+        stage1(2)
+        stage1(3)
     with jax.named_scope("stage23_1"):
         stage2(1)
         stage3(1)
     with jax.named_scope("stage4_0"):
         stage4(0)
+    with jax.named_scope("w_middle"):
+        w_middle()
+    with jax.named_scope("stage2_2"):
+        stage2(2)
+    with jax.named_scope("stage2_3"):
+        stage2(3)
+    with jax.named_scope("stage3_2"):
+        stage3(2)
+    with jax.named_scope("stage3_3"):
+        stage3(3)
     with jax.named_scope("stage4_1"):
         stage4(1)
-    with jax.named_scope("stage1_23"):
-        stage1(2)
-        stage1(3)
-    with jax.named_scope("w_middle"):
-        w_middle()
+    with jax.named_scope("w_last"):
+        w_last()
+    with jax.named_scope("stage4_2"):
+        stage4(2)
     with jax.named_scope("stage5_0"):
         stage5(0)
+    with jax.named_scope("stage4_3"):
+        stage4(3)
     with jax.named_scope("stage5_1"):
         stage5(1)
-    with jax.named_scope("stage23_2"):
-        stage2(2)
-        stage3(2)
-    with jax.named_scope("w_last"):
-        w_last()
-    with jax.named_scope("stage23_3"):
-        stage2(3)
-        stage3(3)
     with jax.named_scope("w_all"):
         w_all()
-    with jax.named_scope("stage4_2"):
-        stage4(2)
     with jax.named_scope("product_low"):
         product(0, 2)
     with jax.named_scope("half_out_low"):
         half_out(0)
         half_out(1)
-    with jax.named_scope("stage4_3"):
-        stage4(3)
+    with jax.named_scope("stage5_2"):
+        stage5(2)
+    with jax.named_scope("product_2"):
+        product(2, 1)
+    with jax.named_scope("half_out_2"):
+        half_out(2)
+    with jax.named_scope("stage5_3"):
+        stage5(3)
+    with jax.named_scope("product_3"):
+        product(3, 1)
+    with jax.named_scope("half_out_3"):
+        half_out(3)
     with jax.named_scope("whole_out_low"):
         whole_out(0)
         whole_out(1)
-    with jax.named_scope("stage5_2"):
-        stage5(2)
-    with jax.named_scope("stage5_3"):
-        stage5(3)
-    with jax.named_scope("product_high"):
-        product(2, 2)
-    with jax.named_scope("half_out_high"):
-        half_out(2)
-        half_out(3)
-    with jax.named_scope("whole_out_high"):
+    with jax.named_scope("whole_out_2"):
         whole_out(2)
+    with jax.named_scope("whole_out_3"):
         whole_out(3)
 
     with jax.named_scope("finish"):
@@ -633,7 +639,6 @@
 
     with jax.named_scope("drain"):
         full = keys.at[0, 0]
-        part_key = keys.at[0, 0, pl.ds(0, 32)]
 
         def sent(ref, number):
             copy(ref, ref, number, partner).wait_send()
@@ -649,19 +654,19 @@
         sent(qx.at[0, 0], SWAP)
         sent(qx.at[0, 0], SWAP2)
         drain(full, D1, 4)
-        drain(full, D1H, 2)
+        drain(full, FAR, 2)
         drain(full, D2, 16)
-        drain(part_key, D2H, 16)
-        drain(full, PAIR, 32)
+        drain(full, D2H, 8)
+        drain(keys.at[pl.ds(0, 16), 0], PAIR, 2)
         drain(wg.at[0, 0, pl.ds(0, span)], WFULL, 4)
-        drain(wg.at[0, 0, pl.ds(0, span)], WHALF, 2)
+        sent(wg.at[0, 0], WHALF)
         drain(wg.at[0, 0], WPAIR, 4)
         for g in range(CHUNKS):
             at = ABASE + ASTRIDE * g
             sent(astage.at[g, 0], at + APAIR)
             sent(ag.at[0, 0], at + AX)
             drain(ag.at[0, 0], at + AZ, 4)
-            drain(ag.at[0, 0, 0], at + AZH, 2)
+            sent(ag.at[0, 0], at + AZH)
             sent(ag.at[0, 0], at + AX2)
         drain(summand.at[0, 0], XSUM, 8)
         for g in range(CHUNKS):

time: 112 us -> 89.7 us (0.80)
  Pallas kernels: 109 us -> 87.1 us
    pallas_call x1, Pallas kernels: 109 us -> 87.1 us  [local(): pl.pallas_call(body, out_shape=jax.ShapeDtypeStruct((2, 4, ROWS, 1792), b...]
where the time goes in v8:
time: 89.7 us; the launch traced here: 89.5 us
  Pallas kernels  87.1 us (97%)
  local copies, waits for them, and re-layouts  1.82 us (2%)
    pallas_call x1, Pallas kernels, local(): pl.pallas_call(body, out_shape=jax.ShapeDtypeStruct((2, 4, ROWS, 1792), b...  87.1 us
    unnamed x1, local copies, waits for them, and re-layouts  1.82 us

profile of v8, /device:TPU:100, one launch (start us, length us, event | category | flops | bytes accessed | tf_op | source)
XLA Modules:
  0.0 89.5 jit_solution(13937981113507788590)
XLA Ops:
  0.7 87.1 %layer.1 = bf16[2,4,16,1792]{3,2,1,0:T(8,128)(2,1)} custom-call(bf16[2,2,32,1536]{3,2,1,0:T(8,128)(2,1)} %bitcast.8, bf16[576,128]{1,0:T(8,128)(2,1)} %bitcast.9, f32[1,512]{1,0:T(1,128)} %bitcast.11, f32[4,64,64]{2,1,0:T(8,128)} %constant.2.clone.table_hbm, s32[32,128]{1,0:T(8,128)} %bitcast.10, s32[1]{0:T(128)S(6)} %copy.11.prompt, ...), custom_call_target="tpu_custom_call" | custom-call | flops 20000000000 | bytes 16000000 | tf_op jit(solution)/shard_map/layer/pallas_call | solution.py:688
  87.7 1.8 %copy.12 = bf16[128,1792]{1,0:T(8,128)(2,1)} copy(bf16[128,1792]{1,0:T(8,128)(2,1)} %bitcast.6) | data formatting | bytes 917504

commit v9 on v8

--- a/solution.py
+++ b/solution.py
@@ -21,6 +21,7 @@
 MESH = pl.DeviceIdType.MESH
 
 HEADS = 16
+PER = 8
 CHUNKS = 4
 HALF = 64
 ROWS = 16
@@ -45,6 +46,8 @@
 OUT = ABASE + ASTRIDE * CHUNKS
 XSUM = OUT + 8
 NSEM = XSUM + 8
+S_CROSS, S_SWAP, S_KEYS, S_PAIR, S_W, S_WPAIR, S_APAIR, S_XSUM, S_A, S_OUT = 0, 1, 2, 3, 4, 5, 6, 7, 8, 12
+NSENT = S_OUT + 8
 
 
 def turn(values, cosine, sine):
@@ -76,8 +79,10 @@
     keys,
     qs,
     ctx,
-    astage,
-    ag,
+    low_stage,
+    high_stage,
+    low,
+    high,
     wg,
     part,
     outgoing,
@@ -107,11 +112,11 @@
         _, zz, yy = place(0, o1, o2)
         return (xh, zz, yy, xl, c)
 
-    def copy(src, dst, number, device, leaving=None):
+    def copy(src, dst, number, device, leaving=0):
         return pltpu.make_async_remote_copy(
             src_ref=src,
             dst_ref=dst,
-            send_sem=out_sem.at[number if leaving is None else leaving],
+            send_sem=out_sem.at[leaving],
             recv_sem=in_sem.at[number],
             device_id=device,
             device_id_type=MESH,
@@ -189,9 +194,9 @@
             return ref
         return ref.at[pl.ds(32 * which, 32)]
 
-    def key_copy(number, t, o1, o2, device, which=None):
+    def key_copy(number, t, o1, o2, device, which=None, leaving=S_KEYS):
         ref = key(t, o1, o2, which)
-        return copy(ref, ref, number, device)
+        return copy(ref, ref, number, device, leaving)
 
     offsets = (0, 1, 3, 2)
     lower, upper = xh, 1 - xh
@@ -200,7 +205,7 @@
         k, o = 2 * q + t, offsets[q]
         key_copy(D2 + 2 * k, t, o, 0, near(0, 1)).start()
         key_copy(D2 + 2 * k + 1, t, o, 0, near(0, -1)).start()
-        key_copy(PAIR + t, t, o, 0, partner).start()
+        key_copy(PAIR + t, t, o, 0, partner, leaving=S_PAIR).start()
 
     def first_out(t):
         key_copy(D1 + 2 * t, t, 0, 0, near(1, 0)).start()
@@ -222,8 +227,8 @@
         key_copy(CROSS, 1, 0, 0, cross).wait_recv()
 
     with jax.named_scope("spread"):
-        key_copy(CROSS, 0, 0, 0, cross).start()
-        copy(q_hbm.at[1 - xh, c], qx.at[xh, c], SWAP, swap_peer).start()
+        key_copy(CROSS, 0, 0, 0, cross, leaving=S_CROSS).start()
+        copy(q_hbm.at[1 - xh, c], qx.at[xh, c], SWAP, swap_peer, S_SWAP).start()
         pl.when(xh == 1)(cross_in)
         first_out(lower)
         pl.when(xh == 0)(cross_in)
@@ -255,15 +260,15 @@
         k, o = 2 * q + t, offsets[q]
         key_copy(D2 + 2 * k, t, o, -1, near(0, 1)).wait_recv()
         key_copy(D2H + k, t, o, -1, near(0, 1), 0).start()
-        key_copy(PAIR + t, t, o, -1, partner).start()
+        key_copy(PAIR + t, t, o, -1, partner, leaving=S_PAIR).start()
         key_copy(D2 + 2 * k + 1, t, o, 1, near(0, -1)).wait_recv()
         key_copy(D2H + k, t, o, 1, near(0, -1), 1).start()
-        key_copy(PAIR + t, t, o, 1, partner).start()
+        key_copy(PAIR + t, t, o, 1, partner, leaving=S_PAIR).start()
 
     def last_in(q, t):
         k, o = 2 * q + t, offsets[q]
         key_copy(D2H + k, t, o, 2, near(0, 1)).wait_recv()
-        key_copy(PAIR + t, t, o, 2, partner).start()
+        key_copy(PAIR + t, t, o, 2, partner, leaving=S_PAIR).start()
 
     def pair_in(t):
         ref = keys.at[pl.ds(0, 16), 1 - c]
@@ -273,10 +278,10 @@
 
     def w_copy(number, row, device, which):
         ref = wg.at[c, row, pl.ds(which * span, span)]
-        return copy(ref, ref, number, device)
+        return copy(ref, ref, number, device, S_W)
 
     def w_pair(row, number):
-        return copy(wg.at[c, row], wg.at[c, row], WPAIR + number, partner)
+        return copy(wg.at[c, row], wg.at[c, row], WPAIR + number, partner, S_WPAIR)
 
     def w_pair_in(row, number):
         return copy(wg.at[1 - c, row], wg.at[1 - c, row], WPAIR + number, partner)
@@ -295,7 +300,7 @@
 
     def swap_on():
         copy(qx.at[1 - xh, c], qx.at[1 - xh, c], SWAP, swap_peer).wait_recv()
-        copy(qx.at[1 - xh, c], qx.at[1 - xh, c], SWAP2, partner).start()
+        copy(qx.at[1 - xh, c], qx.at[1 - xh, c], SWAP2, partner, S_SWAP).start()
 
     with jax.named_scope("swap"):
         pl.when(xh == 1)(swap_on)
@@ -336,39 +341,40 @@
         pair_in(lower)
 
     scale = LOG2E / math.sqrt(NOPE + ROPE)
-    tile_rows = HEADS * HALF
     reach = BLOCK // 128
 
-    def attend(half, hooks):
+    def attend(half, hooks, first, count):
         where = shard[half]
         blocks = where // reach
-        m_ref[...] = jnp.full_like(m_ref, -1e30)
-        l_ref[...] = jnp.zeros_like(l_ref)
-        acc_ref[...] = jnp.zeros_like(acc_ref)
+        tile_rows = count * HALF
+        upto = pl.ds(0, tile_rows)
+        m_ref[upto] = jnp.full((tile_rows, 128), -1e30, jnp.float32)
+        l_ref[upto] = jnp.zeros((tile_rows, 128), jnp.float32)
+        acc_ref[upto] = jnp.zeros((tile_rows, KVR), jnp.float32)
 
         def step(b, causal):
             block = keys[pl.ds(b * reach, reach)].reshape(BLOCK, WIDE)
             scores = lax.dot_general(
-                qs[half].reshape(tile_rows, WIDE),
+                qs[half, first : first + count].reshape(tile_rows, WIDE),
                 block,
                 (((1,), (1,)), ((), ())),
                 preferred_element_type=jnp.float32,
             )
             scores = scores * scale + bias[pl.ds(b, 1), :]
             if causal is not None:
-                scores = (scores.reshape(HEADS, HALF, BLOCK) + causal[None]).reshape(
+                scores = (scores.reshape(count, HALF, BLOCK) + causal[None]).reshape(
                     tile_rows, BLOCK
                 )
-            before = m_ref[...]
+            before = m_ref[upto]
             m_new = jnp.maximum(before, jnp.max(scores, axis=1, keepdims=True))
             alpha = jnp.exp2(before - m_new)
             lifted = jnp.exp2(scores - jnp.concatenate([m_new] * (BLOCK // 128), axis=1))
-            total = l_ref[...] * alpha
+            total = l_ref[upto] * alpha
             for k in range(BLOCK // 128):
                 total = total + lifted[:, k * 128 : (k + 1) * 128]
-            l_ref[...] = total
-            m_ref[...] = m_new
-            acc_ref[...] = acc_ref[...] * jnp.concatenate([alpha] * (KVR // 128), axis=1) + jnp.dot(
+            l_ref[upto] = total
+            m_ref[upto] = m_new
+            acc_ref[upto] = acc_ref[upto] * jnp.concatenate([alpha] * (KVR // 128), axis=1) + jnp.dot(
                 lifted.astype(jnp.bfloat16), block[:, :KVR], preferred_element_type=jnp.float32
             )
 
@@ -382,40 +388,55 @@
         token = where * 128 + xh * HALF + lax.broadcasted_iota(jnp.int32, (HALF, BLOCK), 0)
         position = blocks * BLOCK + lax.broadcasted_iota(jnp.int32, (HALF, BLOCK), 1)
         step(blocks, jnp.where(position <= token, 0.0, -1e30))
-        total = jnp.sum(l_ref[...], axis=1, keepdims=True)
-        ctx[...] = (acc_ref[...] / total).astype(jnp.bfloat16).reshape(HEADS, HALF, KVR)
+        total = jnp.sum(l_ref[upto], axis=1, keepdims=True)
+        ctx[:count] = (acc_ref[upto] / total).astype(jnp.bfloat16).reshape(count, HALF, KVR)
 
     here = xh * 4 + z
 
-    def values(half):
+    def value_rows(h, at):
+        w_value = wkv[:, h * 256 + NOPE : (h + 1) * 256]
+        return jnp.dot(ctx[at], w_value, preferred_element_type=jnp.float32).astype(jnp.bfloat16)
+
+    def values_low(g):
+        for n in range(PER):
+            attended = value_rows(g * PER + n, n)
+            for to in range(2):
+                low_stage[g, to, :, n * VD : (n + 1) * VD] = attended[
+                    to * 2 * ROWS : (to + 1) * 2 * ROWS
+                ]
+        pair_copy(g).start()
+        low[here, g, c] = low_stage[g, c]
+
+    def values_high():
         for h in range(HEADS):
-            w_value = wkv[:, h * 256 + NOPE : (h + 1) * 256]
-            attended = jnp.dot(ctx[h], w_value, preferred_element_type=jnp.float32).astype(
-                jnp.bfloat16
-            )
+            attended = value_rows(h, h)
             for r in range(2):
                 for to in range(2):
                     at = to * 2 * ROWS + r * ROWS
-                    astage[2 * half + r, to, :, h * VD : (h + 1) * VD] = attended[at : at + ROWS]
-        for g in (2 * half, 2 * half + 1):
-            pair_copy(g).start()
-            ag[here, g, c] = astage[g, c]
+                    high_stage[r, to, :, h * VD : (h + 1) * VD] = attended[at : at + ROWS]
+        for r in range(2):
+            pair_copy(2 + r).start()
+            high[here, r, c] = high_stage[r, c]
+
+    def block_of(slot, g):
+        return low.at[slot, g] if g < 2 else high.at[slot, g - 2]
 
     def a_copy(g, number, t, o, device, which=None):
         slot = (xh + t - 2 * xh * t) * 4 + lax.rem(z + o + 4, 4)
-        ref = ag.at[slot, g]
+        ref = block_of(slot, g)
         if which is not None:
             ref = ref.at[which]
-        return copy(ref, ref, ABASE + ASTRIDE * g + number, device)
+        return copy(ref, ref, ABASE + ASTRIDE * g + number, device, S_A + g)
 
     def pair_copy(g):
+        staged = low_stage.at[g, 1 - c] if g < 2 else high_stage.at[g - 2, 1 - c]
         return copy(
-            astage.at[g, 1 - c], ag.at[here, g, c], ABASE + ASTRIDE * g + APAIR, partner
+            staged, block_of(here, g).at[c], ABASE + ASTRIDE * g + APAIR, partner, S_APAIR
         )
 
     def pair_copy_in(g):
-        ref = ag.at[here, g, 1 - c]
-        return copy(ref, ref, ABASE + ASTRIDE * g + APAIR, partner)
+        ref = block_of(here, g).at[1 - c]
+        return copy(ref, ref, ABASE + ASTRIDE * g + APAIR, partner, S_APAIR)
 
     def stage1(g):
         pair_copy_in(g).wait_recv()
@@ -466,19 +487,33 @@
         for k, o in enumerate((0, 3, 1, 2)):
             w_pair_in(lax.rem(y + o, 4), k).wait_recv()
 
-    def product(first, count):
-        rows = 8 * count * ROWS
+    def multiplied(rows, weights):
+        return lax.dot_general(
+            rows, weights, (((1,), (1,)), ((), ())), preferred_element_type=jnp.float32
+        )
+
+    def product_low():
+        rows, depth = 16 * ROWS, PER * VD
+        total = jnp.zeros((rows, 4 * 224), jnp.float32)
+        for g in range(2):
+            for core in range(2):
+                total = total + multiplied(
+                    low[:, g, core].reshape(rows, depth),
+                    wg[core, :, :, g * depth : (g + 1) * depth].reshape(4 * 224, depth),
+                )
+        total = total.reshape(8, 2 * ROWS, 4 * 224)
+        for n in range(2):
+            part[n] = total[:, n * ROWS : (n + 1) * ROWS]
+
+    def product_high(r):
+        rows = 8 * ROWS
         total = jnp.zeros((rows, 4 * 224), jnp.float32)
         for core in range(2):
-            total = total + lax.dot_general(
-                ag[:, first : first + count, core].reshape(rows, HEADS * VD),
+            total = total + multiplied(
+                high[:, r, core].reshape(rows, HEADS * VD),
                 wg[core].reshape(4 * 224, HEADS * VD),
-                (((1,), (1,)), ((), ())),
-                preferred_element_type=jnp.float32,
             )
-        total = total.reshape(8, count * ROWS, 4 * 224)
-        for n in range(count):
-            part[first + n] = total[:, n * ROWS : (n + 1) * ROWS]
+        part[2 + r] = total.reshape(8, ROWS, 4 * 224)
 
     def slots(half, k):
         straight, mirrored = k, 3 - k
@@ -487,10 +522,11 @@
 
     def half_out(g):
         for k in range(2):
-            low, high = slots(g // 2, 2 * (1 - xl) + k)
-            outgoing[g, 0, k, 0] = part[g, low].astype(jnp.bfloat16)
-            outgoing[g, 0, k, 1] = part[g, high].astype(jnp.bfloat16)
-            copy(outgoing.at[g, 0, k], summand.at[g, k], XSUM + 2 * g + k, beside).start()
+            for xs, at in enumerate(slots(g // 2, 2 * (1 - xl) + k)):
+                outgoing[g, 0, k, xs] = part[g, at].astype(jnp.bfloat16)
+            copy(
+                outgoing.at[g, 0, k], summand.at[g, k], XSUM + 2 * g + k, beside, S_XSUM
+            ).start()
 
     def whole_out(g):
         half = g // 2
@@ -498,8 +534,7 @@
         for k in range(2):
             row = 2 * xl + k
             copy(outgoing.at[g, 0, k], summand.at[g, k], XSUM + 2 * g + k, beside).wait_recv()
-            low, high = slots(half, row)
-            for xs, at in enumerate((low, high)):
+            for xs, at in enumerate(slots(half, row)):
                 outgoing[g, 1, k, xs] = (
                     part[g, at] + summand[g, k, xs].astype(jnp.float32)
                 ).astype(jnp.bfloat16)
@@ -509,7 +544,7 @@
             @pl.when(jnp.logical_not(own))
             def _():
                 copy(
-                    outgoing.at[g, 1, k], target, OUT + number, owners[half][k], OUT + 2 * g + k
+                    outgoing.at[g, 1, k], target, OUT + number, owners[half][k], S_OUT + 2 * g + k
                 ).start()
 
             @pl.when(own)
@@ -518,7 +553,7 @@
                     outgoing.at[g, 1, k], target, local_sem.at[10 + g % 2]
                 ).start()
 
-    def early_hooks(b, blocks):
+    def first_hooks(b, blocks):
         @pl.when(b == 0)
         def _():
             with jax.named_scope("relay_u"):
@@ -526,23 +561,28 @@
                     relay(q, upper)
                 start_w()
 
-        @pl.when((b == blocks) & (blocks > 0))
+    def last_in_u():
+        with jax.named_scope("last_in_u"):
+            for q in (0, 2, 1, 3):
+                last_in(q, upper)
+
+    def second_hooks(b, blocks):
+        @pl.when((b == jnp.minimum(2, blocks)) & (blocks > 0))
         def _():
-            with jax.named_scope("last_in_u"):
-                for q in (0, 2, 1, 3):
-                    last_in(q, upper)
+            with jax.named_scope("stage1_0"):
+                stage1(0)
+            last_in_u()
 
     def late_hooks(b, blocks):
         @pl.when((b == 0) & (shard[0] < reach))
         def _():
-            with jax.named_scope("last_in_u"):
-                for q in (0, 2, 1, 3):
-                    last_in(q, upper)
+            with jax.named_scope("stage1_0"):
+                stage1(0)
+            last_in_u()
 
         @pl.when(b == 1)
         def _():
-            with jax.named_scope("stage1_01"):
-                stage1(0)
+            with jax.named_scope("stage1_1"):
                 stage1(1)
 
         @pl.when(b == 4)
@@ -550,7 +590,7 @@
             with jax.named_scope("pair_in_u"):
                 pair_in(upper)
 
-        @pl.when(b == blocks)
+        @pl.when(b == blocks - 1)
         def _():
             with jax.named_scope("stage23_0"):
                 stage2(0)
@@ -558,22 +598,31 @@
                 w_relay(0)
                 w_relay(1)
 
+        @pl.when(b == blocks)
+        def _():
+            with jax.named_scope("stage23_1"):
+                stage2(1)
+                stage3(1)
+
     with jax.named_scope("attend_low"):
-        attend(0, early_hooks)
+        attend(0, first_hooks, 0, PER)
     with jax.named_scope("values"):
-        values(0)
+        values_low(0)
+    with jax.named_scope("attend_low"):
+        attend(0, second_hooks, PER, PER)
+    with jax.named_scope("values"):
+        values_low(1)
     with jax.named_scope("attend_high"):
-        attend(1, late_hooks)
+        attend(1, late_hooks, 0, HEADS)
     with jax.named_scope("values"):
-        values(1)
+        values_high()
+    with jax.named_scope("stage4_0"):
+        stage4(0)
     with jax.named_scope("stage1_23"):
         stage1(2)
         stage1(3)
-    with jax.named_scope("stage23_1"):
-        stage2(1)
-        stage3(1)
-    with jax.named_scope("stage4_0"):
-        stage4(0)
+    with jax.named_scope("stage4_1"):
+        stage4(1)
     with jax.named_scope("w_middle"):
         w_middle()
     with jax.named_scope("stage2_2"):
@@ -584,35 +633,33 @@
         stage3(2)
     with jax.named_scope("stage3_3"):
         stage3(3)
-    with jax.named_scope("stage4_1"):
-        stage4(1)
     with jax.named_scope("w_last"):
         w_last()
     with jax.named_scope("stage4_2"):
         stage4(2)
     with jax.named_scope("stage5_0"):
         stage5(0)
+    with jax.named_scope("stage5_1"):
+        stage5(1)
     with jax.named_scope("stage4_3"):
         stage4(3)
-    with jax.named_scope("stage5_1"):
-        stage5(1)
     with jax.named_scope("w_all"):
         w_all()
     with jax.named_scope("product_low"):
-        product(0, 2)
+        product_low()
     with jax.named_scope("half_out_low"):
         half_out(0)
         half_out(1)
     with jax.named_scope("stage5_2"):
         stage5(2)
     with jax.named_scope("product_2"):
-        product(2, 1)
+        product_high(0)
     with jax.named_scope("half_out_2"):
         half_out(2)
     with jax.named_scope("stage5_3"):
         stage5(3)
     with jax.named_scope("product_3"):
-        product(3, 1)
+        product_high(1)
     with jax.named_scope("half_out_3"):
         half_out(3)
     with jax.named_scope("whole_out_low"):
@@ -638,44 +685,27 @@
                 pltpu.make_async_copy(outgoing.at[0, 1, 0], piece, local_sem.at[10 + r]).wait()
 
     with jax.named_scope("drain"):
-        full = keys.at[0, 0]
-
-        def sent(ref, number):
-            copy(ref, ref, number, partner).wait_send()
-
-        def drain(ref, first, count):
-            def one(n, carry):
-                sent(ref, first + n)
-                return carry
-
-            lax.fori_loop(0, count, one, 0)
-
-        sent(full, CROSS)
-        sent(qx.at[0, 0], SWAP)
-        sent(qx.at[0, 0], SWAP2)
-        drain(full, D1, 4)
-        drain(full, FAR, 2)
-        drain(full, D2, 16)
-        drain(full, D2H, 8)
-        drain(keys.at[pl.ds(0, 16), 0], PAIR, 2)
-        drain(wg.at[0, 0, pl.ds(0, span)], WFULL, 4)
-        sent(wg.at[0, 0], WHALF)
-        drain(wg.at[0, 0], WPAIR, 4)
+
+        def sent(ref, leaving):
+            copy(ref, ref, 0, partner, leaving).wait_send()
+
+        sent(keys.at[0, 0], S_CROSS)
+        sent(qx.at[0], S_SWAP)
+        sent(keys.at[pl.ds(0, 15)], S_KEYS)
+        sent(keys.at[pl.ds(0, 16)], S_PAIR)
+        sent(wg.at[0, pl.ds(0, 3)], S_W)
+        sent(wg.at[0], S_WPAIR)
+        sent(low_stage, S_APAIR)
+        sent(summand, S_XSUM)
         for g in range(CHUNKS):
-            at = ABASE + ASTRIDE * g
-            sent(astage.at[g, 0], at + APAIR)
-            sent(ag.at[0, 0], at + AX)
-            drain(ag.at[0, 0], at + AZ, 4)
-            sent(ag.at[0, 0], at + AZH)
-            sent(ag.at[0, 0], at + AX2)
-        drain(summand.at[0, 0], XSUM, 8)
+            sent(low.at[pl.ds(0, 7), 0], S_A + g)
         for g in range(CHUNKS):
             for k in range(2):
                 own = (mine == 1) & (xh == g // 2) & (z == 2 * xl + k)
 
                 @pl.when(jnp.logical_not(own))
                 def _(g=g, k=k):
-                    sent(summand.at[0, 0], OUT + 2 * g + k)
+                    sent(summand.at[0, 0], S_OUT + 2 * g + k)
 
 
 def local(q_latent, kv_latent, kv_gain, w_q_b, w_kv_b, w_o, prompt_len, response_mask):
@@ -684,14 +714,13 @@
     table = np.stack([np.cos(fine), np.sin(fine), np.cos(HALF * fine), np.sin(HALF * fine)])
     hbm = pl.BlockSpec(memory_space=pltpu.HBM)
     bf16 = jnp.bfloat16
-    depth = HEADS * VD
     result = pl.pallas_call(
         body,
         out_shape=jax.ShapeDtypeStruct((2, 4, ROWS, 1792), bf16),
         in_specs=[hbm] * 5 + [pl.BlockSpec(memory_space=pltpu.SMEM)] + [hbm] * 3,
         out_specs=hbm,
         scratch_shapes=[
-            pltpu.SemaphoreType.DMA((NSEM,)),
+            pltpu.SemaphoreType.DMA((NSENT,)),
             pltpu.SemaphoreType.DMA((NSEM,)),
             pltpu.SemaphoreType.DMA((17,)),
             pltpu.VMEM((WIDE, 128), bf16),
@@ -704,8 +733,10 @@
             pltpu.VMEM((32, 2, HALF, WIDE), bf16),
             pltpu.VMEM((2, HEADS, HALF, WIDE), bf16),
             pltpu.VMEM((HEADS, HALF, KVR), bf16),
-            pltpu.VMEM((CHUNKS, 2, ROWS, depth), bf16),
-            pltpu.VMEM((8, CHUNKS, 2, ROWS, depth), bf16),
+            pltpu.VMEM((2, 2, 2 * ROWS, PER * VD), bf16),
+            pltpu.VMEM((2, 2, ROWS, HEADS * VD), bf16),
+            pltpu.VMEM((8, 2, 2, 2 * ROWS, PER * VD), bf16),
+            pltpu.VMEM((8, 2, 2, ROWS, HEADS * VD), bf16),
             pltpu.VMEM((2, 4, 224, 2048), bf16),
             pltpu.VMEM((CHUNKS, 8, ROWS, 4 * 224), jnp.float32),
             pltpu.VMEM((CHUNKS, 2, 2, 2, ROWS, 4 * 224), bf16),

time: 89.7 us -> 86.4 us (0.963); the launches traced: 89.5 us -> 85.2 us
  Pallas kernels: 87.1 us -> 82.8 us
    pallas_call x1, Pallas kernels: 87.1 us -> 82.8 us  [local(): pl.pallas_call(body, out_shape=jax.ShapeDtypeStruct((2, 4, ROWS, 1792), b...]
where the time goes in v9:
time: 86.4 us; the launch traced here: 85.2 us
  Pallas kernels  82.8 us (96%)
  local copies, waits for them, and re-layouts  1.82 us (2%)
    pallas_call x1, Pallas kernels, local(): pl.pallas_call(body, out_shape=jax.ShapeDtypeStruct((2, 4, ROWS, 1792), b...  82.8 us
    unnamed x1, local copies, waits for them, and re-layouts  1.82 us

profile of v9, /device:TPU:100, one launch (start us, length us, event | category | flops | bytes accessed | tf_op | source)
XLA Modules:
  0.0 85.2 jit_solution(9762299494369751934)
XLA Ops:
  0.7 82.8 %layer.1 = bf16[2,4,16,1792]{3,2,1,0:T(8,128)(2,1)} custom-call(bf16[2,2,32,1536]{3,2,1,0:T(8,128)(2,1)} %bitcast.8, bf16[576,128]{1,0:T(8,128)(2,1)} %bitcast.9, f32[1,512]{1,0:T(1,128)} %bitcast.11, f32[4,64,64]{2,1,0:T(8,128)} %constant.2.clone.table_hbm, s32[32,128]{1,0:T(8,128)} %bitcast.10, s32[1]{0:T(128)S(6)} %copy.11.prompt, ...), custom_call_target="tpu_custom_call" | custom-call | flops 20000000000 | bytes 16000000 | tf_op jit(solution)/shard_map/layer/pallas_call | solution.py:717
  83.4 1.8 %copy.12 = bf16[128,1792]{1,0:T(8,128)(2,1)} copy(bf16[128,1792]{1,0:T(8,128)(2,1)} %bitcast.6) | data formatting | bytes 917504

commit v10 on v9

--- a/solution.py
+++ b/solution.py
@@ -316,27 +316,27 @@
         own_rows.wait()
         pltpu.make_async_copy(wkv_hbm, wkv, local_sem.at[8]).wait()
         copy(qx.at[1 - xh, 1 - c], qx.at[1 - xh, 1 - c], SWAP2, partner).wait_recv()
-    project_in(0, 1)
+    project_in(0, 1, 2)
     with jax.named_scope("relay_l21"):
         relay(2, lower)
         relay(1, lower)
-    project_in(2)
+    project_in(3)
     with jax.named_scope("relay_l3"):
         relay(3, lower)
     with jax.named_scope("first_in_u"):
         first_in(upper)
-    project_in(3)
+    project_in(4)
     with jax.named_scope("far_u"):
         far_in(upper)
     with jax.named_scope("last_in_l"):
         for q in (0, 2, 1):
             last_in(q, lower)
-    project_in(4)
+    project_in(5)
     with jax.named_scope("last_in_l3"):
         last_in(3, lower)
     with jax.named_scope("relay_u0"):
         relay(0, upper)
-    project_in(5, 6, 7)
+    project_in(6, 7)
     with jax.named_scope("pair_in_l"):
         pair_in(lower)
 
@@ -764,7 +764,7 @@
         w_kv_b,
         w_o.T,
     )
-    return result.reshape(128, 1792)
+    return jnp.where(prompt_len[0] > 0, result.reshape(128, 1792), 0)
 
 
 def solution(mesh):

time: 86.4 us -> 86.1 us (level)
  other arithmetic: 0 us -> 1.83 us
  local copies, waits for them, and re-layouts: 1.82 us -> 0 us
    select_n x0 -> x1, other arithmetic: none -> 1.83 us  [local(): return jnp.where(prompt_len[0] > 0, result.reshape(128, 1792), 0)]
    unnamed x1 -> x0, local copies, waits for them, and re-layouts: 1.82 us -> none
where the time goes in v10:
time: 86.1 us; the launch traced here: 85.6 us
  Pallas kernels  83.1 us (97%)
  other arithmetic  1.83 us (2%)
    pallas_call x1, Pallas kernels, local(): pl.pallas_call(body, out_shape=jax.ShapeDtypeStruct((2, 4, ROWS, 1792), b...  83.1 us
    select_n x1, other arithmetic, local(): return jnp.where(prompt_len[0] > 0, result.reshape(128, 1792), 0)  1.83 us

profile of v10, /device:TPU:100, one launch (start us, length us, event | category | flops | bytes accessed | tf_op | source)
XLA Modules:
  0.0 85.6 jit_solution(11442142770975644836)
XLA Ops:
  0.7 83.1 %layer.1 = bf16[2,4,16,1792]{3,2,1,0:T(8,128)(2,1)} custom-call(bf16[2,2,32,1536]{3,2,1,0:T(8,128)(2,1)} %bitcast.8, bf16[576,128]{1,0:T(8,128)(2,1)} %bitcast.9, f32[1,512]{1,0:T(1,128)} %bitcast.11, f32[4,64,64]{2,1,0:T(8,128)} %constant.7.clone.table_hbm, s32[32,128]{1,0:T(8,128)} %bitcast.10, s32[1]{0:T(128)S(6)} %copy.10.prompt, ...), custom_call_target="tpu_custom_call" | custom-call | flops 20000000000 | bytes 16000000 | tf_op jit(solution)/shard_map/layer/pallas_call | solution.py:717
  83.8 1.8 %broadcast_select_fusion = bf16[2,4,16,1792]{3,2,1,0:T(8,128)(2,1)} fusion(bf16[2,4,16,1792]{3,2,1,0:T(8,128)(2,1)} %layer.1, pred[]{:T(512)} %bitcast), kind=kLoop, calls=%fused_computation | loop fusion | flops 229376 | bytes 917505 | tf_op jit(solution)/shard_map/jit(_where)/select_n | solution.py:767

commit v11 on v10

--- a/solution.py
+++ b/solution.py
@@ -505,15 +505,17 @@
         for n in range(2):
             part[n] = total[:, n * ROWS : (n + 1) * ROWS]
 
-    def product_high(r):
-        rows = 8 * ROWS
+    def product_high():
+        rows = 16 * ROWS
         total = jnp.zeros((rows, 4 * 224), jnp.float32)
         for core in range(2):
             total = total + multiplied(
-                high[:, r, core].reshape(rows, HEADS * VD),
+                high[:, :, core].reshape(rows, HEADS * VD),
                 wg[core].reshape(4 * 224, HEADS * VD),
             )
-        part[2 + r] = total.reshape(8, ROWS, 4 * 224)
+        total = total.reshape(8, 2 * ROWS, 4 * 224)
+        for n in range(2):
+            part[2 + n] = total[:, n * ROWS : (n + 1) * ROWS]
 
     def slots(half, k):
         straight, mirrored = k, 3 - k
@@ -650,17 +652,13 @@
     with jax.named_scope("half_out_low"):
         half_out(0)
         half_out(1)
-    with jax.named_scope("stage5_2"):
+    with jax.named_scope("stage5_23"):
         stage5(2)
-    with jax.named_scope("product_2"):
-        product_high(0)
-    with jax.named_scope("half_out_2"):
+        stage5(3)
+    with jax.named_scope("product_high"):
+        product_high()
+    with jax.named_scope("half_out_high"):
         half_out(2)
-    with jax.named_scope("stage5_3"):
-        stage5(3)
-    with jax.named_scope("product_3"):
-        product_high(1)
-    with jax.named_scope("half_out_3"):
         half_out(3)
     with jax.named_scope("whole_out_low"):
         whole_out(0)

time: 86.1 us -> 86.1 us (level)
  no operation moved by 1% of the time
where the time goes in v11:
time: 86.1 us; the launch traced here: 84.8 us
  Pallas kernels  82.3 us (96%)
  other arithmetic  1.83 us (2%)
    pallas_call x1, Pallas kernels, local(): pl.pallas_call(body, out_shape=jax.ShapeDtypeStruct((2, 4, ROWS, 1792), b...  82.3 us
    select_n x1, other arithmetic, local(): return jnp.where(prompt_len[0] > 0, result.reshape(128, 1792), 0)  1.83 us

profile of v11, /device:TPU:100, one launch (start us, length us, event | category | flops | bytes accessed | tf_op | source)
XLA Modules:
  0.0 84.8 jit_solution(12095672023638795262)
XLA Ops:
  0.7 82.3 %layer.1 = bf16[2,4,16,1792]{3,2,1,0:T(8,128)(2,1)} custom-call(bf16[2,2,32,1536]{3,2,1,0:T(8,128)(2,1)} %bitcast.8, bf16[576,128]{1,0:T(8,128)(2,1)} %bitcast.9, f32[1,512]{1,0:T(1,128)} %bitcast.11, f32[4,64,64]{2,1,0:T(8,128)} %constant.7.clone.table_hbm, s32[32,128]{1,0:T(8,128)} %bitcast.10, s32[1]{0:T(128)S(6)} %copy.10.prompt, ...), custom_call_target="tpu_custom_call" | custom-call | flops 20000000000 | bytes 16000000 | tf_op jit(solution)/shard_map/layer/pallas_call | solution.py:715
  83.0 1.8 %broadcast_select_fusion = bf16[2,4,16,1792]{3,2,1,0:T(8,128)(2,1)} fusion(bf16[2,4,16,1792]{3,2,1,0:T(8,128)(2,1)} %layer.1, pred[]{:T(512)} %bitcast), kind=kLoop, calls=%fused_computation | loop fusion | flops 229376 | bytes 917505 | tf_op jit(solution)/shard_map/jit(_where)/select_n | solution.py:765

commit v12 on v10

--- a/solution.py
+++ b/solution.py
@@ -554,7 +554,7 @@
                 ).start()
 
     def first_hooks(b, blocks):
-        @pl.when(b == 0)
+        @pl.when(b == jnp.minimum(1, blocks))
         def _():
             with jax.named_scope("relay_u"):
                 for q in (2, 1, 3):

time: 86.1 us -> 86.8 us (level)
  Pallas kernels: 83.1 us -> 84.2 us
    pallas_call x1, Pallas kernels: 83.1 us -> 84.2 us  [local(): pl.pallas_call(body, out_shape=jax.ShapeDtypeStruct((2, 4, ROWS, 1792), b...]
where the time goes in v12:
time: 86.8 us; the launch traced here: 86.6 us
  Pallas kernels  84.2 us (97%)
  other arithmetic  1.83 us (2%)
    pallas_call x1, Pallas kernels, local(): pl.pallas_call(body, out_shape=jax.ShapeDtypeStruct((2, 4, ROWS, 1792), b...  84.2 us
    select_n x1, other arithmetic, local(): return jnp.where(prompt_len[0] > 0, result.reshape(128, 1792), 0)  1.83 us

profile of v12, /device:TPU:100, one launch (start us, length us, event | category | flops | bytes accessed | tf_op | source)
XLA Modules:
  0.0 86.6 jit_solution(8909033730846031967)
XLA Ops:
  0.7 84.2 %layer.1 = bf16[2,4,16,1792]{3,2,1,0:T(8,128)(2,1)} custom-call(bf16[2,2,32,1536]{3,2,1,0:T(8,128)(2,1)} %bitcast.8, bf16[576,128]{1,0:T(8,128)(2,1)} %bitcast.9, f32[1,512]{1,0:T(1,128)} %bitcast.11, f32[4,64,64]{2,1,0:T(8,128)} %constant.7.clone.table_hbm, s32[32,128]{1,0:T(8,128)} %bitcast.10, s32[1]{0:T(128)S(6)} %copy.10.prompt, ...), custom_call_target="tpu_custom_call" | custom-call | flops 20000000000 | bytes 16000000 | tf_op jit(solution)/shard_map/layer/pallas_call | solution.py:717
  84.8 1.8 %broadcast_select_fusion = bf16[2,4,16,1792]{3,2,1,0:T(8,128)(2,1)} fusion(bf16[2,4,16,1792]{3,2,1,0:T(8,128)(2,1)} %layer.1, pred[]{:T(512)} %bitcast), kind=kLoop, calls=%fused_computation | loop fusion | flops 229376 | bytes 917505 | tf_op jit(solution)/shard_map/jit(_where)/select_n | solution.py:767
